TPU v7x, 32 devices: a whole 2x2x4 slice. The times are simulated.
32 devices in a mesh: fsdp: 8 (over y, x, core), seq: 4 (over z).
Axes of the slice: x: 2, y: 2, z: 4, core: 2. Of those that a mesh axis runs over, the one named last changes fastest.
Arguments:
- tokens: bfloat16 [8192, 768], P(('fsdp', 'seq')), may hold values from -6 to 6
- segments: int32 [8, 1024], P('fsdp'), may hold values from 0 to 3, never falling along the last dimension, each value on 1 to 512 neighbouring positions
- cotangent: bfloat16 [8192, 768], P(('fsdp', 'seq')), may hold values from -6 to 6
- query_weight: float32 [768, 768], P(('fsdp', 'seq')), may hold values from -0.21875 to 0.21875
- query_bias: float32 [768], P(('fsdp', 'seq')), may hold values from -3 to 3
- key_weight: float32 [768, 768], P(('fsdp', 'seq')), may hold values from -0.21875 to 0.21875
- value_weight: float32 [768, 768], P(('fsdp', 'seq')), may hold values from -0.21875 to 0.21875
- value_bias: float32 [768], P(('fsdp', 'seq')), may hold values from -3 to 3
- mixer_weight: float32 [768, 768], P(('fsdp', 'seq')), may hold values from -1.5 to 1.5
- mixer_bias: float32 [768], P(('fsdp', 'seq')), may hold values from -1.75 to 1.75
- first_gain: float32 [768], P(('fsdp', 'seq')), may hold values from 0.5 to 1.5
- first_shift: float32 [768], P(('fsdp', 'seq')), may hold values from -1.75 to 1.75
- inner_weight: float32 [768, 3072], P(('fsdp', 'seq')), may hold values from -0.21875 to 0.21875
- inner_bias: float32 [3072], P(('fsdp', 'seq')), may hold values from -3 to 3
- outer_weight: float32 [3072, 768], P(('fsdp', 'seq')), may hold values from -0.15625 to 0.15625
- outer_bias: float32 [768], P(('fsdp', 'seq')), may hold values from -1.75 to 1.75
- second_gain: float32 [768], P(('fsdp', 'seq')), may hold values from 0.5 to 1.5
- second_shift: float32 [768], P(('fsdp', 'seq')), may hold values from -1.75 to 1.75
Outputs:
- layer_out: bfloat16 [8192, 768], P(('fsdp', 'seq'))
- tokens_grad: bfloat16 [8192, 768], P(('fsdp', 'seq'))
- query_weight_grad: float32 [768, 768], P(('fsdp', 'seq'))
- query_bias_grad: float32 [768], P(('fsdp', 'seq'))
- key_weight_grad: float32 [768, 768], P(('fsdp', 'seq'))
- value_weight_grad: float32 [768, 768], P(('fsdp', 'seq'))
- value_bias_grad: float32 [768], P(('fsdp', 'seq'))
- mixer_weight_grad: float32 [768, 768], P(('fsdp', 'seq'))
- mixer_bias_grad: float32 [768], P(('fsdp', 'seq'))
- first_gain_grad: float32 [768], P(('fsdp', 'seq'))
- first_shift_grad: float32 [768], P(('fsdp', 'seq'))
- inner_weight_grad: float32 [768, 3072], P(('fsdp', 'seq'))
- inner_bias_grad: float32 [3072], P(('fsdp', 'seq'))
- outer_weight_grad: float32 [3072, 768], P(('fsdp', 'seq'))
- outer_bias_grad: float32 [768], P(('fsdp', 'seq'))
- second_gain_grad: float32 [768], P(('fsdp', 'seq'))
- second_shift_grad: float32 [768], P(('fsdp', 'seq'))
Inputs may be any that keep to these rules, and one draw needn't show every extreme that they name: `segments`: within each sequence the document numbers never fall; each document covers 1 to 512 positions, one of them exactly that many.
All inputs are finite; a program needn't handle non-finite values.
Results may differ from a plain program's by a relative error of at most 0.015.
The roundings to bfloat16 on the way count: a program that leaves them out, or rounds other values in their place, can miss the bound.
Values may be sent and summed in bfloat16 or wider, within the bound.
No kernel may reach another device: no remote copies, remote signals or barrier semaphores. Data moves between devices by JAX's collectives and lax.ppermute only.
A program may use at most 192 MiB of HBM per device.

v0:
```python
import jax
import jax.numpy as jnp
from jax import lax
from jax.sharding import PartitionSpec as P

HD = 64


EPSILON = 1e-12
NEGATIVE = -1e30


def product(left, right):
    return jnp.dot(left, right, preferred_element_type=jnp.float32)


def product_tn(left, right):
    return lax.dot_general(
        left, right, (((0,), (0,)), ((), ())), preferred_element_type=jnp.float32
    )


def product_nt(left, right):
    return lax.dot_general(
        left, right, (((1,), (1,)), ((), ())), preferred_element_type=jnp.float32
    )


def column_sum(values):
    return jnp.sum(values.astype(jnp.float32), axis=0)


def normalize(hidden, gain, shift):
    centred = hidden - jnp.mean(hidden, axis=-1, keepdims=True)
    scale = lax.rsqrt(jnp.mean(centred * centred, axis=-1, keepdims=True) + EPSILON)
    normed = centred * scale
    return (normed * gain + shift, normed, scale)


def normalize_back(grad_out, normed, scale, gain):
    grad_normed = grad_out * gain
    grad_hidden = scale * (
        grad_normed
        - jnp.mean(grad_normed, axis=-1, keepdims=True)
        - normed * jnp.mean(grad_normed * normed, axis=-1, keepdims=True)
    )
    return (grad_hidden, jnp.sum(grad_out * normed, axis=0), jnp.sum(grad_out, axis=0))


def attend_forward(queries, keys, values, segment):
    length, width = queries.shape
    heads = width // HD
    block = min(512, length)
    count = length // block
    scale = HD ** (-0.5)
    key_heads = keys.reshape(length, heads, HD)
    value_heads = values.reshape(length, heads, HD)
    query_blocks = queries.reshape(count, block, heads, HD)
    segment_blocks = segment.reshape(count, block)

    def one_block(inputs):
        query_block, segment_block = inputs
        scores = (
            jnp.einsum("qhd,khd->hqk", query_block, key_heads, preferred_element_type=jnp.float32)
            * scale
        )
        allowed = (segment_block[:, None] == segment[None, :])[None]
        masked = jnp.where(allowed, scores, NEGATIVE)
        peak = jnp.max(masked, axis=-1, keepdims=True)
        weights = jnp.where(allowed, jnp.exp(masked - peak), 0.0)
        total = jnp.sum(weights, axis=-1, keepdims=True)
        probs = (weights / total).astype(jnp.bfloat16)
        mixed = jnp.einsum("hqk,khd->qhd", probs, value_heads, preferred_element_type=jnp.float32)
        return (mixed.astype(jnp.bfloat16), (peak + jnp.log(total))[..., 0])

    mixed, logsum = lax.map(one_block, (query_blocks, segment_blocks))
    return (mixed.reshape(length, width), logsum)


def attend_back(queries, keys, values, segment, logsum, grad_mixed):
    length, width = queries.shape
    heads = width // HD
    block = min(512, length)
    count = length // block
    scale = HD ** (-0.5)
    key_heads = keys.reshape(length, heads, HD)
    value_heads = values.reshape(length, heads, HD)
    query_blocks = queries.reshape(count, block, heads, HD)
    grad_blocks = grad_mixed.reshape(count, block, heads, HD)
    segment_blocks = segment.reshape(count, block)

    def one_block(carry, inputs):
        key_total, value_total = carry
        query_block, segment_block, logsum_block, grad_block = inputs
        scores = (
            jnp.einsum("qhd,khd->hqk", query_block, key_heads, preferred_element_type=jnp.float32)
            * scale
        )
        allowed = (segment_block[:, None] == segment[None, :])[None]
        probs = jnp.where(allowed, jnp.exp(scores - logsum_block[..., None]), 0.0)
        grad_probs = jnp.einsum(
            "qhd,khd->hqk", grad_block, value_heads, preferred_element_type=jnp.float32
        )
        delta = jnp.sum(probs * grad_probs, axis=-1, keepdims=True)
        grad_scores = (probs * (grad_probs - delta)).astype(jnp.bfloat16)
        grad_query = (
            jnp.einsum("hqk,khd->qhd", grad_scores, key_heads, preferred_element_type=jnp.float32)
            * scale
        )
        key_total = (
            key_total
            + jnp.einsum(
                "hqk,qhd->khd", grad_scores, query_block, preferred_element_type=jnp.float32
            )
            * scale
        )
        value_total = value_total + jnp.einsum(
            "hqk,qhd->khd",
            probs.astype(jnp.bfloat16),
            grad_block,
            preferred_element_type=jnp.float32,
        )
        return ((key_total, value_total), grad_query.astype(jnp.bfloat16))

    start = jnp.zeros((length, heads, HD), jnp.float32)
    (key_total, value_total), grad_queries = lax.scan(
        one_block, (start, start), (query_blocks, segment_blocks, logsum, grad_blocks)
    )
    return (
        grad_queries.reshape(length, width),
        key_total.reshape(length, width).astype(jnp.bfloat16),
        value_total.reshape(length, width).astype(jnp.bfloat16),
    )


def on_device(
    tokens,
    segments,
    cotangent,
    query_weight,
    query_bias,
    key_weight,
    value_weight,
    value_bias,
    mixer_weight,
    mixer_bias,
    first_gain,
    first_shift,
    inner_weight,
    inner_bias,
    outer_weight,
    outer_bias,
    second_gain,
    second_shift,
):
    lowered = [
        piece.astype(jnp.bfloat16)
        for piece in (
            query_weight,
            query_bias,
            key_weight,
            value_weight,
            value_bias,
            mixer_weight,
            mixer_bias,
            first_gain,
            first_shift,
            inner_weight,
            inner_bias,
            outer_weight,
            outer_bias,
            second_gain,
            second_shift,
        )
    ]
    gathered = (
        lax.all_gather(lowered[0], ("fsdp", "seq"), axis=0, tiled=True),
        lax.all_gather(lowered[1], ("fsdp", "seq"), axis=0, tiled=True),
        lax.all_gather(lowered[2], ("fsdp", "seq"), axis=0, tiled=True),
        lax.all_gather(lowered[3], ("fsdp", "seq"), axis=0, tiled=True),
        lax.all_gather(lowered[4], ("fsdp", "seq"), axis=0, tiled=True),
        lax.all_gather(lowered[5], ("fsdp", "seq"), axis=0, tiled=True),
        lax.all_gather(lowered[6], ("fsdp", "seq"), axis=0, tiled=True),
        lax.all_gather(lowered[7], ("fsdp", "seq"), axis=0, tiled=True),
        lax.all_gather(lowered[8], ("fsdp", "seq"), axis=0, tiled=True),
        lax.all_gather(lowered[9], ("fsdp", "seq"), axis=0, tiled=True),
        lax.all_gather(lowered[10], ("fsdp", "seq"), axis=0, tiled=True),
        lax.all_gather(lowered[11], ("fsdp", "seq"), axis=0, tiled=True),
        lax.all_gather(lowered[12], ("fsdp", "seq"), axis=0, tiled=True),
        lax.all_gather(lowered[13], ("fsdp", "seq"), axis=0, tiled=True),
        lax.all_gather(lowered[14], ("fsdp", "seq"), axis=0, tiled=True),
    )
    (
        query_full,
        qbias_full,
        key_full,
        value_full,
        vbias_full,
        mixer_full,
        mbias_full,
        gain_one,
        shift_one,
        inner_full,
        ibias_full,
        outer_full,
        obias_full,
        gain_two,
        shift_two,
    ) = gathered
    queries = (product(tokens, query_full) + qbias_full).astype(jnp.bfloat16)
    keys = product(tokens, key_full).astype(jnp.bfloat16)
    values = (product(tokens, value_full) + vbias_full).astype(jnp.bfloat16)
    query_heads, key_heads, value_heads = (
        lax.all_to_all(queries, "seq", split_axis=1, concat_axis=0, tiled=True),
        lax.all_to_all(keys, "seq", split_axis=1, concat_axis=0, tiled=True),
        lax.all_to_all(values, "seq", split_axis=1, concat_axis=0, tiled=True),
    )
    segment = segments[0]
    mixed_heads, logsum = attend_forward(query_heads, key_heads, value_heads, segment)
    mixed_rows = lax.all_to_all(mixed_heads, "seq", split_axis=0, concat_axis=1, tiled=True)
    attended = product(mixed_rows, mixer_full) + mbias_full
    first_out, first_normed, first_scale = normalize(
        tokens.astype(jnp.float32) + attended, gain_one, shift_one
    )
    first_low = first_out.astype(jnp.bfloat16)
    inner_pre = product(first_low, inner_full) + ibias_full
    active, gelu_back = jax.vjp(lambda value: jax.nn.gelu(value, approximate=False), inner_pre)
    active_low = active.astype(jnp.bfloat16)
    outer = product(active_low, outer_full) + obias_full
    result, second_normed, second_scale = normalize(first_out + outer, gain_two, shift_two)
    again = (
        lax.all_gather(lowered[0], ("fsdp", "seq"), axis=0, tiled=True),
        lax.all_gather(lowered[1], ("fsdp", "seq"), axis=0, tiled=True),
        lax.all_gather(lowered[2], ("fsdp", "seq"), axis=0, tiled=True),
        lax.all_gather(lowered[3], ("fsdp", "seq"), axis=0, tiled=True),
        lax.all_gather(lowered[4], ("fsdp", "seq"), axis=0, tiled=True),
        lax.all_gather(lowered[5], ("fsdp", "seq"), axis=0, tiled=True),
        lax.all_gather(lowered[6], ("fsdp", "seq"), axis=0, tiled=True),
        lax.all_gather(lowered[7], ("fsdp", "seq"), axis=0, tiled=True),
        lax.all_gather(lowered[8], ("fsdp", "seq"), axis=0, tiled=True),
        lax.all_gather(lowered[9], ("fsdp", "seq"), axis=0, tiled=True),
        lax.all_gather(lowered[10], ("fsdp", "seq"), axis=0, tiled=True),
        lax.all_gather(lowered[11], ("fsdp", "seq"), axis=0, tiled=True),
        lax.all_gather(lowered[12], ("fsdp", "seq"), axis=0, tiled=True),
        lax.all_gather(lowered[13], ("fsdp", "seq"), axis=0, tiled=True),
        lax.all_gather(lowered[14], ("fsdp", "seq"), axis=0, tiled=True),
    )
    (
        query_full,
        qbias_full,
        key_full,
        value_full,
        vbias_full,
        mixer_full,
        mbias_full,
        gain_one,
        shift_one,
        inner_full,
        ibias_full,
        outer_full,
        obias_full,
        gain_two,
        shift_two,
    ) = again
    grad_second, grad_gain_two, grad_shift_two = normalize_back(
        cotangent.astype(jnp.float32), second_normed, second_scale, gain_two
    )
    grad_outer = grad_second.astype(jnp.bfloat16)
    grad_outer_weight = product_tn(active_low, grad_outer)
    grad_outer_bias = column_sum(grad_outer)
    grad_inner = gelu_back(product_nt(grad_outer, outer_full))[0].astype(jnp.bfloat16)
    grad_inner_weight = product_tn(first_low, grad_inner)
    grad_inner_bias = column_sum(grad_inner)
    grad_first_out = grad_second + product_nt(grad_inner, inner_full)
    grad_residual, grad_gain_one, grad_shift_one = normalize_back(
        grad_first_out, first_normed, first_scale, gain_one
    )
    grad_attended = grad_residual.astype(jnp.bfloat16)
    grad_mixer_weight = product_tn(mixed_rows, grad_attended)
    grad_mixer_bias = column_sum(grad_attended)
    grad_mixed = product_nt(grad_attended, mixer_full).astype(jnp.bfloat16)
    grad_mixed_heads = lax.all_to_all(grad_mixed, "seq", split_axis=1, concat_axis=0, tiled=True)
    grad_query_heads, grad_key_heads, grad_value_heads = attend_back(
        query_heads, key_heads, value_heads, segment, logsum, grad_mixed_heads
    )
    grad_queries, grad_keys, grad_values = (
        lax.all_to_all(grad_query_heads, "seq", split_axis=0, concat_axis=1, tiled=True),
        lax.all_to_all(grad_key_heads, "seq", split_axis=0, concat_axis=1, tiled=True),
        lax.all_to_all(grad_value_heads, "seq", split_axis=0, concat_axis=1, tiled=True),
    )
    grad_query_weight = product_tn(tokens, grad_queries)
    grad_query_bias = column_sum(grad_queries)
    grad_key_weight = product_tn(tokens, grad_keys)
    grad_value_weight = product_tn(tokens, grad_values)
    grad_value_bias = column_sum(grad_values)
    grad_tokens = (
        grad_residual
        + product_nt(grad_queries, query_full)
        + product_nt(grad_keys, key_full)
        + product_nt(grad_values, value_full)
    )
    summed = (
        lax.psum_scatter(grad_query_weight, ("fsdp", "seq"), scatter_dimension=0, tiled=True),
        lax.psum_scatter(grad_query_bias, ("fsdp", "seq"), scatter_dimension=0, tiled=True),
        lax.psum_scatter(grad_key_weight, ("fsdp", "seq"), scatter_dimension=0, tiled=True),
        lax.psum_scatter(grad_value_weight, ("fsdp", "seq"), scatter_dimension=0, tiled=True),
        lax.psum_scatter(grad_value_bias, ("fsdp", "seq"), scatter_dimension=0, tiled=True),
        lax.psum_scatter(grad_mixer_weight, ("fsdp", "seq"), scatter_dimension=0, tiled=True),
        lax.psum_scatter(grad_mixer_bias, ("fsdp", "seq"), scatter_dimension=0, tiled=True),
        lax.psum_scatter(grad_gain_one, ("fsdp", "seq"), scatter_dimension=0, tiled=True),
        lax.psum_scatter(grad_shift_one, ("fsdp", "seq"), scatter_dimension=0, tiled=True),
        lax.psum_scatter(grad_inner_weight, ("fsdp", "seq"), scatter_dimension=0, tiled=True),
        lax.psum_scatter(grad_inner_bias, ("fsdp", "seq"), scatter_dimension=0, tiled=True),
        lax.psum_scatter(grad_outer_weight, ("fsdp", "seq"), scatter_dimension=0, tiled=True),
        lax.psum_scatter(grad_outer_bias, ("fsdp", "seq"), scatter_dimension=0, tiled=True),
        lax.psum_scatter(grad_gain_two, ("fsdp", "seq"), scatter_dimension=0, tiled=True),
        lax.psum_scatter(grad_shift_two, ("fsdp", "seq"), scatter_dimension=0, tiled=True),
    )
    return (
        result.astype(jnp.bfloat16),
        grad_tokens.astype(jnp.bfloat16),
        summed[0],
        summed[1],
        summed[2],
        summed[3],
        summed[4],
        summed[5],
        summed[6],
        summed[7],
        summed[8],
        summed[9],
        summed[10],
        summed[11],
        summed[12],
        summed[13],
        summed[14],
    )


def solution(mesh):
    placed = (
        P(("fsdp", "seq"), None),
        P("fsdp", None),
        P(("fsdp", "seq"), None),
        P(("fsdp", "seq"), None),
        P(("fsdp", "seq")),
        P(("fsdp", "seq"), None),
        P(("fsdp", "seq"), None),
        P(("fsdp", "seq")),
        P(("fsdp", "seq"), None),
        P(("fsdp", "seq")),
        P(("fsdp", "seq")),
        P(("fsdp", "seq")),
        P(("fsdp", "seq"), None),
        P(("fsdp", "seq")),
        P(("fsdp", "seq"), None),
        P(("fsdp", "seq")),
        P(("fsdp", "seq")),
        P(("fsdp", "seq")),
    )
    return jax.shard_map(
        on_device,
        mesh=mesh,
        in_specs=placed,
        out_specs=(
            P(("fsdp", "seq"), None),
            P(("fsdp", "seq"), None),
            P(("fsdp", "seq"), None),
            P(("fsdp", "seq")),
            P(("fsdp", "seq"), None),
            P(("fsdp", "seq"), None),
            P(("fsdp", "seq")),
            P(("fsdp", "seq"), None),
            P(("fsdp", "seq")),
            P(("fsdp", "seq")),
            P(("fsdp", "seq")),
            P(("fsdp", "seq"), None),
            P(("fsdp", "seq")),
            P(("fsdp", "seq"), None),
            P(("fsdp", "seq")),
            P(("fsdp", "seq")),
            P(("fsdp", "seq")),
        ),
        check_vma=False,
    )
```

profile of v0, /device:TPU:0, one launch (start us, length us, event | category | flops | bytes accessed | tf_op | source)
XLA Modules:
  0.0 1102.4 jit_solution(12381397289811144292)
XLA Ops:
  7.2 1.5 convert_element_type.166
  8.9 1.5 convert_element_type.172
  10.4 1.5 convert_element_type.170
  12.0 1.5 convert_element_type.176
  13.6 1.6 convert_element_type.184
  23.0 42.3 %all-reduce.19 = (bf16[3072]{0:T(1024)(128)(2,1)S(1)}, bf16[768]{0:T(1024)(128)(2,1)S(1)}, bf16[768]{0:T(1024)(128)(2,1)S(1)}, bf16[768]{0:T(1024)(128)(2,1)S(1)...) all-reduce(bf16[3072]{0:T(1024)(128)(2,1)S(1)} %dynamic-update-slic, ...), channel_id=1, replica_groups=mesh['fsdp'=8,'seq'=4] {'fsdp','seq'}, use_global_device_ids=true, to_apply=%add.5 | all-reduce | flops 9216 | bytes 36864
  65.4 2.8 all-gather.7.cloned.1.call-done
  68.2 1.9 fusion.52
  71.0 3.5 all-to-all-start
  74.5 51.0 %all-gather.11.cloned.1.call-done = bf16[768,768]{1,0:T(8,128)(2,1)} async-done(((bf16[24,768]{1,0:T(8,128)(2,1)}), bf16[768,768]{1,0:T(8,128)(2,1)}) %all-gather.11.cloned.1.call-update) | async-done | bytes 1179664 | tf_op jit(solution)/shard_map/all_gather | solution.py:180
  125.6 1.7 fusion.53
  128.3 3.5 all-to-all-start.2
  131.8 51.0 %all-gather.9.cloned.1.call-done = bf16[768,768]{1,0:T(8,128)(2,1)} async-done(((bf16[24,768]{1,0:T(8,128)(2,1)}), bf16[768,768]{1,0:T(8,128)(2,1)}) %all-gather.9.cloned.1.call-update) | async-done | bytes 1179664 | tf_op jit(solution)/shard_map/all_gather | solution.py:179
  182.8 1.7 convolution_convert_fusion.1
  185.5 3.5 all-to-all-start.1
  192.4 9.4 all-to-all-done.1
  202.4 13.2 %while.27 = (s32[]{:T(128)}, bf16[2,512,3,64]{1,3,2,0:T(8,128)(2,1)S(1)}, f32[2,3,512]{2,1,0:T(4,128)S(1)}, s32[2,512]{1,0:T(2,128)S(1)}, s32[1,1024]{1,0:T(1,12...) while((s32[]{:T(128)}, ...), condition=%wide.region_3.4_spmd, body=%wide.region_0.3_spmd.sunk | while | flops 425294336 | bytes 22220908 | solution.py:76
  202.8 1.4 fusion.136
  204.2 2.3 fusion.137
  206.5 2.5 fusion.138
  209.4 1.4 fusion.136
  210.8 2.3 fusion.137
  213.1 2.5 fusion.138
  217.0 3.9 all-to-all-start.3
  220.9 18.9 %all-gather.13.cloned.1.call-done = bf16[768,768]{1,0:T(8,128)(2,1)} async-done(((bf16[24,768]{1,0:T(8,128)(2,1)}), bf16[768,768]{1,0:T(8,128)(2,1)}) %all-gather.13.cloned.1.call-update) | async-done | bytes 1179664 | tf_op jit(solution)/shard_map/all_gather | solution.py:182
  239.8 1.9 fusion.77
  241.9 63.6 %all-gather.15.cloned.1.call-done = bf16[768,3072]{1,0:T(8,128)(2,1)} async-done(((bf16[24,3072]{1,0:T(8,128)(2,1)}), bf16[768,3072]{1,0:T(8,128)(2,1)}) %all-gather.15.cloned.1.call-update) | async-done | bytes 4718608 | tf_op jit(solution)/shard_map/all_gather | solution.py:186
  305.5 11.6 %multiply_convert_fusion.1 = (bf16[256,3072]{1,0:T(8,128)(2,1)}, f32[256,3072]{1,0:T(8,128)}, f32[256,3072]{1,0:T(8,128)}) fusion(f32[3072]{0:T(1024)S(1)} %convert_element_type.186, bf16[768,3072]{1,0:T(8,128)(2,1)} %all-gather.15.cloned.1.call-done, f32[256,768]{1,0:T(8,128)S(1)} %get-tuple-element.397, f32[768]{0:T(1024)S(1)} %convert_element_type.182, ...), kind=kOutput, calls=%fused_computation.58 | convolution fusion | flops 1260847104 | bytes 13389824 | tf_op jit(solution)/shard_map/dot_general | solution.py:14
  317.1 53.6 %all-gather.17.cloned.1.call-done = bf16[3072,768]{1,0:T(8,128)(2,1)} async-done(((bf16[96,768]{1,0:T(8,128)(2,1)}), bf16[3072,768]{1,0:T(8,128)(2,1)}) %all-gather.17.cloned.1.call-update) | async-done | bytes 4718608 | tf_op jit(solution)/shard_map/all_gather | solution.py:188
  370.7 4.5 fusion.78
  376.4 1.7 convert_reduce_fusion.2
  378.1 2.7 convert_reduce_fusion
  380.9 2.2 multiply_reduce_fusion.1
  385.5 3.5 all-to-all-start.4
  389.0 1.9 fusion.63
  391.2 10.1 all-to-all-done.4
  402.7 28.8 %while.28 = (s32[]{:T(128)}, f32[1024,3,64]{0,2,1:T(8,128)}, f32[1024,3,64]{0,2,1:T(8,128)}, bf16[2,512,3,64]{1,3,2,0:T(8,128)(2,1)}, bf16[2,512,3,64]{1,3,2,0:T...) while((s32[]{:T(128)}, f32[1024,3,64]{0,2,1:T(8,128)}, ...), condition=%wide.region_14.15_spmd.clone, body=%wide.region_12.14_spmd.clone.sunk | while | flops 1031928320 | bytes 118743112 | solution.py:126
  404.2 2.6 multiply_reduce_fusion.7
  406.8 1.9 multiply_convert_fusion.3
  408.7 2.6 fusion.149
  411.3 1.8 fusion.151
  413.1 3.6 fusion.150
  418.3 2.6 multiply_reduce_fusion.7
  420.9 1.9 multiply_convert_fusion.3
  422.8 2.9 fusion.149
  425.7 1.8 fusion.151
  427.5 3.9 fusion.150
  431.5 1.5 copy.111
  433.1 13.9 %all_to_all.134 = bf16[4,256,192]{1,2,0:T(8,128)(2,1)S(1)} all-to-all(bf16[4,256,192]{1,2,0:T(8,128)(2,1)S(1)} %copy.112), channel_id=1, replica_groups=mesh['fsdp'=8,'seq'=4] {'seq'}, dimensions={0} | all-to-all | bytes 786432 | tf_op jit(solution)/shard_map/all_to_all | solution.py:287
  448.2 2.0 copy.122
  450.7 15.4 %all_to_all.135 = bf16[4,256,192]{1,2,0:T(8,128)(2,1)S(1)} all-to-all(bf16[4,256,192]{1,2,0:T(8,128)(2,1)S(1)} %copy.113), channel_id=1, replica_groups=mesh['fsdp'=8,'seq'=4] {'seq'}, dimensions={0} | all-to-all | bytes 786432 | tf_op jit(solution)/shard_map/all_to_all | solution.py:288
  467.3 2.0 copy.124
  471.0 14.6 %all_to_all.136 = bf16[4,256,192]{1,2,0:T(8,128)(2,1)S(1)} all-to-all(bf16[4,256,192]{1,2,0:T(8,128)(2,1)S(1)} %copy.114), channel_id=1, replica_groups=mesh['fsdp'=8,'seq'=4] {'seq'}, dimensions={0} | all-to-all | bytes 786432 | tf_op jit(solution)/shard_map/all_to_all | solution.py:289
  486.9 1.9 copy.126
  490.2 5.2 fusion.72
  497.1 5.1 fusion.66
  503.8 39.1 %all-reduce.18 = (f32[768]{0:T(1024)S(1)}, f32[768]{0:T(1024)S(1)}, f32[768]{0:T(1024)S(1)}, f32[768]{0:T(1024)S(1)}, f32[768]{0:T(1024)S(1)}, /*index=5*/f32[30...) all-reduce(f32[768]{0:T(1024)S(1)} %reduce_sum.184, ...), channel_id=3, replica_groups=mesh['fsdp'=8,'seq'=4] {'fsdp','seq'}, use_global_device_ids=true, to_apply=%region_17.18.clone | all-reduce | flops 9216 | bytes 73728
  548.2 1.9 convolution_add_fusion.3
  550.6 1.3 fusion.54
  551.9 51.4 %reduce-scatter.19.cloned.1.call-done = f32[24,768]{1,0:T(8,128)} async-done(((f32[768,768]{1,0:T(8,128)}), f32[24,768]{1,0:T(8,128)}) %reduce-scatter.19.cloned.1.call-update) | async-done | bytes 73744
  603.2 104.5 %reduce-scatter.21.cloned.1.call-done = f32[24,768]{1,0:T(8,128)} async-done(((f32[768,768]{1,0:T(8,128)}), f32[24,768]{1,0:T(8,128)}) %reduce-scatter.21.cloned.1.call-update) | async-done | bytes 73744
  707.7 104.3 %reduce-scatter.23.cloned.1.call-done = f32[24,768]{1,0:T(8,128)} async-done(((f32[768,768]{1,0:T(8,128)}), f32[24,768]{1,0:T(8,128)}) %reduce-scatter.23.cloned.1.call-update) | async-done | bytes 73744
  812.1 141.7 %reduce-scatter.15.cloned.1.call-done = f32[24,3072]{1,0:T(8,128)} async-done(((f32[768,3072]{1,0:T(8,128)}), f32[24,3072]{1,0:T(8,128)}) %reduce-scatter.15.cloned.1.call-update) | async-done | bytes 294928 | tf_op jit(solution)/shard_map/reduce_scatter | solution.py:312
  953.8 141.5 %reduce-scatter.17.cloned.1.call-done = f32[96,768]{1,0:T(8,128)} async-done(((f32[3072,768]{1,0:T(8,128)}), f32[96,768]{1,0:T(8,128)}) %reduce-scatter.17.cloned.1.call-update) | async-done | bytes 294928 | tf_op jit(solution)/shard_map/reduce_scatter | solution.py:314
  (285 shorter events, 41.4 us)
Async XLA Ops:
  7.2 118.4 %copy-start.13 = (bf16[256,768]{1,0:T(8,128)(2,1)S(1)}, bf16[256,768]{1,0:T(8,128)(2,1)}, u32[]{:S(2)}) copy-start(bf16[256,768]{1,0:T(8,128)(2,1)} %param.22) | copy-start | bytes 1179652
  7.2 61.0 %all-gather.7.cloned.1.call-start = ((), (), s32[]{:S(2)}) async-start(), calls=%async_computation.14 | async-start | bytes 1216512 | tf_op jit(solution)/shard_map/all_gather | solution.py:177
  8.8 116.8 %all-gather.11.cloned.1.call-start = ((), (), s32[]{:S(2)}) async-start(), calls=%async_computation.16 | async-start | bytes 1216512 | tf_op jit(solution)/shard_map/all_gather | solution.py:180
  10.4 172.4 %all-gather.9.cloned.1.call-start = ((), (), s32[]{:S(2)}) async-start(), calls=%async_computation.15 | async-start | bytes 1216512 | tf_op jit(solution)/shard_map/all_gather | solution.py:179
  12.0 227.8 %all-gather.13.cloned.1.call-start = ((), (), s32[]{:S(2)}) async-start(), calls=%async_computation.17 | async-start | bytes 1216512 | tf_op jit(solution)/shard_map/all_gather | solution.py:182
  13.6 292.0 %all-gather.15.cloned.1.call-start = ((), (), s32[]{:S(2)}) async-start(), calls=%async_computation.18 | async-start | bytes 4866048 | tf_op jit(solution)/shard_map/all_gather | solution.py:186
  71.0 57.3 %all-to-all-start = ((bf16[256,4,192]{0,2,1:T(8,128)(2,1)}), bf16[256,4,192]{0,2,1:T(8,128)(2,1)S(1)}, u32[]{:S(2)}, u32[]{:S(2)}) async-start(bf16[256,4,192]{0,2,1:T(8,128)(2,1)} %bitcast.6), calls=%async_computation | async-start | bytes 786432 | tf_op jit(solution)/shard_map/all_to_all | solution.py:214
  74.5 114.7 %copy-start.33 = (f32[96,768]{1,0:T(8,128)S(1)}, f32[96,768]{1,0:T(8,128)}, u32[]{:S(2)}) copy-start(f32[96,768]{1,0:T(8,128)} %param.36) | copy-start | bytes 884740
  127.3 63.1 %copy-start.32 = (s32[1,1024]{1,0:T(1,128)S(1)}, s32[1,1024]{1,0:T(1,128)}, u32[]{:S(2)}) copy-start(s32[1,1024]{1,0:T(1,128)} %param.23) | copy-start | bytes 12292
  128.3 57.2 %all-to-all-start.2 = ((bf16[256,4,192]{0,2,1:T(8,128)(2,1)}), bf16[256,4,192]{0,2,1:T(8,128)(2,1)S(1)}, u32[]{:S(2)}, u32[]{:S(2)}) async-start(bf16[256,4,192]{0,2,1:T(8,128)(2,1)} %bitcast.10), calls=%async_computation.2 | async-start | bytes 786432 | tf_op jit(solution)/shard_map/all_to_all | solution.py:216
  185.5 16.3 %all-to-all-start.1 = ((bf16[256,4,192]{0,2,1:T(8,128)(2,1)}), bf16[256,4,192]{0,2,1:T(8,128)(2,1)S(1)}, u32[]{:S(2)}, u32[]{:S(2)}) async-start(bf16[256,4,192]{0,2,1:T(8,128)(2,1)} %bitcast.8), calls=%async_computation.1 | async-start | bytes 786432 | tf_op jit(solution)/shard_map/all_to_all | solution.py:215
  189.0 181.7 %all-gather.17.cloned.1.call-start = ((), (), s32[]{:S(2)}) async-start(), calls=%async_computation.19 | async-start | bytes 4866048 | tf_op jit(solution)/shard_map/all_gather | solution.py:188
  217.0 22.8 %all-to-all-start.3 = ((bf16[4,256,192]{1,2,0:T(8,128)(2,1)}), bf16[4,256,192]{1,2,0:T(8,128)(2,1)S(1)}, u32[]{:S(2)}, u32[]{:S(2)}) async-start(bf16[4,256,192]{1,2,0:T(8,128)(2,1)} %copy.106), calls=%async_computation.3 | async-start | bytes 786432 | tf_op jit(solution)/shard_map/all_to_all | solution.py:220
  220.9 149.8 %copy-start.36 = (f32[768]{0:T(1024)}, f32[768]{0:T(1024)S(1)}, u32[]{:S(2)}) copy-start(f32[768]{0:T(1024)S(1)} %convert_element_type.182) | copy-start | bytes 9220
  241.6 141.5 %copy-start.11 = (f32[256,768]{1,0:T(8,128)}, f32[256,768]{1,0:T(8,128)S(1)}, u32[]{:S(2)}) copy-start(f32[256,768]{1,0:T(8,128)S(1)} %get-tuple-element.397) | copy-start | bytes 2359300
  241.7 141.5 %copy-start.40 = (f32[256]{0:T(256)}, f32[256]{0:T(256)S(1)}, u32[]{:S(2)}) copy-start(f32[256]{0:T(256)S(1)} %broadcast_multiply_fusion.5) | copy-start | bytes 3076
  241.9 141.3 %copy-start.46 = (f32[256]{0:T(256)}, f32[256]{0:T(256)S(1)}, u32[]{:S(2)}) copy-start(f32[256]{0:T(256)S(1)} %add_rsqrt_fusion.1) | copy-start | bytes 3076
  370.7 7.4 slice-start.2
  370.7 4.7 copy-start.28
  370.7 7.4 slice-start.3
  370.7 7.4 copy-start.52
  375.2 2.9 copy-start.51
  376.4 4.5 slice-start
  378.1 2.8 copy-start.25
  378.1 2.8 slice-start.1
  380.9 2.3 copy-start.29
  380.9 3.1 copy-start.22
  384.0 6.9 copy-start.9
  385.5 15.8 %all-to-all-start.4 = ((bf16[256,4,192]{0,2,1:T(8,128)(2,1)}), bf16[256,4,192]{0,2,1:T(8,128)(2,1)S(1)}, u32[]{:S(2)}, u32[]{:S(2)}) async-start(bf16[256,4,192]{0,2,1:T(8,128)(2,1)} %bitcast.14), calls=%async_computation.4 | async-start | bytes 786432 | tf_op jit(solution)/shard_map/all_to_all | solution.py:282
  388.9 162.9 %reduce-scatter.13.cloned.1.call-start = ((), (), s32[]{:S(2)}) async-start(), calls=%async_computation.20 | async-start | bytes 2433024 | tf_op jit(solution)/shard_map/reduce_scatter | solution.py:308
  390.9 212.3 %reduce-scatter.19.cloned.1.call-start = ((), (), s32[]{:S(2)}) async-start(), calls=%async_computation.23 | async-start | bytes 2433024
  402.7 4.1 copy-start.19
  403.7 3.0 copy-start
  404.1 2.6 copy-start.2
  408.7 4.4 copy-start.1
  413.1 3.6 copy-start.6
  413.1 3.6 copy-start.8
  413.1 3.6 copy-start.20
  413.1 3.6 copy-start.35
  413.1 3.6 copy-start.39
  416.8 4.1 copy-start.19
  417.8 3.0 copy-start
  418.2 2.6 copy-start.2
  422.8 4.7 copy-start.1
  425.7 1.8 copy-start.3
  427.5 3.9 copy-start.6
  427.5 3.9 copy-start.8
  427.5 3.9 copy-start.20
  427.5 3.9 copy-start.35
  427.5 3.9 copy-start.39
  431.4 16.3 %copy-start.14 = (bf16[256,768]{1,0:T(8,128)(2,1)S(1)}, bf16[256,768]{1,0:T(8,128)(2,1)}, u32[]{:S(2)}) copy-start(bf16[256,768]{1,0:T(8,128)(2,1)} %param.22) | copy-start | bytes 1179652
  448.2 2.1 copy-start.4
  450.3 257.5 %reduce-scatter.21.cloned.1.call-start = ((), (), s32[]{:S(2)}) async-start(), calls=%async_computation.24 | async-start | bytes 2433024
  469.4 342.7 %reduce-scatter.23.cloned.1.call-start = ((), (), s32[]{:S(2)}) async-start(), calls=%async_computation.25 | async-start | bytes 2433024
  486.8 2.3 copy-start.12
  486.8 2.3 copy-start.37
  486.8 2.3 copy-start.41
  486.9 2.3 copy-start.47
  488.8 464.9 %reduce-scatter.15.cloned.1.call-start = ((), (), s32[]{:S(2)}) async-start(), calls=%async_computation.21 | async-start | bytes 9732096 | tf_op jit(solution)/shard_map/reduce_scatter | solution.py:312
  495.5 599.8 %reduce-scatter.17.cloned.1.call-start = ((), (), s32[]{:S(2)}) async-start(), calls=%async_computation.22 | async-start | bytes 9732096 | tf_op jit(solution)/shard_map/reduce_scatter | solution.py:314
  502.2 45.9 %copy-start.10 = (f32[256,768]{1,0:T(8,128)S(1)}, f32[256,768]{1,0:T(8,128)}, u32[]{:S(2)}) copy-start(f32[256,768]{1,0:T(8,128)} %copy-done.9) | copy-start | bytes 2359300
  502.3 47.8 %copy-start.21 = (bf16[768,768]{1,0:T(8,128)(2,1)S(1)}, bf16[768,768]{1,0:T(8,128)(2,1)}, u32[]{:S(2)}) copy-start(bf16[768,768]{1,0:T(8,128)(2,1)} %all-gather.9.cloned.1.call-done) | copy-start | bytes 3538948
  502.3 47.8 %copy-start.24 = (bf16[4,256,192]{1,2,0:T(8,128)(2,1)S(1)}, bf16[4,256,192]{1,2,0:T(8,128)(2,1)}, u32[]{:S(2)}) copy-start(bf16[4,256,192]{1,2,0:T(8,128)(2,1)} %copy-done.23) | copy-start | bytes 1179652
  548.2 2.4 copy-start.31
  (24 other events, 32.0 us)
Sparse Core Ops, SparseCore 0:
  11.4 56.7 all-gather.6
  71.6 53.9 all-gather.10
  129.0 53.8 all-gather.8
  186.1 53.6 all-gather.12
  243.0 62.4 all-gather.14
  308.8 61.8 all-gather.16
  395.6 103.1 reduce-scatter.12
  504.6 98.5 reduce-scatter.18
  609.1 98.5 reduce-scatter.20
  713.4 98.5 reduce-scatter.22
  818.5 135.2 reduce-scatter.14
  960.1 135.1 reduce-scatter.16
where the time goes:
time: 1110 us; the launch traced here: 1100 us
  waiting for transfers between devices  804 us (72%)
  blocking collectives  125 us (11%)
  matrix products  77.6 us (7%)
  other arithmetic  30.4 us (3%)
  local copies, waits for them, and re-layouts  30.3 us (3%)
  starting transfers between devices  19 us (2%)
  between operations  15.2 us (1%)
    unnamed x15, waiting for transfers between devices  260 us
    reduce_scatter x1, waiting for transfers between devices, on_device(): lax.psum_scatter(grad_inner_weight, ('fsdp', 'seq'), scatter_dimension=0,...  142 us
    reduce_scatter x1, waiting for transfers between devices, on_device(): lax.psum_scatter(grad_outer_weight, ('fsdp', 'seq'), scatter_dimension=0,...  142 us
    unnamed x2, blocking collectives  81.4 us
    all_gather x1, waiting for transfers between devices, on_device(): lax.all_gather(lowered[9], ('fsdp', 'seq'), axis=0, tiled=True)  63.6 us
    all_gather x1, waiting for transfers between devices, on_device(): lax.all_gather(lowered[11], ('fsdp', 'seq'), axis=0, tiled=True)  53.6 us
    all_gather x1, waiting for transfers between devices, on_device(): lax.all_gather(lowered[3], ('fsdp', 'seq'), axis=0, tiled=True)  51 us
    all_gather x1, waiting for transfers between devices, on_device(): lax.all_gather(lowered[2], ('fsdp', 'seq'), axis=0, tiled=True)  51 us
  transfers between devices with their start and end apart: 17, of which 13 were waited for; matrix products, arithmetic and copies ran while one was open for 10% of the time, Pallas kernels for 0%

commit v1 on v0

v1 whole, which is shorter than its diff:
```python
import functools

import jax
import jax.numpy as jnp
from jax import lax
from jax.sharding import PartitionSpec as P

HD = 64


EPSILON = 1e-12
NEGATIVE = -1e30


def product(left, right):
    return jnp.dot(left, right, preferred_element_type=jnp.float32)


def product_tn(left, right):
    return lax.dot_general(
        left, right, (((0,), (0,)), ((), ())), preferred_element_type=jnp.float32
    )


def product_nt(left, right):
    return lax.dot_general(
        left, right, (((1,), (1,)), ((), ())), preferred_element_type=jnp.float32
    )


def column_sum(values):
    return jnp.sum(values.astype(jnp.float32), axis=0)


def normalize(hidden, gain, shift):
    centred = hidden - jnp.mean(hidden, axis=-1, keepdims=True)
    scale = lax.rsqrt(jnp.mean(centred * centred, axis=-1, keepdims=True) + EPSILON)
    normed = centred * scale
    return (normed * gain + shift, normed, scale)


def normalize_back(grad_out, normed, scale, gain):
    grad_normed = grad_out * gain
    grad_hidden = scale * (
        grad_normed
        - jnp.mean(grad_normed, axis=-1, keepdims=True)
        - normed * jnp.mean(grad_normed * normed, axis=-1, keepdims=True)
    )
    return (grad_hidden, jnp.sum(grad_out * normed, axis=0), jnp.sum(grad_out, axis=0))


def attend_forward(queries, keys, values, segment):
    length, width = queries.shape
    heads = width // HD
    block = min(512, length)
    count = length // block
    scale = HD ** (-0.5)
    key_heads = keys.reshape(length, heads, HD)
    value_heads = values.reshape(length, heads, HD)
    query_blocks = queries.reshape(count, block, heads, HD)
    segment_blocks = segment.reshape(count, block)

    def one_block(inputs):
        query_block, segment_block = inputs
        scores = (
            jnp.einsum("qhd,khd->hqk", query_block, key_heads, preferred_element_type=jnp.float32)
            * scale
        )
        allowed = (segment_block[:, None] == segment[None, :])[None]
        masked = jnp.where(allowed, scores, NEGATIVE)
        peak = jnp.max(masked, axis=-1, keepdims=True)
        weights = jnp.where(allowed, jnp.exp(masked - peak), 0.0)
        total = jnp.sum(weights, axis=-1, keepdims=True)
        probs = (weights / total).astype(jnp.bfloat16)
        mixed = jnp.einsum("hqk,khd->qhd", probs, value_heads, preferred_element_type=jnp.float32)
        return (mixed.astype(jnp.bfloat16), (peak + jnp.log(total))[..., 0])

    mixed, logsum = lax.map(one_block, (query_blocks, segment_blocks))
    return (mixed.reshape(length, width), logsum)


def attend_back(queries, keys, values, segment, logsum, grad_mixed):
    length, width = queries.shape
    heads = width // HD
    block = min(512, length)
    count = length // block
    scale = HD ** (-0.5)
    key_heads = keys.reshape(length, heads, HD)
    value_heads = values.reshape(length, heads, HD)
    query_blocks = queries.reshape(count, block, heads, HD)
    grad_blocks = grad_mixed.reshape(count, block, heads, HD)
    segment_blocks = segment.reshape(count, block)

    def one_block(carry, inputs):
        key_total, value_total = carry
        query_block, segment_block, logsum_block, grad_block = inputs
        scores = (
            jnp.einsum("qhd,khd->hqk", query_block, key_heads, preferred_element_type=jnp.float32)
            * scale
        )
        allowed = (segment_block[:, None] == segment[None, :])[None]
        probs = jnp.where(allowed, jnp.exp(scores - logsum_block[..., None]), 0.0)
        grad_probs = jnp.einsum(
            "qhd,khd->hqk", grad_block, value_heads, preferred_element_type=jnp.float32
        )
        delta = jnp.sum(probs * grad_probs, axis=-1, keepdims=True)
        grad_scores = (probs * (grad_probs - delta)).astype(jnp.bfloat16)
        grad_query = (
            jnp.einsum("hqk,khd->qhd", grad_scores, key_heads, preferred_element_type=jnp.float32)
            * scale
        )
        key_total = (
            key_total
            + jnp.einsum(
                "hqk,qhd->khd", grad_scores, query_block, preferred_element_type=jnp.float32
            )
            * scale
        )
        value_total = value_total + jnp.einsum(
            "hqk,qhd->khd",
            probs.astype(jnp.bfloat16),
            grad_block,
            preferred_element_type=jnp.float32,
        )
        return ((key_total, value_total), grad_query.astype(jnp.bfloat16))

    start = jnp.zeros((length, heads, HD), jnp.float32)
    (key_total, value_total), grad_queries = lax.scan(
        one_block, (start, start), (query_blocks, segment_blocks, logsum, grad_blocks)
    )
    return (
        grad_queries.reshape(length, width),
        key_total.reshape(length, width).astype(jnp.bfloat16),
        value_total.reshape(length, width).astype(jnp.bfloat16),
    )


def hop(value, axis, bit, size):
    return lax.ppermute(value, axis, [(i, i ^ bit) for i in range(size)])


def pick(blocks, index):
    return lax.dynamic_index_in_dim(blocks, index, 0, keepdims=False)


def spread_seq(own):
    one = hop(own, "seq", 1, 4)
    three = hop(own, "seq", 3, 4)
    two = hop(three, "seq", 1, 4)
    return [own, one, two, three]


def spread_plane(blocks):
    from_x = hop(blocks, "fsdp", 2, 8)
    from_y = hop(blocks, "fsdp", 4, 8)
    far_low = hop(from_x[:2], "fsdp", 4, 8)
    far_high = hop(from_y[2:], "fsdp", 2, 8)
    parts = [[blocks], [from_x], [from_y], [far_low, far_high]]
    whole = []
    for part in parts:
        whole.append(part)
        whole.append([hop(piece, "fsdp", 1, 8) for piece in part])
    return [jnp.concatenate(part, axis=0) if len(part) > 1 else part[0] for part in whole]


def in_order(blocks, me):
    return jnp.stack([pick(blocks, j ^ me) for j in range(blocks.shape[0])])


def sum_plane(grad, me):
    theirs = jnp.stack([pick(grad, me ^ (2 * k + 1)) for k in range(4)])
    mine = [pick(grad, me ^ (2 * k)) for k in range(4)]
    got = hop(theirs, "fsdp", 1, 8)
    total = [mine[k] + got[k] for k in range(4)]
    half = total[3].shape[0] // 2
    far_y = hop(total[3][:half], "fsdp", 4, 8)
    far_x = hop(total[3][half:], "fsdp", 2, 8)
    to_x = jnp.concatenate([total[1][:half] + far_y, total[1][half:]], axis=0)
    to_y = jnp.concatenate([total[2][:half], total[2][half:] + far_x], axis=0)
    near_x = hop(to_x, "fsdp", 2, 8)
    near_y = hop(to_y, "fsdp", 4, 8)
    return total[0] + near_x + near_y


def sum_seq(blocks, z):
    far = hop(pick(blocks, z ^ 2), "seq", 1, 4)
    near = hop(pick(blocks, z ^ 1), "seq", 1, 4)
    last = hop(pick(blocks, z ^ 3) + far, "seq", 3, 4)
    return (
        pick(blocks, z).astype(jnp.float32)
        + near.astype(jnp.float32)
        + last.astype(jnp.float32)
    )


def gather_rows(own, fast, f, z):
    if not fast:
        return lax.all_gather(own, ("fsdp", "seq"), axis=0, tiled=True)
    rows, width = own.shape
    pieces = jnp.stack(spread_plane(jnp.stack(spread_seq(own))))
    pieces = in_order(pieces, f)
    pieces = jnp.stack([pick(pieces.swapaxes(0, 1), j ^ z) for j in range(4)], axis=1)
    return pieces.reshape(32 * rows, width)


def reduce_rows(grad, fast, f, z):
    if not fast:
        return lax.psum_scatter(
            grad.astype(jnp.float32), ("fsdp", "seq"), scatter_dimension=0, tiled=True
        )
    rows = grad.shape[0] // 32
    mine = sum_plane(grad.reshape(8, 4, rows, grad.shape[1]), f)
    return sum_seq(mine, z)


def on_device(
    sizes,
    tokens,
    segments,
    cotangent,
    query_weight,
    query_bias,
    key_weight,
    value_weight,
    value_bias,
    mixer_weight,
    mixer_bias,
    first_gain,
    first_shift,
    inner_weight,
    inner_bias,
    outer_weight,
    outer_bias,
    second_gain,
    second_shift,
):
    nf, nz = sizes
    fast = (nf, nz) == (8, 4)
    f, z = lax.axis_index("fsdp"), lax.axis_index("seq")
    low = jnp.bfloat16
    share, width = query_weight.shape
    wide = inner_weight.shape[1]
    cut = width // nz
    ratio = wide // width
    small = jnp.stack(
        [
            piece.astype(low)
            for piece in (
                query_bias,
                value_bias,
                mixer_bias,
                first_gain,
                first_shift,
                outer_bias,
                second_gain,
                second_shift,
            )
        ]
        + list(inner_bias.astype(low).reshape(ratio, share)),
        axis=1,
    )
    heads_of = [
        piece.astype(low).reshape(share, nz, cut) for piece in (query_weight, key_weight, value_weight)
    ]

    if fast:
        pieces = jnp.stack(spread_seq(tokens))
        rows_all = in_order(pieces, z).reshape(-1, width)
    else:
        rows_all = lax.all_gather(tokens, "seq", axis=0, tiled=True)

    def message(target):
        return jnp.concatenate(
            [lax.dynamic_index_in_dim(piece, target, 1, keepdims=False) for piece in heads_of] + [small],
            axis=1,
        )

    if fast:
        got = [message(z)] + [hop(message(z ^ k), "seq", k, 4) for k in (1, 2, 3)]
        got = jnp.stack(spread_plane(jnp.stack(got)))
        got = in_order(got, f)
        got = jnp.stack([pick(got.swapaxes(0, 1), j ^ z) for j in range(4)], axis=1)
        heads_full = got.reshape(width, -1)
    else:
        packed = jnp.concatenate(
            [piece.astype(low) for piece in (query_weight, key_weight, value_weight)] + [small], axis=1
        )
        packed = lax.all_gather(packed, ("fsdp", "seq"), axis=0, tiled=True)
        heads_full = jnp.concatenate(
            [
                lax.dynamic_slice_in_dim(packed, k * width + z * cut, cut, axis=1)
                for k in range(3)
            ]
            + [packed[:, 3 * width :]],
            axis=1,
        )
    small_full = heads_full[:, 3 * cut :].astype(jnp.float32).T
    (qbias, vbias, mbias, gain_one, shift_one, obias, gain_two, shift_two) = [
        small_full[k] for k in range(8)
    ]
    ibias = (
        small_full[8:].reshape(ratio, nf * nz, share).swapaxes(0, 1).reshape(wide)
    )
    qbias = lax.dynamic_slice_in_dim(qbias, z * cut, cut)
    vbias = lax.dynamic_slice_in_dim(vbias, z * cut, cut)

    packed = jnp.concatenate(
        [mixer_weight.astype(low)]
        + [inner_weight[:, k * width : (k + 1) * width].astype(low) for k in range(ratio)],
        axis=0,
    )
    packed = gather_rows(packed, fast, f, z).reshape(nf * nz, 1 + ratio, share, width)
    mixer_full = packed[:, 0].reshape(width, width)
    inner_full = jnp.concatenate(
        [packed[:, 1 + k].reshape(width, width) for k in range(ratio)], axis=1
    )
    outer_full = gather_rows(outer_weight.astype(low), fast, f, z)

    projected = product(rows_all, heads_full[:, : 3 * cut])
    query_heads = (projected[:, :cut] + qbias).astype(low)
    key_heads = projected[:, cut : 2 * cut].astype(low)
    value_heads = (projected[:, 2 * cut :] + vbias).astype(low)
    segment = segments[0]
    mixed_heads, logsum = attend_forward(query_heads, key_heads, value_heads, segment)
    mixed_rows = lax.all_to_all(mixed_heads, "seq", split_axis=0, concat_axis=1, tiled=True)
    attended = product(mixed_rows, mixer_full) + mbias
    first_out, first_normed, first_scale = normalize(
        tokens.astype(jnp.float32) + attended, gain_one, shift_one
    )
    first_low = first_out.astype(low)
    inner_pre = product(first_low, inner_full) + ibias
    active, gelu_back = jax.vjp(lambda value: jax.nn.gelu(value, approximate=False), inner_pre)
    active_low = active.astype(low)
    outer = product(active_low, outer_full) + obias
    result, second_normed, second_scale = normalize(first_out + outer, gain_two, shift_two)
    grad_second, grad_gain_two, grad_shift_two = normalize_back(
        cotangent.astype(jnp.float32), second_normed, second_scale, gain_two
    )
    grad_outer = grad_second.astype(low)
    grad_outer_weight = product_tn(active_low, grad_outer).astype(low)
    grad_outer_bias = column_sum(grad_outer)
    outer_sum = reduce_rows(grad_outer_weight, fast, f, z)
    grad_inner = gelu_back(product_nt(grad_outer, outer_full))[0].astype(low)
    grad_inner_weight = product_tn(first_low, grad_inner).astype(low)
    grad_inner_bias = column_sum(grad_inner)
    grad_first_out = grad_second + product_nt(grad_inner, inner_full)
    grad_residual, grad_gain_one, grad_shift_one = normalize_back(
        grad_first_out, first_normed, first_scale, gain_one
    )
    grad_attended = grad_residual.astype(low)
    grad_mixer_weight = product_tn(mixed_rows, grad_attended).astype(low)
    grad_mixer_bias = column_sum(grad_attended)
    packed = jnp.concatenate(
        [grad_mixer_weight.reshape(nf * nz, 1, share, width)]
        + [
            grad_inner_weight[:, k * width : (k + 1) * width].reshape(nf * nz, 1, share, width)
            for k in range(ratio)
        ],
        axis=1,
    ).reshape(-1, width)
    packed_sum = reduce_rows(packed, fast, f, z)
    mixer_sum = packed_sum[:share]
    inner_sum = jnp.concatenate(
        [packed_sum[(1 + k) * share : (2 + k) * share] for k in range(ratio)], axis=1
    )
    grad_mixed = product_nt(grad_attended, mixer_full).astype(low)
    grad_mixed_heads = lax.all_to_all(grad_mixed, "seq", split_axis=1, concat_axis=0, tiled=True)
    grad_query_heads, grad_key_heads, grad_value_heads = attend_back(
        query_heads, key_heads, value_heads, segment, logsum, grad_mixed_heads
    )
    grads = jnp.concatenate([grad_query_heads, grad_key_heads, grad_value_heads], axis=1)
    heads_grad = product_tn(rows_all, grads).astype(low)
    zero = jnp.zeros((width,), jnp.float32)
    small_grad = jnp.stack(
        [
            lax.dynamic_update_slice_in_dim(zero, column_sum(grad_query_heads), z * cut, 0),
            lax.dynamic_update_slice_in_dim(zero, column_sum(grad_value_heads), z * cut, 0),
            grad_mixer_bias,
            grad_gain_one,
            grad_shift_one,
            grad_outer_bias,
            grad_gain_two,
            grad_shift_two,
        ]
        + list(grad_inner_bias.reshape(nf * nz, ratio, share).swapaxes(0, 1).reshape(ratio, width)),
        axis=1,
    ).astype(low)
    heads_grad = jnp.concatenate([heads_grad, small_grad], axis=1)
    if fast:
        mine = sum_plane(heads_grad.reshape(8, 4, share, -1), f)
        parts = [pick(mine, z)] + [hop(pick(mine, z ^ k), "seq", k, 4) for k in (1, 2, 3)]
        parts = in_order(jnp.stack(parts), z)
    else:
        mine = lax.psum_scatter(heads_grad, "fsdp", scatter_dimension=0, tiled=True)
        parts = lax.all_to_all(
            mine.reshape(nz, share, -1), "seq", split_axis=0, concat_axis=0, tiled=True
        )
    parts = parts.astype(jnp.float32)
    projections = [
        jnp.concatenate([parts[j, :, k * cut : (k + 1) * cut] for j in range(nz)], axis=1)
        for k in range(3)
    ]
    small_sum = jnp.sum(parts[:, :, 3 * cut :], axis=0).T
    back_rows = product_nt(grads, heads_full[:, : 3 * cut]).astype(low).reshape(nz, -1, width)
    if fast:
        back = sum_seq(back_rows, z)
    else:
        back = lax.psum_scatter(back_rows, "seq", scatter_dimension=0, tiled=True)[0]
    grad_tokens = grad_residual + back
    return (
        result.astype(low),
        grad_tokens.astype(low),
        projections[0],
        small_sum[0],
        projections[1],
        projections[2],
        small_sum[1],
        mixer_sum,
        small_sum[2],
        small_sum[3],
        small_sum[4],
        inner_sum,
        small_sum[8:].reshape(-1),
        outer_sum,
        small_sum[5],
        small_sum[6],
        small_sum[7],
    )


def solution(mesh):
    placed = (
        P(("fsdp", "seq"), None),
        P("fsdp", None),
        P(("fsdp", "seq"), None),
        P(("fsdp", "seq"), None),
        P(("fsdp", "seq")),
        P(("fsdp", "seq"), None),
        P(("fsdp", "seq"), None),
        P(("fsdp", "seq")),
        P(("fsdp", "seq"), None),
        P(("fsdp", "seq")),
        P(("fsdp", "seq")),
        P(("fsdp", "seq")),
        P(("fsdp", "seq"), None),
        P(("fsdp", "seq")),
        P(("fsdp", "seq"), None),
        P(("fsdp", "seq")),
        P(("fsdp", "seq")),
        P(("fsdp", "seq")),
    )
    sizes = (mesh.shape["fsdp"], mesh.shape["seq"])
    return jax.shard_map(
        functools.partial(on_device, sizes),
        mesh=mesh,
        in_specs=placed,
        out_specs=(
            P(("fsdp", "seq"), None),
            P(("fsdp", "seq"), None),
            P(("fsdp", "seq"), None),
            P(("fsdp", "seq")),
            P(("fsdp", "seq"), None),
            P(("fsdp", "seq"), None),
            P(("fsdp", "seq")),
            P(("fsdp", "seq"), None),
            P(("fsdp", "seq")),
            P(("fsdp", "seq")),
            P(("fsdp", "seq")),
            P(("fsdp", "seq"), None),
            P(("fsdp", "seq")),
            P(("fsdp", "seq"), None),
            P(("fsdp", "seq")),
            P(("fsdp", "seq")),
            P(("fsdp", "seq")),
        ),
        check_vma=False,
    )
```

time: 1110 us -> 346 us (0.31)
  waiting for transfers between devices: 804 us -> 82.9 us
  blocking collectives: 125 us -> 0 us
  starting transfers between devices: 19 us -> 96.4 us
  other arithmetic: 30.4 us -> 54.5 us
  matrix products: 77.6 us -> 54.5 us
  local copies, waits for them, and re-layouts: 30.3 us -> 50.3 us
  between operations: 15.2 us -> 2.64 us
    reduce_scatter x3 -> x0, waiting for transfers between devices: 283 us -> none  [the longest x1 142 us: on_device(): lax.psum_scatter(grad_inner_weight, ('fsdp', 'seq'), scatter_dimension=0,...]
    unnamed x15 -> x0, waiting for transfers between devices: 260 us -> none
    all_gather x6 -> x0, waiting for transfers between devices: 241 us -> none  [the longest x1 63.6 us: on_device(): lax.all_gather(lowered[9], ('fsdp', 'seq'), axis=0, tiled=True)]
    ppermute x0 -> x66, waiting for transfers between devices: none -> 82.9 us  [hop(): return lax.ppermute(value, axis, [(i, i ^ bit) for i in range(size)])]
    unnamed x2 -> x0, blocking collectives: 81.4 us -> none
    ppermute x0 -> x66, starting transfers between devices: none -> 76.6 us  [hop(): return lax.ppermute(value, axis, [(i, i ^ bit) for i in range(size)])]
    all_to_all x3 -> x0, blocking collectives: 43.9 us -> none  [the longest x1 15.4 us: on_device(): lax.all_to_all(grad_key_heads, 'seq', split_axis=0, concat_axis=1, tiled=...]
    another operation x0 -> x25, other arithmetic: none -> 17.1 us  [the longest x8 5.25 us: on_device(): jnp.stack([piece.astype(low) for piece in (query_bias, value_bias, mixer_...]
  transfers between devices with their start and end apart: 17 -> 68, of which waited for: 13 -> 27; matrix products, arithmetic and copies ran while one was open for 10% -> 34% of each run, Pallas kernels for 0% -> 0%
where the time goes in v1:
time: 346 us; the launch traced here: 341 us
  starting transfers between devices  96.4 us (28%)
  waiting for transfers between devices  82.9 us (24%)
  other arithmetic  54.5 us (16%)
  matrix products  54.5 us (16%)
  local copies, waits for them, and re-layouts  50.3 us (15%)
    ppermute x66, waiting for transfers between devices, hop(): return lax.ppermute(value, axis, [(i, i ^ bit) for i in range(size)])  82.9 us
    ppermute x66, starting transfers between devices, hop(): return lax.ppermute(value, axis, [(i, i ^ bit) for i in range(size)])  76.6 us
    unnamed x157, local copies, waits for them, and re-layouts  17.4 us
    all_to_all x1, starting transfers between devices, on_device(): lax.all_to_all(mixed_heads, 'seq', split_axis=0, concat_axis=1, tiled=True)  14.9 us
    dot_general x4, matrix products, product(): return jnp.dot(left, right, preferred_element_type=jnp.float32)  12.6 us
    dot_general x4, matrix products, product_tn(): lax.dot_general(left, right, (((0,), (0,)), ((), ())), preferred_element_...  11.5 us
    dot_general x4, matrix products, product_nt(): lax.dot_general(left, right, (((1,), (1,)), ((), ())), preferred_element_...  8.39 us
  transfers between devices with their start and end apart: 68, of which 27 were waited for; matrix products, arithmetic and copies ran while one was open for 34% of the time, Pallas kernels for 0%

profile of v1, /device:TPU:0, one launch (start us, length us, event | category | flops | bytes accessed | tf_op | source)
XLA Modules:
  0.0 341.5 jit_solution(10547446052001975019)
XLA Ops:
  0.7 1.7 convert_element_type.208
  2.4 3.1 collective-permute-start.27
  5.5 2.5 collective-permute-start.28
  21.2 2.3 collective-permute-start.3
  29.3 1.8 collective-permute-done.7
  44.3 1.8 collective-permute-start
  46.1 2.8 collective-permute-start.17
  48.9 9.1 %collective-permute-done.1 = bf16[256,768]{1,0:T(8,128)(2,1)} collective-permute-done((bf16[256,768]{1,0:T(8,128)(2,1)S(1)}, bf16[256,768]{1,0:T(8,128)(2,1)}, u32[]{:S(2)}, u32[]{:S(2)}) %collective-permute-start.1) | collective-permute-done | bytes 393248 | tf_op jit(solution)/shard_map/ppermute | solution.py:139
  58.0 7.2 %collective-permute-start.2 = (bf16[256,768]{1,0:T(8,128)(2,1)}, bf16[256,768]{1,0:T(8,128)(2,1)S(1)}, u32[]{:S(2)}, u32[]{:S(2)}) collective-permute-start(bf16[256,768]{1,0:T(8,128)(2,1)} %collective-permute-done.1), channel_id=1, source_target_pairs={{0,1},{1,0},{2,3},{3,2},{4,5},{5,4},{6,7},{7,6},{8,9},{9,8},{10,11... | collective-permute-start | bytes 1179656 | tf_op jit(solution)/shard_map/ppermute | solution.py:139
  68.5 4.4 %collective-permute-done.17 = bf16[120,768]{1,0:T(8,128)(2,1)S(1)} collective-permute-done((bf16[120,768]{1,0:T(8,128)(2,1)S(1)}, bf16[120,768]{1,0:T(8,128)(2,1)S(1)}, u32[]{:S(2)}, u32[]{:S(2)}) %collective-permute-start.17) | collective-permute-done | bytes 184352 | tf_op jit(solution)/shard_map/ppermute | solution.py:139
  77.7 3.5 %collective-permute-done.2 = bf16[256,768]{1,0:T(8,128)(2,1)S(1)} collective-permute-done((bf16[256,768]{1,0:T(8,128)(2,1)}, bf16[256,768]{1,0:T(8,128)(2,1)S(1)}, u32[]{:S(2)}, u32[]{:S(2)}) %collective-permute-start.2) | collective-permute-done | bytes 393248 | tf_op jit(solution)/shard_map/ppermute | solution.py:139
  84.6 14.4 %while.27 = (s32[]{:T(128)}, bf16[2,512,3,64]{1,3,2,0:T(8,128)(2,1)S(1)}, f32[2,3,512]{2,1,0:T(4,128)}, s32[2,512]{1,0:T(2,128)S(1)}, s32[1,1024]{1,0:T(1,128)S(...) while((s32[]{:T(128)}, ...), condition=%wide.region_3.4_spmd, body=%wide.region_0.3_spmd.sunk | while | flops 425294336 | bytes 22216820 | solution.py:78
  86.4 2.3 fusion.152
  88.7 2.5 fusion.153
  93.6 2.3 fusion.152
  95.9 2.5 fusion.153
  100.4 14.9 %all-to-all-start = ((bf16[4,256,192]{1,2,0:T(8,128)(2,1)}), bf16[4,256,192]{1,2,0:T(8,128)(2,1)S(1)}, u32[]{:S(2)}, u32[]{:S(2)}) async-start(bf16[4,256,192]{1,2,0:T(8,128)(2,1)} %copy.326), calls=%async_computation | async-start | bytes 786432 | tf_op jit(solution)/shard_map/all_to_all | solution.py:325
  117.0 1.9 bitcast_dynamic-update-slice_fusion.11
  118.9 2.0 bitcast_dynamic-update-slice_fusion.10
  125.0 2.0 bitcast_dynamic-update-slice_fusion.5
  128.0 6.9 %collective-permute-done.21 = bf16[4,120,768]{2,1,0:T(8,128)(2,1)S(1)} collective-permute-done((bf16[4,120,768]{2,1,0:T(8,128)(2,1)}, bf16[4,120,768]{2,1,0:T(8,128)(2,1)S(1)}, u32[]{:S(2)}, u32[]{:S(2)}) %collective-permute-start.21) | collective-permute-done | bytes 737312 | tf_op jit(solution)/shard_map/ppermute | solution.py:139
  139.0 2.2 collective-permute-done.35
  141.9 2.0 collective-permute-done.37
  144.6 4.0 %collective-permute-done.23 = bf16[2,120,768]{2,1,0:T(8,128)(2,1)S(1)} collective-permute-done((bf16[2,120,768]{2,1,0:T(8,128)(2,1)S(1)}, bf16[2,120,768]{2,1,0:T(8,128)(2,1)S(1)}, u32[]{:S(2)}, u32[]{:S(2)}) %collective-permute-start.23) | collective-permute-done | bytes 368672 | tf_op jit(solution)/shard_map/ppermute | solution.py:139
  149.7 2.7 pad_maximum_fusion.2
  155.9 2.2 fusion.106
  160.6 9.3 %multiply_convert_fusion.1 = (bf16[256,3072]{1,0:T(8,128)(2,1)S(1)}, f32[256,3072]{1,0:T(8,128)S(1)}, f32[256,3072]{1,0:T(8,128)S(1)}) fusion(f32[3072]{0:T(1024)S(1)} %copy-done.39, bf16[768,768]{1,0:T(8,128)(2,1)S(1)} %bitcast.458, bf16[768,768]{1,0:T(8,128)(2,1)S(1)} %bitcast.460, bf16[768,768]{1,0:T(8,128)(2,1)S(1)} %bitcast.462, ...), kind=kOutput, calls=%fused_computation.62 | convolution fusion | flops 1279721472 | bytes 13389824 | tf_op jit(solution)/shard_map/dot_general | solution.py:16
  173.9 3.0 fusion.111
  176.9 2.1 multiply_reduce_fusion.1
  181.9 3.7 %convolution_convert_fusion.1 = bf16[768,3072]{1,0:T(8,128)(2,1)} fusion(bf16[256,3072]{1,0:T(8,128)(2,1)S(1)} %get-tuple-element.442, f32[256,768]{1,0:T(8,128)S(1)} %get-tuple-element.436, f32[768]{0:T(1024)S(1)} %get-tuple-element.265, f32[768]{0:T(1024)S(1)} %get-tuple-element.266, f32[256]{0:T(256)S(1)} %add_rsqrt_fusion.1, ...), kind=kOutput, calls=%fused_computation.55 | convolution fusion | flops 1211301888 | bytes 7086080 | tf_op jit(solution)/shard_map/dot_general | solution.py:20
  185.6 3.7 %convolution_convert_fusion = bf16[3072,768]{1,0:T(8,128)(2,1)} fusion(bf16[256,3072]{1,0:T(8,128)(2,1)S(1)} %get-tuple-element.324, f32[256,768]{1,0:T(8,128)S(1)} %get-tuple-element.319), kind=kOutput, calls=%fused_computation.54 | convolution fusion | flops 1210515456 | bytes 7077888 | tf_op jit(solution)/shard_map/dot_general | solution.py:20
  192.6 4.9 %all-to-all-start.1 = ((bf16[256,4,192]{0,2,1:T(8,128)(2,1)}), bf16[256,4,192]{0,2,1:T(8,128)(2,1)S(1)}, u32[]{:S(2)}, u32[]{:S(2)}) async-start(bf16[256,4,192]{0,2,1:T(8,128)(2,1)} %bitcast.75), calls=%async_computation.1 | async-start | bytes 786432 | tf_op jit(solution)/shard_map/all_to_all | solution.py:367
  200.5 2.7 fusion.107
  203.2 1.8 constant_dynamic-slice_fusion.5
  205.0 1.7 pad_maximum_fusion.4
  207.5 2.5 copy-done.1
  210.1 1.7 constant_dynamic-slice_fusion.9
  214.2 20.6 %while.28 = (s32[]{:T(128)}, f32[1024,3,64]{0,2,1:T(8,128)S(1)}, f32[1024,3,64]{0,2,1:T(8,128)}, bf16[2,512,3,64]{1,3,2,0:T(8,128)(2,1)S(1)}, bf16[2,512,3,64]{1...) while((s32[]{:T(128)}, f32[1024,3,64]{0,2,1:T(8,128)S(1)}, ...), condition=%wide.region_14.15_spmd.clone, body=%wide.region_12.14_spmd.clone.sunk | while | flops 1031928320 | bytes 60940512 | solution.py:128
  218.1 2.6 multiply_reduce_fusion.7
  220.7 1.9 multiply_convert_fusion.3
  228.4 2.6 multiply_reduce_fusion.7
  231.0 1.9 multiply_convert_fusion.3
  236.8 2.5 convolution_convert_fusion.4
  241.2 2.8 convolution_convert_fusion.2
  244.8 2.1 collective-permute-start.40
  254.4 1.9 pad_maximum_fusion.3
  259.0 2.3 collective-permute-start.49
  261.5 2.0 collective-permute-start.47
  270.9 2.3 slice_add_fusion.8
  273.3 1.7 collective-permute-start.61
  275.4 4.8 %collective-permute-done.61 = bf16[2,96,768]{2,1,0:T(8,128)(2,1)S(1)} collective-permute-done((bf16[2,96,768]{2,1,0:T(8,128)(2,1)S(1)}, bf16[2,96,768]{2,1,0:T(8,128)(2,1)S(1)}, u32[]{:S(2)}, u32[]{:S(2)}) %collective-permute-start.61) | collective-permute-done | bytes 294944 | tf_op jit(solution)/shard_map/ppermute | solution.py:139
  280.3 2.1 collective-permute-start.62
  282.3 2.1 collective-permute-done.59
  284.7 1.8 slice_add_fusion.4
  286.5 2.1 collective-permute-start.53
  288.6 12.0 %collective-permute-done.53 = bf16[2,120,768]{2,1,0:T(8,128)(2,1)S(1)} collective-permute-done((bf16[2,120,768]{2,1,0:T(8,128)(2,1)S(1)}, bf16[2,120,768]{2,1,0:T(8,128)(2,1)S(1)}, u32[]{:S(2)}, u32[]{:S(2)}) %collective-permute-start.53) | collective-permute-done | bytes 368672 | tf_op jit(solution)/shard_map/ppermute | solution.py:139
  302.3 9.8 %collective-permute-done.51 = bf16[2,120,768]{2,1,0:T(8,128)(2,1)S(1)} collective-permute-done((bf16[2,120,768]{2,1,0:T(8,128)(2,1)S(1)}, bf16[2,120,768]{2,1,0:T(8,128)(2,1)S(1)}, u32[]{:S(2)}, u32[]{:S(2)}) %collective-permute-start.51) | collective-permute-done | bytes 368672 | tf_op jit(solution)/shard_map/ppermute | solution.py:139
  315.1 1.9 fusion.66
  320.5 3.0 collective-permute-done.54
  323.5 1.8 collective-permute-done.52
  328.1 2.6 collective-permute-start.65
  330.7 1.7 collective-permute-done.56
  332.4 2.5 collective-permute-start.57
  337.1 2.8 collective-permute-done.57
  (477 shorter events, 133.5 us)
Async XLA Ops:
  2.4 41.9 %collective-permute-start.27 = (bf16[96,768]{1,0:T(8,128)(2,1)}, bf16[96,768]{1,0:T(8,128)(2,1)S(1)}, u32[]{:S(2)}, u32[]{:S(2)}) collective-permute-start(bf16[96,768]{1,0:T(8,128)(2,1)} %convert_element_type.208), channel_id=1, source_target_pairs={{0,1},{1,0},{2,3},{3,2},{4,5},{5,4},{6,7},{7,6},{8,9},{9,8},{10,11... | collective-permute-start | bytes 442376 | tf_op jit(solution)/shard_map/ppermute | solution.py:139
  5.5 33.3 %collective-permute-start.28 = (bf16[96,768]{1,0:T(8,128)(2,1)}, bf16[96,768]{1,0:T(8,128)(2,1)S(1)}, u32[]{:S(2)}, u32[]{:S(2)}) collective-permute-start(bf16[96,768]{1,0:T(8,128)(2,1)} %convert_element_type.208), channel_id=1, source_target_pairs={{0,3},{1,2},{2,1},{3,0},{4,7},{5,6},{6,5},{7,4},{8,11},{9,10},{10,... | collective-permute-start | bytes 442376 | tf_op jit(solution)/shard_map/ppermute | solution.py:139
  18.7 7.4 %collective-permute-start.5 = (bf16[24,588]{1,0:T(8,128)(2,1)S(1)}, bf16[24,588]{1,0:T(8,128)(2,1)S(1)}, u32[]{:S(2)}, u32[]{:S(2)}) collective-permute-start(bf16[24,588]{1,0:T(8,128)(2,1)S(1)} %concatenate.83), channel_id=1, source_target_pairs={{0,3},{1,2},{2,1},{3,0},{4,7},{5,6},{6,5},{7,4},{8,11},{9,10},{10,... | collective-permute-start | bytes 84680 | tf_op jit(solution)/shard_map/ppermute | solution.py:139
  20.2 5.9 %collective-permute-start.4 = (bf16[24,588]{1,0:T(8,128)(2,1)S(1)}, bf16[24,588]{1,0:T(8,128)(2,1)S(1)}, u32[]{:S(2)}, u32[]{:S(2)}) collective-permute-start(bf16[24,588]{1,0:T(8,128)(2,1)S(1)} %concatenate.82), channel_id=1, source_target_pairs={{0,2},{1,3},{2,0},{3,1},{4,6},{5,7},{6,4},{7,5},{8,10},{9,11},{10,... | collective-permute-start | bytes 84680 | tf_op jit(solution)/shard_map/ppermute | solution.py:139
  21.2 4.9 %collective-permute-start.3 = (bf16[24,588]{1,0:T(8,128)(2,1)S(1)}, bf16[24,588]{1,0:T(8,128)(2,1)S(1)}, u32[]{:S(2)}, u32[]{:S(2)}) collective-permute-start(bf16[24,588]{1,0:T(8,128)(2,1)S(1)} %concatenate.81), channel_id=1, source_target_pairs={{0,1},{1,0},{2,3},{3,2},{4,5},{5,4},{6,7},{7,6},{8,9},{9,8},{10,11... | collective-permute-start | bytes 84680 | tf_op jit(solution)/shard_map/ppermute | solution.py:139
  26.2 4.9 %collective-permute-start.7 = (bf16[4,24,588]{2,1,0:T(8,128)(2,1)S(1)}, bf16[4,24,588]{2,1,0:T(8,128)(2,1)S(1)}, u32[]{:S(2)}, u32[]{:S(2)}) collective-permute-start(bf16[4,24,588]{2,1,0:T(8,128)(2,1)S(1)} %pad_maximum_fusion.21), channel_id=1, source_target_pairs={{0,8},{4,12},{8,0},{12,4},{16,24},{20,28},{24,16},{28,20},{1,9},{5... | collective-permute-start | bytes 338696 | tf_op jit(solution)/shard_map/ppermute | solution.py:139
  27.7 6.7 %collective-permute-start.6 = (bf16[4,24,588]{2,1,0:T(8,128)(2,1)S(1)}, bf16[4,24,588]{2,1,0:T(8,128)(2,1)S(1)}, u32[]{:S(2)}, u32[]{:S(2)}) collective-permute-start(bf16[4,24,588]{2,1,0:T(8,128)(2,1)S(1)} %pad_maximum_fusion.21), channel_id=1, source_target_pairs={{0,4},{4,0},{8,12},{12,8},{16,20},{20,16},{24,28},{28,24},{1,5},{5... | collective-permute-start | bytes 338696 | tf_op jit(solution)/shard_map/ppermute | solution.py:139
  27.7 6.2 %collective-permute-start.9 = (bf16[4,24,588]{2,1,0:T(8,128)(2,1)S(1)}, bf16[4,24,588]{2,1,0:T(8,128)(2,1)S(1)}, u32[]{:S(2)}, u32[]{:S(2)}) collective-permute-start(bf16[4,24,588]{2,1,0:T(8,128)(2,1)S(1)} %pad_maximum_fusion.21), channel_id=1, source_target_pairs={{0,16},{4,20},{8,24},{12,28},{16,0},{20,4},{24,8},{28,12},{1,17},{... | collective-permute-start | bytes 338696 | tf_op jit(solution)/shard_map/ppermute | solution.py:139
  31.1 4.9 %collective-permute-start.11 = (bf16[2,24,588]{2,1,0:T(8,128)(2,1)S(1)}, bf16[2,24,588]{2,1,0:T(8,128)(2,1)S(1)}, u32[]{:S(2)}, u32[]{:S(2)}) collective-permute-start(bf16[2,24,588]{2,1,0:T(8,128)(2,1)S(1)} %slice.450), channel_id=1, source_target_pairs={{0,16},{4,20},{8,24},{12,28},{16,0},{20,4},{24,8},{28,12},{1,17},{... | collective-permute-start | bytes 169352 | tf_op jit(solution)/shard_map/ppermute | solution.py:139
  33.9 4.2 %collective-permute-start.12 = (bf16[2,24,588]{2,1,0:T(8,128)(2,1)S(1)}, bf16[2,24,588]{2,1,0:T(8,128)(2,1)S(1)}, u32[]{:S(2)}, u32[]{:S(2)}) collective-permute-start(bf16[2,24,588]{2,1,0:T(8,128)(2,1)S(1)} %slice.451), channel_id=1, source_target_pairs={{0,8},{4,12},{8,0},{12,4},{16,24},{20,28},{24,16},{28,20},{1,9},{5... | collective-permute-start | bytes 169352 | tf_op jit(solution)/shard_map/ppermute | solution.py:139
  36.0 10.1 %collective-permute-start.16 = (bf16[120,768]{1,0:T(8,128)(2,1)S(1)}, bf16[120,768]{1,0:T(8,128)(2,1)S(1)}, u32[]{:S(2)}, u32[]{:S(2)}) collective-permute-start(bf16[120,768]{1,0:T(8,128)(2,1)S(1)} %constant_dynamic-update-slice_fusion), channel_id=1, source_target_pairs={{0,3},{1,2},{2,1},{3,0},{4,7},{5,6},{6,5},{7,4},{8,11},{9,10},{10,... | collective-permute-start | bytes 552968 | tf_op jit(solution)/shard_map/ppermute | solution.py:139
  38.2 3.3 collective-permute-start.14
  38.7 29.7 %collective-permute-start.15 = (bf16[120,768]{1,0:T(8,128)(2,1)S(1)}, bf16[120,768]{1,0:T(8,128)(2,1)S(1)}, u32[]{:S(2)}, u32[]{:S(2)}) collective-permute-start(bf16[120,768]{1,0:T(8,128)(2,1)S(1)} %constant_dynamic-update-slice_fusion), channel_id=1, source_target_pairs={{0,1},{1,0},{2,3},{3,2},{4,5},{5,4},{6,7},{7,6},{8,9},{9,8},{10,11... | collective-permute-start | bytes 552968 | tf_op jit(solution)/shard_map/ppermute | solution.py:139
  40.1 17.9 %collective-permute-start.1 = (bf16[256,768]{1,0:T(8,128)(2,1)S(1)}, bf16[256,768]{1,0:T(8,128)(2,1)}, u32[]{:S(2)}, u32[]{:S(2)}) collective-permute-start(bf16[256,768]{1,0:T(8,128)(2,1)S(1)} %copy-done.11), channel_id=1, source_target_pairs={{0,3},{1,2},{2,1},{3,0},{4,7},{5,6},{6,5},{7,4},{8,11},{9,10},{10,... | collective-permute-start | bytes 1179656 | tf_op jit(solution)/shard_map/ppermute | solution.py:139
  41.5 23.7 %collective-permute-start.29 = (bf16[96,768]{1,0:T(8,128)(2,1)S(1)}, bf16[96,768]{1,0:T(8,128)(2,1)S(1)}, u32[]{:S(2)}, u32[]{:S(2)}) collective-permute-start(bf16[96,768]{1,0:T(8,128)(2,1)S(1)} %collective-permute-done.28), channel_id=1, source_target_pairs={{0,1},{1,0},{2,3},{3,2},{4,5},{5,4},{6,7},{7,6},{8,9},{9,8},{10,11... | collective-permute-start | bytes 442376 | tf_op jit(solution)/shard_map/ppermute | solution.py:139
  44.3 32.0 %collective-permute-start = (bf16[256,768]{1,0:T(8,128)(2,1)S(1)}, bf16[256,768]{1,0:T(8,128)(2,1)S(1)}, u32[]{:S(2)}, u32[]{:S(2)}) collective-permute-start(bf16[256,768]{1,0:T(8,128)(2,1)S(1)} %copy-done.11), channel_id=1, source_target_pairs={{0,1},{1,0},{2,3},{3,2},{4,5},{5,4},{6,7},{7,6},{8,9},{9,8},{10,11... | collective-permute-start | bytes 1179656 | tf_op jit(solution)/shard_map/ppermute | solution.py:139
  46.1 26.8 %collective-permute-start.17 = (bf16[120,768]{1,0:T(8,128)(2,1)S(1)}, bf16[120,768]{1,0:T(8,128)(2,1)S(1)}, u32[]{:S(2)}, u32[]{:S(2)}) collective-permute-start(bf16[120,768]{1,0:T(8,128)(2,1)S(1)} %collective-permute-done.16), channel_id=1, source_target_pairs={{0,1},{1,0},{2,3},{3,2},{4,5},{5,4},{6,7},{7,6},{8,9},{9,8},{10,11... | collective-permute-start | bytes 552968 | tf_op jit(solution)/shard_map/ppermute | solution.py:139
  58.0 23.2 %collective-permute-start.2 = (bf16[256,768]{1,0:T(8,128)(2,1)}, bf16[256,768]{1,0:T(8,128)(2,1)S(1)}, u32[]{:S(2)}, u32[]{:S(2)}) collective-permute-start(bf16[256,768]{1,0:T(8,128)(2,1)} %collective-permute-done.1), channel_id=1, source_target_pairs={{0,1},{1,0},{2,3},{3,2},{4,5},{5,4},{6,7},{7,6},{8,9},{9,8},{10,11... | collective-permute-start | bytes 1179656 | tf_op jit(solution)/shard_map/ppermute | solution.py:139
  66.1 49.2 %collective-permute-start.31 = (bf16[4,96,768]{2,1,0:T(8,128)(2,1)}, bf16[4,96,768]{2,1,0:T(8,128)(2,1)}, u32[]{:S(2)}, u32[]{:S(2)}) collective-permute-start(bf16[4,96,768]{2,1,0:T(8,128)(2,1)} %pad_maximum_fusion.14), channel_id=1, source_target_pairs={{0,8},{4,12},{8,0},{12,4},{16,24},{20,28},{24,16},{28,20},{1,9},{5... | collective-permute-start | bytes 1769480 | tf_op jit(solution)/shard_map/ppermute | solution.py:139
  68.5 48.4 %collective-permute-start.30 = (bf16[4,96,768]{2,1,0:T(8,128)(2,1)}, bf16[4,96,768]{2,1,0:T(8,128)(2,1)}, u32[]{:S(2)}, u32[]{:S(2)}) collective-permute-start(bf16[4,96,768]{2,1,0:T(8,128)(2,1)} %pad_maximum_fusion.14), channel_id=1, source_target_pairs={{0,4},{4,0},{8,12},{12,8},{16,20},{20,16},{24,28},{28,24},{1,5},{5... | collective-permute-start | bytes 1769480 | tf_op jit(solution)/shard_map/ppermute | solution.py:139
  72.9 49.1 %collective-permute-start.33 = (bf16[4,96,768]{2,1,0:T(8,128)(2,1)}, bf16[4,96,768]{2,1,0:T(8,128)(2,1)}, u32[]{:S(2)}, u32[]{:S(2)}) collective-permute-start(bf16[4,96,768]{2,1,0:T(8,128)(2,1)} %pad_maximum_fusion.14), channel_id=1, source_target_pairs={{0,16},{4,20},{8,24},{12,28},{16,0},{20,4},{24,8},{28,12},{1,17},{... | collective-permute-start | bytes 1769480 | tf_op jit(solution)/shard_map/ppermute | solution.py:139
  76.3 50.7 %collective-permute-start.19 = (bf16[4,120,768]{2,1,0:T(8,128)(2,1)}, bf16[4,120,768]{2,1,0:T(8,128)(2,1)S(1)}, u32[]{:S(2)}, u32[]{:S(2)}) collective-permute-start(bf16[4,120,768]{2,1,0:T(8,128)(2,1)} %pad_maximum_fusion.11), channel_id=1, source_target_pairs={{0,8},{4,12},{8,0},{12,4},{16,24},{20,28},{24,16},{28,20},{1,9},{5... | collective-permute-start | bytes 2211848 | tf_op jit(solution)/shard_map/ppermute | solution.py:139
  81.2 42.3 %collective-permute-start.18 = (bf16[4,120,768]{2,1,0:T(8,128)(2,1)}, bf16[4,120,768]{2,1,0:T(8,128)(2,1)}, u32[]{:S(2)}, u32[]{:S(2)}) collective-permute-start(bf16[4,120,768]{2,1,0:T(8,128)(2,1)} %pad_maximum_fusion.11), channel_id=1, source_target_pairs={{0,4},{4,0},{8,12},{12,8},{16,20},{20,16},{24,28},{28,24},{1,5},{5... | collective-permute-start | bytes 2211848 | tf_op jit(solution)/shard_map/ppermute | solution.py:139
  100.4 57.8 %all-to-all-start = ((bf16[4,256,192]{1,2,0:T(8,128)(2,1)}), bf16[4,256,192]{1,2,0:T(8,128)(2,1)S(1)}, u32[]{:S(2)}, u32[]{:S(2)}) async-start(bf16[4,256,192]{1,2,0:T(8,128)(2,1)} %copy.326), calls=%async_computation | async-start | bytes 786432 | tf_op jit(solution)/shard_map/all_to_all | solution.py:325
  115.3 19.6 %collective-permute-start.21 = (bf16[4,120,768]{2,1,0:T(8,128)(2,1)}, bf16[4,120,768]{2,1,0:T(8,128)(2,1)S(1)}, u32[]{:S(2)}, u32[]{:S(2)}) collective-permute-start(bf16[4,120,768]{2,1,0:T(8,128)(2,1)} %pad_maximum_fusion.11), channel_id=1, source_target_pairs={{0,16},{4,20},{8,24},{12,28},{16,0},{20,4},{24,8},{28,12},{1,17},{... | collective-permute-start | bytes 2211848 | tf_op jit(solution)/shard_map/ppermute | solution.py:139
  116.9 19.6 %collective-permute-start.32 = (bf16[4,96,768]{2,1,0:T(8,128)(2,1)}, bf16[4,96,768]{2,1,0:T(8,128)(2,1)S(1)}, u32[]{:S(2)}, u32[]{:S(2)}) collective-permute-start(bf16[4,96,768]{2,1,0:T(8,128)(2,1)} %collective-permute-done.31), channel_id=1, source_target_pairs={{0,4},{4,0},{8,12},{12,8},{16,20},{20,16},{24,28},{28,24},{1,5},{5... | collective-permute-start | bytes 1769480 | tf_op jit(solution)/shard_map/ppermute | solution.py:139
  122.0 19.2 %collective-permute-start.35 = (bf16[2,96,768]{2,1,0:T(8,128)(2,1)S(1)}, bf16[2,96,768]{2,1,0:T(8,128)(2,1)S(1)}, u32[]{:S(2)}, u32[]{:S(2)}) collective-permute-start(bf16[2,96,768]{2,1,0:T(8,128)(2,1)S(1)} %slice.474), channel_id=1, source_target_pairs={{0,16},{4,20},{8,24},{12,28},{16,0},{20,4},{24,8},{28,12},{1,17},{... | collective-permute-start | bytes 884744 | tf_op jit(solution)/shard_map/ppermute | solution.py:139
  123.6 17.7 %collective-permute-start.36 = (bf16[2,96,768]{2,1,0:T(8,128)(2,1)S(1)}, bf16[2,96,768]{2,1,0:T(8,128)(2,1)S(1)}, u32[]{:S(2)}, u32[]{:S(2)}) collective-permute-start(bf16[2,96,768]{2,1,0:T(8,128)(2,1)S(1)} %slice.475), channel_id=1, source_target_pairs={{0,8},{4,12},{8,0},{12,4},{16,24},{20,28},{24,16},{28,20},{1,9},{5... | collective-permute-start | bytes 884744 | tf_op jit(solution)/shard_map/ppermute | solution.py:139
  127.0 14.7 %collective-permute-start.34 = (bf16[4,96,768]{2,1,0:T(8,128)(2,1)}, bf16[4,96,768]{2,1,0:T(8,128)(2,1)S(1)}, u32[]{:S(2)}, u32[]{:S(2)}) collective-permute-start(bf16[4,96,768]{2,1,0:T(8,128)(2,1)} %collective-permute-done.33), channel_id=1, source_target_pairs={{0,4},{4,0},{8,12},{12,8},{16,20},{20,16},{24,28},{28,24},{1,5},{5... | collective-permute-start | bytes 1769480 | tf_op jit(solution)/shard_map/ppermute | solution.py:139
  134.9 13.6 %collective-permute-start.23 = (bf16[2,120,768]{2,1,0:T(8,128)(2,1)S(1)}, bf16[2,120,768]{2,1,0:T(8,128)(2,1)S(1)}, u32[]{:S(2)}, u32[]{:S(2)}) collective-permute-start(bf16[2,120,768]{2,1,0:T(8,128)(2,1)S(1)} %slice.463), channel_id=1, source_target_pairs={{0,16},{4,20},{8,24},{12,28},{16,0},{20,4},{24,8},{28,12},{1,17},{... | collective-permute-start | bytes 1105928 | tf_op jit(solution)/shard_map/ppermute | solution.py:139
  136.5 12.2 %collective-permute-start.24 = (bf16[2,120,768]{2,1,0:T(8,128)(2,1)S(1)}, bf16[2,120,768]{2,1,0:T(8,128)(2,1)S(1)}, u32[]{:S(2)}, u32[]{:S(2)}) collective-permute-start(bf16[2,120,768]{2,1,0:T(8,128)(2,1)S(1)} %slice.464), channel_id=1, source_target_pairs={{0,8},{4,12},{8,0},{12,4},{16,24},{20,28},{24,16},{28,20},{1,9},{5... | collective-permute-start | bytes 1105928 | tf_op jit(solution)/shard_map/ppermute | solution.py:139
  141.2 11.2 %collective-permute-start.20 = (bf16[4,120,768]{2,1,0:T(8,128)(2,1)S(1)}, bf16[4,120,768]{2,1,0:T(8,128)(2,1)S(1)}, u32[]{:S(2)}, u32[]{:S(2)}) collective-permute-start(bf16[4,120,768]{2,1,0:T(8,128)(2,1)S(1)} %collective-permute-done.19), channel_id=1, source_target_pairs={{0,4},{4,0},{8,12},{12,8},{16,20},{20,16},{24,28},{28,24},{1,5},{5... | collective-permute-start | bytes 2211848 | tf_op jit(solution)/shard_map/ppermute | solution.py:139
  141.2 2.6 collective-permute-start.37
  143.9 10.1 %collective-permute-start.22 = (bf16[4,120,768]{2,1,0:T(8,128)(2,1)S(1)}, bf16[4,120,768]{2,1,0:T(8,128)(2,1)S(1)}, u32[]{:S(2)}, u32[]{:S(2)}) collective-permute-start(bf16[4,120,768]{2,1,0:T(8,128)(2,1)S(1)} %collective-permute-done.21), channel_id=1, source_target_pairs={{0,4},{4,0},{8,12},{12,8},{16,20},{20,16},{24,28},{28,24},{1,5},{5... | collective-permute-start | bytes 2211848 | tf_op jit(solution)/shard_map/ppermute | solution.py:139
  148.6 5.5 %collective-permute-start.25 = (bf16[2,120,768]{2,1,0:T(8,128)(2,1)S(1)}, bf16[2,120,768]{2,1,0:T(8,128)(2,1)S(1)}, u32[]{:S(2)}, u32[]{:S(2)}) collective-permute-start(bf16[2,120,768]{2,1,0:T(8,128)(2,1)S(1)} %collective-permute-done.23), channel_id=1, source_target_pairs={{0,4},{4,0},{8,12},{12,8},{16,20},{20,16},{24,28},{28,24},{1,5},{5... | collective-permute-start | bytes 1105928 | tf_op jit(solution)/shard_map/ppermute | solution.py:139
  148.7 5.4 %collective-permute-start.26 = (bf16[2,120,768]{2,1,0:T(8,128)(2,1)S(1)}, bf16[2,120,768]{2,1,0:T(8,128)(2,1)S(1)}, u32[]{:S(2)}, u32[]{:S(2)}) collective-permute-start(bf16[2,120,768]{2,1,0:T(8,128)(2,1)S(1)} %collective-permute-done.24), channel_id=1, source_target_pairs={{0,4},{4,0},{8,12},{12,8},{16,20},{20,16},{24,28},{28,24},{1,5},{5... | collective-permute-start | bytes 1105928 | tf_op jit(solution)/shard_map/ppermute | solution.py:139
  192.6 19.2 %all-to-all-start.1 = ((bf16[256,4,192]{0,2,1:T(8,128)(2,1)}), bf16[256,4,192]{0,2,1:T(8,128)(2,1)S(1)}, u32[]{:S(2)}, u32[]{:S(2)}) async-start(bf16[256,4,192]{0,2,1:T(8,128)(2,1)} %bitcast.75), calls=%async_computation.1 | async-start | bytes 786432 | tf_op jit(solution)/shard_map/all_to_all | solution.py:367
  206.7 64.2 %collective-permute-start.58 = (bf16[4,4,96,768]{3,2,1,0:T(8,128)(2,1)}, bf16[4,4,96,768]{3,2,1,0:T(8,128)(2,1)}, u32[]{:S(2)}, u32[]{:S(2)}) collective-permute-start(bf16[4,4,96,768]{3,2,1,0:T(8,128)(2,1)} %pad_maximum_fusion.4), channel_id=1, source_target_pairs={{0,4},{4,0},{8,12},{12,8},{16,20},{20,16},{24,28},{28,24},{1,5},{5... | collective-permute-start | bytes 7077896 | tf_op jit(solution)/shard_map/ppermute | solution.py:139
  240.6 6.3 %collective-permute-start.42 = (bf16[4,4,24,588]{3,2,1,0:T(8,128)(2,1)S(1)}, bf16[4,4,24,588]{3,2,1,0:T(8,128)(2,1)S(1)}, u32[]{:S(2)}, u32[]{:S(2)}) collective-permute-start(bf16[4,4,24,588]{3,2,1,0:T(8,128)(2,1)S(1)} %pad_maximum_fusion.17), channel_id=1, source_target_pairs={{0,4},{4,0},{8,12},{12,8},{16,20},{20,16},{24,28},{28,24},{1,5},{5... | collective-permute-start | bytes 1354760 | tf_op jit(solution)/shard_map/ppermute | solution.py:139
  244.8 16.7 %collective-permute-start.40 = (bf16[256,768]{1,0:T(8,128)(2,1)S(1)}, bf16[256,768]{1,0:T(8,128)(2,1)S(1)}, u32[]{:S(2)}, u32[]{:S(2)}) collective-permute-start(bf16[256,768]{1,0:T(8,128)(2,1)S(1)} %get-tuple-element.364), channel_id=1, source_target_pairs={{0,1},{1,0},{2,3},{3,2},{4,5},{5,4},{6,7},{7,6},{8,9},{9,8},{10,11... | collective-permute-start | bytes 1179656 | tf_op jit(solution)/shard_map/ppermute | solution.py:139
  247.0 4.3 %collective-permute-start.45 = (bf16[2,24,588]{2,1,0:T(8,128)(2,1)S(1)}, bf16[2,24,588]{2,1,0:T(8,128)(2,1)S(1)}, u32[]{:S(2)}, u32[]{:S(2)}) collective-permute-start(bf16[2,24,588]{2,1,0:T(8,128)(2,1)S(1)} %get-tuple-element.416), channel_id=1, source_target_pairs={{0,8},{4,12},{8,0},{12,4},{16,24},{20,28},{24,16},{28,20},{1,9},{5... | collective-permute-start | bytes 169352 | tf_op jit(solution)/shard_map/ppermute | solution.py:139
  248.5 4.5 %collective-permute-start.43 = (bf16[2,24,588]{2,1,0:T(8,128)(2,1)S(1)}, bf16[2,24,588]{2,1,0:T(8,128)(2,1)S(1)}, u32[]{:S(2)}, u32[]{:S(2)}) collective-permute-start(bf16[2,24,588]{2,1,0:T(8,128)(2,1)S(1)} %get-tuple-element.415), channel_id=1, source_target_pairs={{0,16},{4,20},{8,24},{12,28},{16,0},{20,4},{24,8},{28,12},{1,17},{... | collective-permute-start | bytes 169352 | tf_op jit(solution)/shard_map/ppermute | solution.py:139
  251.4 4.9 %collective-permute-start.46 = (bf16[4,24,588]{2,1,0:T(8,128)(2,1)S(1)}, bf16[4,24,588]{2,1,0:T(8,128)(2,1)S(1)}, u32[]{:S(2)}, u32[]{:S(2)}) collective-permute-start(bf16[4,24,588]{2,1,0:T(8,128)(2,1)S(1)} %pad_maximum_fusion.23), channel_id=1, source_target_pairs={{0,16},{4,20},{8,24},{12,28},{16,0},{20,4},{24,8},{28,12},{1,17},{... | collective-permute-start | bytes 338696 | tf_op jit(solution)/shard_map/ppermute | solution.py:139
  253.0 4.9 %collective-permute-start.44 = (bf16[4,24,588]{2,1,0:T(8,128)(2,1)S(1)}, bf16[4,24,588]{2,1,0:T(8,128)(2,1)S(1)}, u32[]{:S(2)}, u32[]{:S(2)}) collective-permute-start(bf16[4,24,588]{2,1,0:T(8,128)(2,1)S(1)} %pad_maximum_fusion.22), channel_id=1, source_target_pairs={{0,8},{4,12},{8,0},{12,4},{16,24},{20,28},{24,16},{28,20},{1,9},{5... | collective-permute-start | bytes 338696 | tf_op jit(solution)/shard_map/ppermute | solution.py:139
  256.3 28.4 %collective-permute-start.50 = (bf16[4,4,120,768]{3,2,1,0:T(8,128)(2,1)}, bf16[4,4,120,768]{3,2,1,0:T(8,128)(2,1)}, u32[]{:S(2)}, u32[]{:S(2)}) collective-permute-start(bf16[4,4,120,768]{3,2,1,0:T(8,128)(2,1)} %pad_maximum_fusion.3), channel_id=1, source_target_pairs={{0,4},{4,0},{8,12},{12,8},{16,20},{20,16},{24,28},{28,24},{1,5},{5... | collective-permute-start | bytes 8847368 | tf_op jit(solution)/shard_map/ppermute | solution.py:139
  259.0 5.9 %collective-permute-start.49 = (bf16[24,588]{1,0:T(8,128)(2,1)S(1)}, bf16[24,588]{1,0:T(8,128)(2,1)S(1)}, u32[]{:S(2)}, u32[]{:S(2)}) collective-permute-start(bf16[24,588]{1,0:T(8,128)(2,1)S(1)} %get-tuple-element.412), channel_id=1, source_target_pairs={{0,3},{1,2},{2,1},{3,0},{4,7},{5,6},{6,5},{7,4},{8,11},{9,10},{10,... | collective-permute-start | bytes 84680 | tf_op jit(solution)/shard_map/ppermute | solution.py:139
  261.4 5.1 %collective-permute-start.48 = (bf16[24,588]{1,0:T(8,128)(2,1)S(1)}, bf16[24,588]{1,0:T(8,128)(2,1)S(1)}, u32[]{:S(2)}, u32[]{:S(2)}) collective-permute-start(bf16[24,588]{1,0:T(8,128)(2,1)S(1)} %get-tuple-element.413), channel_id=1, source_target_pairs={{0,2},{1,3},{2,0},{3,1},{4,6},{5,7},{6,4},{7,5},{8,10},{9,11},{10,... | collective-permute-start | bytes 84680 | tf_op jit(solution)/shard_map/ppermute | solution.py:139
  261.5 6.3 %collective-permute-start.47 = (bf16[24,588]{1,0:T(8,128)(2,1)S(1)}, bf16[24,588]{1,0:T(8,128)(2,1)S(1)}, u32[]{:S(2)}, u32[]{:S(2)}) collective-permute-start(bf16[24,588]{1,0:T(8,128)(2,1)S(1)} %get-tuple-element.414), channel_id=1, source_target_pairs={{0,1},{1,0},{2,3},{3,2},{4,5},{5,4},{6,7},{7,6},{8,9},{9,8},{10,11... | collective-permute-start | bytes 84680 | tf_op jit(solution)/shard_map/ppermute | solution.py:139
  264.9 48.8 %collective-permute-start.39 = (bf16[256,768]{1,0:T(8,128)(2,1)}, bf16[256,768]{1,0:T(8,128)(2,1)S(1)}, u32[]{:S(2)}, u32[]{:S(2)}) collective-permute-start(bf16[256,768]{1,0:T(8,128)(2,1)} %get-tuple-element.363), channel_id=1, source_target_pairs={{0,1},{1,0},{2,3},{3,2},{4,5},{5,4},{6,7},{7,6},{8,9},{9,8},{10,11... | collective-permute-start | bytes 1179656 | tf_op jit(solution)/shard_map/ppermute | solution.py:139
  266.5 48.6 %collective-permute-start.41 = (bf16[256,768]{1,0:T(8,128)(2,1)}, bf16[256,768]{1,0:T(8,128)(2,1)S(1)}, u32[]{:S(2)}, u32[]{:S(2)}) collective-permute-start(bf16[256,768]{1,0:T(8,128)(2,1)} %bitcast_add_fusion), channel_id=1, source_target_pairs={{0,3},{1,2},{2,1},{3,0},{4,7},{5,6},{6,5},{7,4},{8,11},{9,10},{10,... | collective-permute-start | bytes 1179656 | tf_op jit(solution)/shard_map/ppermute | solution.py:139
  273.3 6.9 %collective-permute-start.61 = (bf16[2,96,768]{2,1,0:T(8,128)(2,1)S(1)}, bf16[2,96,768]{2,1,0:T(8,128)(2,1)S(1)}, u32[]{:S(2)}, u32[]{:S(2)}) collective-permute-start(bf16[2,96,768]{2,1,0:T(8,128)(2,1)S(1)} %get-tuple-element.388), channel_id=1, source_target_pairs={{0,8},{4,12},{8,0},{12,4},{16,24},{20,28},{24,16},{28,20},{1,9},{5... | collective-permute-start | bytes 884744 | tf_op jit(solution)/shard_map/ppermute | solution.py:139
  275.0 9.4 %collective-permute-start.59 = (bf16[2,96,768]{2,1,0:T(8,128)(2,1)S(1)}, bf16[2,96,768]{2,1,0:T(8,128)(2,1)S(1)}, u32[]{:S(2)}, u32[]{:S(2)}) collective-permute-start(bf16[2,96,768]{2,1,0:T(8,128)(2,1)S(1)} %get-tuple-element.387), channel_id=1, source_target_pairs={{0,16},{4,20},{8,24},{12,28},{16,0},{20,4},{24,8},{28,12},{1,17},{... | collective-permute-start | bytes 884744 | tf_op jit(solution)/shard_map/ppermute | solution.py:139
  280.3 36.7 %collective-permute-start.62 = (bf16[4,96,768]{2,1,0:T(8,128)(2,1)S(1)}, bf16[4,96,768]{2,1,0:T(8,128)(2,1)S(1)}, u32[]{:S(2)}, u32[]{:S(2)}) collective-permute-start(bf16[4,96,768]{2,1,0:T(8,128)(2,1)S(1)} %pad_maximum_fusion.16), channel_id=1, source_target_pairs={{0,16},{4,20},{8,24},{12,28},{16,0},{20,4},{24,8},{28,12},{1,17},{... | collective-permute-start | bytes 1769480 | tf_op jit(solution)/shard_map/ppermute | solution.py:139
  284.6 32.4 %collective-permute-start.60 = (bf16[4,96,768]{2,1,0:T(8,128)(2,1)S(1)}, bf16[4,96,768]{2,1,0:T(8,128)(2,1)S(1)}, u32[]{:S(2)}, u32[]{:S(2)}) collective-permute-start(bf16[4,96,768]{2,1,0:T(8,128)(2,1)S(1)} %pad_maximum_fusion.15), channel_id=1, source_target_pairs={{0,8},{4,12},{8,0},{12,4},{16,24},{20,28},{24,16},{28,20},{1,9},{5... | collective-permute-start | bytes 1769480 | tf_op jit(solution)/shard_map/ppermute | solution.py:139
  286.5 14.1 %collective-permute-start.53 = (bf16[2,120,768]{2,1,0:T(8,128)(2,1)S(1)}, bf16[2,120,768]{2,1,0:T(8,128)(2,1)S(1)}, u32[]{:S(2)}, u32[]{:S(2)}) collective-permute-start(bf16[2,120,768]{2,1,0:T(8,128)(2,1)S(1)} %get-tuple-element.384), channel_id=1, source_target_pairs={{0,8},{4,12},{8,0},{12,4},{16,24},{20,28},{24,16},{28,20},{1,9},{5... | collective-permute-start | bytes 1105928 | tf_op jit(solution)/shard_map/ppermute | solution.py:139
  300.6 11.5 %collective-permute-start.51 = (bf16[2,120,768]{2,1,0:T(8,128)(2,1)S(1)}, bf16[2,120,768]{2,1,0:T(8,128)(2,1)S(1)}, u32[]{:S(2)}, u32[]{:S(2)}) collective-permute-start(bf16[2,120,768]{2,1,0:T(8,128)(2,1)S(1)} %get-tuple-element.383), channel_id=1, source_target_pairs={{0,16},{4,20},{8,24},{12,28},{16,0},{20,4},{24,8},{28,12},{1,17},{... | collective-permute-start | bytes 1105928 | tf_op jit(solution)/shard_map/ppermute | solution.py:139
  312.1 11.5 %collective-permute-start.54 = (bf16[4,120,768]{2,1,0:T(8,128)(2,1)S(1)}, bf16[4,120,768]{2,1,0:T(8,128)(2,1)S(1)}, u32[]{:S(2)}, u32[]{:S(2)}) collective-permute-start(bf16[4,120,768]{2,1,0:T(8,128)(2,1)S(1)} %pad_maximum_fusion.13), channel_id=1, source_target_pairs={{0,16},{4,20},{8,24},{12,28},{16,0},{20,4},{24,8},{28,12},{1,17},{... | collective-permute-start | bytes 2211848 | tf_op jit(solution)/shard_map/ppermute | solution.py:139
  313.8 11.5 %collective-permute-start.52 = (bf16[4,120,768]{2,1,0:T(8,128)(2,1)S(1)}, bf16[4,120,768]{2,1,0:T(8,128)(2,1)S(1)}, u32[]{:S(2)}, u32[]{:S(2)}) collective-permute-start(bf16[4,120,768]{2,1,0:T(8,128)(2,1)S(1)} %pad_maximum_fusion.12), channel_id=1, source_target_pairs={{0,8},{4,12},{8,0},{12,4},{16,24},{20,28},{24,16},{28,20},{1,9},{5... | collective-permute-start | bytes 2211848 | tf_op jit(solution)/shard_map/ppermute | solution.py:139
  318.4 16.5 %collective-permute-start.63 = (bf16[96,768]{1,0:T(8,128)(2,1)S(1)}, bf16[96,768]{1,0:T(8,128)(2,1)S(1)}, u32[]{:S(2)}, u32[]{:S(2)}) collective-permute-start(bf16[96,768]{1,0:T(8,128)(2,1)S(1)} %get-tuple-element.385), channel_id=1, source_target_pairs={{0,1},{1,0},{2,3},{3,2},{4,5},{5,4},{6,7},{7,6},{8,9},{9,8},{10,11... | collective-permute-start | bytes 442376 | tf_op jit(solution)/shard_map/ppermute | solution.py:139
  318.9 9.2 %collective-permute-start.64 = (bf16[96,768]{1,0:T(8,128)(2,1)S(1)}, bf16[96,768]{1,0:T(8,128)(2,1)S(1)}, u32[]{:S(2)}, u32[]{:S(2)}) collective-permute-start(bf16[96,768]{1,0:T(8,128)(2,1)S(1)} %get-tuple-element.386), channel_id=1, source_target_pairs={{0,1},{1,0},{2,3},{3,2},{4,5},{5,4},{6,7},{7,6},{8,9},{9,8},{10,11... | collective-permute-start | bytes 442376 | tf_op jit(solution)/shard_map/ppermute | solution.py:139
  326.6 5.8 %collective-permute-start.56 = (bf16[120,768]{1,0:T(8,128)(2,1)S(1)}, bf16[120,768]{1,0:T(8,128)(2,1)S(1)}, u32[]{:S(2)}, u32[]{:S(2)}) collective-permute-start(bf16[120,768]{1,0:T(8,128)(2,1)S(1)} %get-tuple-element.382), channel_id=1, source_target_pairs={{0,1},{1,0},{2,3},{3,2},{4,5},{5,4},{6,7},{7,6},{8,9},{9,8},{10,11... | collective-permute-start | bytes 552968 | tf_op jit(solution)/shard_map/ppermute | solution.py:139
  328.1 7.1 %collective-permute-start.65 = (bf16[96,768]{1,0:T(8,128)(2,1)S(1)}, bf16[96,768]{1,0:T(8,128)(2,1)S(1)}, u32[]{:S(2)}, u32[]{:S(2)}) collective-permute-start(bf16[96,768]{1,0:T(8,128)(2,1)S(1)} %bitcast_add_fusion.2), channel_id=1, source_target_pairs={{0,3},{1,2},{2,1},{3,0},{4,7},{5,6},{6,5},{7,4},{8,11},{9,10},{10,... | collective-permute-start | bytes 442376 | tf_op jit(solution)/shard_map/ppermute | solution.py:139
  330.7 6.4 %collective-permute-start.55 = (bf16[120,768]{1,0:T(8,128)(2,1)S(1)}, bf16[120,768]{1,0:T(8,128)(2,1)S(1)}, u32[]{:S(2)}, u32[]{:S(2)}) collective-permute-start(bf16[120,768]{1,0:T(8,128)(2,1)S(1)} %get-tuple-element.381), channel_id=1, source_target_pairs={{0,1},{1,0},{2,3},{3,2},{4,5},{5,4},{6,7},{7,6},{8,9},{9,8},{10,11... | collective-permute-start | bytes 552968 | tf_op jit(solution)/shard_map/ppermute | solution.py:139
  332.4 7.4 %collective-permute-start.57 = (bf16[120,768]{1,0:T(8,128)(2,1)S(1)}, bf16[120,768]{1,0:T(8,128)(2,1)S(1)}, u32[]{:S(2)}, u32[]{:S(2)}) collective-permute-start(bf16[120,768]{1,0:T(8,128)(2,1)S(1)} %bitcast_add_fusion.1), channel_id=1, source_target_pairs={{0,3},{1,2},{2,1},{3,0},{4,7},{5,6},{6,5},{7,4},{8,11},{9,10},{10,... | collective-permute-start | bytes 552968 | tf_op jit(solution)/shard_map/ppermute | solution.py:139
  (57 other events, 427.3 us)

commit v2 on v1

--- a/solution.py
+++ b/solution.py
@@ -1,8 +1,11 @@
 import functools
+import math
 
 import jax
 import jax.numpy as jnp
 from jax import lax
+from jax.experimental import pallas as pl
+from jax.experimental.pallas import tpu as pltpu
 from jax.sharding import PartitionSpec as P
 
 HD = 64
@@ -155,62 +158,701 @@
     from_y = hop(blocks, "fsdp", 4, 8)
     far_low = hop(from_x[:2], "fsdp", 4, 8)
     far_high = hop(from_y[2:], "fsdp", 2, 8)
-    parts = [[blocks], [from_x], [from_y], [far_low, far_high]]
-    whole = []
-    for part in parts:
-        whole.append(part)
-        whole.append([hop(piece, "fsdp", 1, 8) for piece in part])
-    return [jnp.concatenate(part, axis=0) if len(part) > 1 else part[0] for part in whole]
-
-
-def in_order(blocks, me):
-    return jnp.stack([pick(blocks, j ^ me) for j in range(blocks.shape[0])])
-
-
-def sum_plane(grad, me):
-    theirs = jnp.stack([pick(grad, me ^ (2 * k + 1)) for k in range(4)])
-    mine = [pick(grad, me ^ (2 * k)) for k in range(4)]
+    out = []
+    for part in ([blocks], [from_x], [from_y], [far_low, far_high]):
+        out += part + [hop(piece, "fsdp", 1, 8) for piece in part]
+    return out
+
+
+def after(values):
+    return lax.optimization_barrier(values)
+
+
+def sum_far(got, mine):
+    half = mine.shape[1] // 2
+    far_y = hop(mine[3, :half] + got[3, :half], "fsdp", 4, 8)
+    far_x = hop(mine[3, half:] + got[3, half:], "fsdp", 2, 8)
+    return far_y, far_x
+
+
+def sum_near(got, mine, far_y, far_x):
+    half = mine.shape[1] // 2
+    to_x = jnp.concatenate([mine[1, :half] + got[1, :half] + far_y, mine[1, half:] + got[1, half:]], axis=0)
+    to_y = jnp.concatenate([mine[2, :half] + got[2, :half], mine[2, half:] + got[2, half:] + far_x], axis=0)
+    return hop(to_x, "fsdp", 2, 8), hop(to_y, "fsdp", 4, 8)
+
+
+def sum_plane(theirs, mine):
     got = hop(theirs, "fsdp", 1, 8)
-    total = [mine[k] + got[k] for k in range(4)]
-    half = total[3].shape[0] // 2
-    far_y = hop(total[3][:half], "fsdp", 4, 8)
-    far_x = hop(total[3][half:], "fsdp", 2, 8)
-    to_x = jnp.concatenate([total[1][:half] + far_y, total[1][half:]], axis=0)
-    to_y = jnp.concatenate([total[2][:half], total[2][half:] + far_x], axis=0)
-    near_x = hop(to_x, "fsdp", 2, 8)
-    near_y = hop(to_y, "fsdp", 4, 8)
-    return total[0] + near_x + near_y
-
-
-def sum_seq(blocks, z):
-    far = hop(pick(blocks, z ^ 2), "seq", 1, 4)
-    near = hop(pick(blocks, z ^ 1), "seq", 1, 4)
-    last = hop(pick(blocks, z ^ 3) + far, "seq", 3, 4)
+    near_x, near_y = sum_near(got, mine, *sum_far(got, mine))
+    return mine[0] + got[0] + near_x + near_y
+
+
+def sum_seq(two, one, three, own):
+    far = hop(two, "seq", 1, 4)
+    near = hop(one, "seq", 1, 4)
+    last = hop(three + far, "seq", 3, 4)
+    return own.astype(jnp.float32) + near.astype(jnp.float32) + last.astype(jnp.float32)
+
+
+def sum_place(total, z):
+    return sum_seq(pick(total, z ^ 2), pick(total, z ^ 1), pick(total, z ^ 3), pick(total, z))
+
+
+def xpose(value):
+    return jnp.transpose(value)
+
+
+def place(pieces, into, sems, me_ref, rows):
+    copies = []
+    for kf, group in enumerate(pieces):
+        for kz in range(4):
+            ref, at = group[kz * len(group) // 4], kz % (4 // len(group))
+            to = ((me_ref[0] ^ kf) * 4 + (me_ref[1] ^ kz)) * rows
+            to = pl.multiple_of(to, 8)
+            target = into.at[:, pl.ds(to, rows)] if len(into.shape) == 3 else into.at[pl.ds(to, rows)]
+            copies.append(pltpu.make_async_copy(ref.at[at], target, sems.at[kf * 4 + kz]))
+    return copies
+
+
+def regroup(refs):
+    out, at = [], 0
+    for kf in range(8):
+        n = 2 if kf >= 6 else 1
+        out.append(refs[at : at + n])
+        at += n
+    return out
+
+
+def dot(left, right, dims=((1,), (0,))):
+    return lax.dot_general(left, right, (dims, ((), ())), preferred_element_type=jnp.float32)
+
+
+NT = ((1,), (1,))
+TN = ((0,), (0,))
+
+
+def prepare_kernel(me_ref, *refs):
+    pieces = regroup(refs[:10])
+    wt_out, small_out, ib_out, bias_out, w, stack, sems = refs[10:]
+    low, z = jnp.bfloat16, me_ref[1]
+    copies = place(pieces, w, sems, me_ref, 24)
+    for copy in copies:
+        copy.start()
+    for copy in copies:
+        copy.wait()
+    wt = xpose(w[...])
+    wt_out[...] = wt
+    small_out[...] = wt[576:592].astype(jnp.float32)
+    for g in range(8):
+        stack[8 * g : 8 * g + 8] = small_out[8:16, 96 * g : 96 * g + 96]
+    heap = stack[...].astype(low)
+    line = lax.broadcasted_iota(jnp.int32, (64, 384), 0) & 7
+    spread = jnp.zeros((64, 384), jnp.float32)
+    for c in range(4):
+        spread = spread + jnp.where(line == c, dot(heap, shares(c)), 0.0)
+    for g in range(8):
+        ib_out[:, 384 * g : 384 * g + 384] = total_rows(spread[8 * g : 8 * g + 8])
+    bias = w[pl.ds(pl.multiple_of(z * 192, 64), 192), 512:640].astype(jnp.float32)
+    bias_out[0] = jnp.broadcast_to(bias[:, 64:65], (192, 128))
+    bias_out[1] = jnp.broadcast_to(bias[:, 65:66], (192, 128))
+
+
+def turn_kernel(me_ref, *refs):
+    xs, xt_out, xt = refs[:4], refs[4], refs[5]
+    for k in range(4):
+        xt[:, 256 * k : 256 * k + 256] = xpose(xs[k][...])
+    for kf in range(8):
+        xt_out[96 * kf : 96 * kf + 96] = xt[pl.ds(pl.multiple_of((me_ref[0] ^ kf) * 96, 32), 96)]
+
+
+def attend_kernel(*refs):
+    xs, refs = refs[:4], refs[4:]
+    wt, bias, seg_row, seg_col, refs = refs[0], refs[1], refs[2], refs[3], refs[4:]
+    q_out, k_out, v_out, *m_out = refs[:7]
+    lse_out, keys, mixed = refs[7:]
+    low = jnp.bfloat16
+    for k in range(4):
+        at = slice(256 * k, 256 * k + 256)
+        qkv = dot(wt[:576], xs[k][...], NT)
+        query = (qkv[:192] + bias[0, :, 0:1]).astype(low)
+        query = (query.astype(jnp.float32) * HD**-0.5).astype(low)
+        key = qkv[192:384].astype(low)
+        value = (qkv[384:] + bias[1, :, 0:1]).astype(low)
+        for h in range(3):
+            rows = slice(64 * h, 64 * h + 64)
+            q_out[h, :, at] = query[rows]
+            k_out[h, :, at] = key[rows]
+            v_out[h, :, at] = value[rows]
+            keys[h, at] = xpose(key[rows])
+
+    def step(i, carry):
+        h, b = lax.shift_right_logical(i, 2), i & 3
+        at = pl.ds(pl.multiple_of(b * 256, 256), 256)
+        scores = dot(keys[h], q_out[h, :, at])
+        column = seg_col[...]
+        allowed = jnp.concatenate([column, column], axis=1) == seg_row[:, at]
+        scores = jnp.where(allowed, scores, NEGATIVE)
+        peak = jnp.max(scores, axis=0, keepdims=True)
+        weights = jnp.exp(scores - peak)
+        total = jnp.sum(weights, axis=0, keepdims=True)
+        probs = (weights * (1.0 / total)).astype(low)
+        mixed[b, h] = dot(v_out[h], probs).astype(low)
+        lse_out[h, :, at] = peak + jnp.log(total)
+        return carry
+
+    lax.fori_loop(0, 12, step, 0)
+    for k in range(4):
+        for h in range(3):
+            m_out[k][64 * h : 64 * h + 64] = mixed[k, h]
+
+
+VM = pl.BlockSpec(memory_space=pltpu.VMEM)
+ANY = pl.BlockSpec(memory_space=pl.ANY)
+SM = pl.BlockSpec(memory_space=pltpu.SMEM)
+
+
+def shape(*dims, dtype=jnp.bfloat16):
+    return jax.ShapeDtypeStruct(dims, dtype)
+
+
+def cost(flops, moved, powers=0):
+    return pl.CostEstimate(flops=1, bytes_accessed=1, transcendentals=0)
+
+
+def prepare_call(me, pieces):
+    f32 = jnp.float32
+    outs = [
+        shape(640, 768),
+        shape(16, 768, dtype=f32),
+        shape(1, 3072, dtype=f32),
+        shape(2, 192, 128, dtype=f32),
+    ]
+    return pl.pallas_call(
+        prepare_kernel,
+        out_shape=outs,
+        in_specs=[SM] + [ANY] * 10,
+        out_specs=[VM] * len(outs),
+        scratch_shapes=[
+            pltpu.VMEM((768, 640), jnp.bfloat16),
+            pltpu.VMEM((64, 96), f32),
+            pltpu.SemaphoreType.DMA((32,)),
+        ],
+        cost_estimate=cost(100_000_000, 4_000_000),
+        name="prepare",
+    )(me, *pieces)
+
+
+def turn_call(me, xs):
+    return pl.pallas_call(
+        turn_kernel,
+        out_shape=shape(768, 1024),
+        in_specs=[SM] + [VM] * 4,
+        out_specs=VM,
+        scratch_shapes=[pltpu.VMEM((768, 1024), jnp.bfloat16)],
+        cost_estimate=cost(100_000_000, 3_200_000),
+        name="turn",
+    )(me, *xs)
+
+
+def attend_call(xs, wt, bias, seg_row, seg_col):
+    outs = [shape(3, 64, 1024)] * 3 + [shape(192, 256)] * 4 + [shape(3, 1, 1024, dtype=jnp.float32)]
+    return pl.pallas_call(
+        attend_kernel,
+        out_shape=outs,
+        in_specs=[VM] * 8,
+        out_specs=[VM] * len(outs),
+        scratch_shapes=[
+            pltpu.VMEM((3, 1024, 64), jnp.bfloat16),
+            pltpu.VMEM((4, 3, 64, 256), jnp.bfloat16),
+        ],
+        cost_estimate=cost(6_000_000_000, 10_000_000, 3_145_728),
+        name="attend",
+    )(*xs, wt, bias, seg_row, seg_col)
+
+
+def pack_kernel(me_ref, vectors, segments, query, key, value, mixer, inner, outer, *refs):
+    messages, both, outs, seg_row, seg_col, rows = refs[:4], refs[4], refs[5], refs[6], refs[7], refs[8]
+    low, z = jnp.bfloat16, me_ref[1]
+    rows[...] = jnp.zeros_like(rows)
+    rows[0:12, 0:24] = vectors[...]
+    small = xpose(rows[...])[:24, :64]
+    parts = []
+    for j in range(4):
+        at = slice(192 * j, 192 * j + 192)
+        parts.append(jnp.concatenate([query[:, at], key[:, at], value[:, at], small], axis=1))
+    for k in range(4):
+        part = parts[3]
+        for j in range(3):
+            part = jnp.where((z ^ k) == j, parts[j], part)
+        messages[k][...] = part.astype(low)
+    both[0] = mixer[...].astype(low)
+    for c in range(4):
+        both[1 + c] = inner[:, 768 * c : 768 * c + 768].astype(low)
+    outs[...] = outer[...].astype(low)
+    for k in range(4):
+        at = slice(256 * k, 256 * k + 256)
+        row = segments[:, pl.ds(pl.multiple_of((z ^ k) * 256, 256), 256)].astype(jnp.float32)
+        seg_row[:, at] = row
+        seg_col[at] = xpose(jnp.broadcast_to(row, (128, 256)))
+
+
+def pack_call(me, vectors, segments, *weights):
+    f32 = jnp.float32
+    outs = [shape(24, 640)] * 4 + [
+        shape(5, 24, 768),
+        shape(96, 768),
+        shape(1, 1024, dtype=f32),
+        shape(1024, 128, dtype=f32),
+    ]
+    return pl.pallas_call(
+        pack_kernel,
+        out_shape=outs,
+        in_specs=[SM] + [VM] * 8,
+        out_specs=[VM] * len(outs),
+        scratch_shapes=[pltpu.VMEM((128, 128), f32)],
+        cost_estimate=cost(1, 1),
+        name="pack",
+    )(me, vectors, segments, *weights)
+
+
+def shares(c):
+    row = lax.broadcasted_iota(jnp.int32, (96, 384), 0)
+    column = lax.broadcasted_iota(jnp.int32, (96, 384), 1)
+    where = row + 72 * ((row >= 24).astype(jnp.int32) + (row >= 48) + (row >= 72)) + 24 * c
+    return (column == where).astype(jnp.float32).astype(jnp.bfloat16)
+
+
+def centre(hidden):
+    centred = hidden - jnp.mean(hidden, axis=-1, keepdims=True)
+    scale = lax.rsqrt(jnp.mean(centred * centred, axis=-1, keepdims=True) + EPSILON)
+    return centred * scale, scale
+
+
+def centre_back(grad_normed, normed, scale):
+    return scale * (
+        grad_normed
+        - jnp.mean(grad_normed, axis=-1, keepdims=True)
+        - normed * jnp.mean(grad_normed * normed, axis=-1, keepdims=True)
+    )
+
+
+def total_rows(value):
+    return jnp.sum(value, axis=0, keepdims=True)
+
+
+def feed_kernel(me_ref, *refs):
+    ms, refs = refs[:4], refs[4:]
+    tokens, cotangent, small, ibias, refs = refs[0], refs[1], refs[2], refs[3], refs[4:]
+    pieces, outers, refs = regroup(refs[:10]), regroup(refs[10:20]), refs[20:]
+    result, slope_out, first_out, normed_out, scale_out, second_out, gouter_out, sums, theirs, mine = refs[:10]
+    wmi, wo, active, sems, osems = refs[10:]
+    low, f32, f, z = jnp.bfloat16, jnp.float32, me_ref[0], me_ref[1]
+    copies = place(pieces, wmi, sems, me_ref, 24)
+    ocopies = place(outers, wo, osems, me_ref, 96)
+    for copy in copies + ocopies:
+        copy.start()
+    for copy in copies:
+        copy.wait()
+    attended = small[2:3]
+    for k in range(4):
+        rows = wmi[0, pl.ds(pl.multiple_of((z ^ k) * 192, 64), 192)]
+        attended = attended + dot(ms[k][...], rows, TN)
+    normed, scale = centre(tokens[...].astype(f32) + attended)
+    normed_out[...] = normed
+    scale_out[...] = jnp.broadcast_to(scale, (256, 128))
+    first = normed * small[3:4] + small[4:5]
+    first_low = first.astype(low)
+    first_out[...] = first_low
+    for copy in ocopies:
+        copy.wait()
+    outer = small[5:6]
+    for c in range(4):
+        at = slice(768 * c, 768 * c + 768)
+        inner = dot(first_low, wmi[1 + c]) + ibias[:, at]
+        half = 0.5 + 0.5 * lax.erf(inner * (0.5**0.5))
+        slope_out[:, at] = half + inner * jnp.exp(-0.5 * inner * inner) * ((2.0 * math.pi) ** -0.5)
+        act = (inner * half).astype(low)
+        active[:, at] = act
+        outer = outer + dot(act, wo[at])
+    normed, scale = centre(first + outer)
+    result[...] = (normed * small[6:7] + small[7:8]).astype(low)
+    grad = cotangent[...].astype(f32)
+    second = centre_back(grad * small[6:7], normed, scale)
+    second_out[...] = second
+    gouter = second.astype(low)
+    gouter_out[...] = gouter
+    sums[0:1] = total_rows(gouter.astype(f32))
+    sums[1:2] = total_rows(grad * normed)
+    sums[2:3] = total_rows(grad)
+    sums[3:8] = jnp.zeros((5, 768), f32)
+
+    def step(kp, carry):
+        for kc, out in ((1, theirs), (0, mine)):
+            at = pl.ds(pl.multiple_of((f ^ (2 * kp + kc)) * 384, 128), 384)
+            out[kp] = dot(active[:, at], gouter_out[...], TN).astype(low)
+        return carry
+
+    lax.fori_loop(0, 4, step, 0)
+
+
+def feed_call(me, ms, tokens, cotangent, small, ibias, pieces, outers):
+    f32 = jnp.float32
+    outs = [
+        shape(256, 768),
+        shape(256, 3072, dtype=f32),
+        shape(256, 768),
+        shape(256, 768, dtype=f32),
+        shape(256, 128, dtype=f32),
+        shape(256, 768, dtype=f32),
+        shape(256, 768),
+        shape(8, 768, dtype=f32),
+        shape(4, 384, 768),
+        shape(4, 384, 768),
+    ]
+    return pl.pallas_call(
+        feed_kernel,
+        out_shape=outs,
+        in_specs=[SM] + [VM] * 8 + [ANY] * 20,
+        out_specs=[VM] * len(outs),
+        scratch_shapes=[
+            pltpu.VMEM((5, 768, 768), jnp.bfloat16),
+            pltpu.VMEM((3072, 768), jnp.bfloat16),
+            pltpu.VMEM((256, 3072), jnp.bfloat16),
+            pltpu.SemaphoreType.DMA((32,)),
+            pltpu.SemaphoreType.DMA((32,)),
+        ],
+        cost_estimate=cost(1, 1),
+        name="feed",
+    )(me, *ms, tokens, cotangent, small, ibias, *pieces, *outers)
+
+
+def feed_back_kernel(me_ref, *refs):
+    small, slope, normed_ref, scale_ref, second, gouter, refs = *refs[:6], refs[6:]
+    pieces, outers, refs = regroup(refs[:10]), regroup(refs[10:20]), refs[20:]
+    residual, sums, isums, gin, d0, d1, d2, d3 = refs[:8]
+    wmi, wo, sems, osems = refs[8:]
+    low, f32, z = jnp.bfloat16, jnp.float32, me_ref[1]
+    copies = place(pieces, wmi, sems, me_ref, 24)
+    ocopies = place(outers, wo, osems, me_ref, 96)
+    for copy in ocopies + copies:
+        copy.start()
+    for copy in ocopies:
+        copy.wait()
+    for c in range(4):
+        at = slice(768 * c, 768 * c + 768)
+        inner = (dot(gouter[...], wo[at], NT) * slope[:, at]).astype(low)
+        gin[:, at] = inner
+        isums[:, at] = total_rows(inner.astype(f32))
+    for copy in copies:
+        copy.wait()
+    first = second[...]
+    for c in range(4):
+        at = slice(768 * c, 768 * c + 768)
+        first = first + dot(gin[:, at], wmi[1 + c], NT)
+    normed = normed_ref[...]
+    grad = centre_back(first * small[3:4], normed, scale_ref[:, 0:1])
+    residual[...] = grad
+    sums[0:1] = total_rows(grad.astype(low).astype(f32))
+    sums[1:2] = total_rows(first * normed)
+    sums[2:3] = total_rows(first)
+    sums[3:8] = jnp.zeros((5, 768), f32)
+    attended = grad.astype(low)
+    for k, out in enumerate((d0, d1, d2, d3)):
+        rows = wmi[0, pl.ds(pl.multiple_of((z ^ k) * 192, 64), 192)]
+        out[...] = dot(rows, attended, NT).astype(low)
+
+
+def feed_back_call(me, small, slope, normed, scale, second, gouter, pieces, outers):
+    f32 = jnp.float32
+    outs = [
+        shape(256, 768, dtype=f32),
+        shape(8, 768, dtype=f32),
+        shape(1, 3072, dtype=f32),
+        shape(256, 3072),
+    ] + [shape(192, 256)] * 4
+    return pl.pallas_call(
+        feed_back_kernel,
+        out_shape=outs,
+        in_specs=[SM] + [VM] * 6 + [ANY] * 20,
+        out_specs=[VM] * len(outs),
+        scratch_shapes=[
+            pltpu.VMEM((5, 768, 768), jnp.bfloat16),
+            pltpu.VMEM((3072, 768), jnp.bfloat16),
+            pltpu.SemaphoreType.DMA((32,)),
+            pltpu.SemaphoreType.DMA((32,)),
+        ],
+        cost_estimate=cost(8_000_000_000, 25_000_000),
+        name="feed_back",
+    )(me, small, slope, normed, scale, second, gouter, *pieces, *outers)
+
+
+def feed_grad_kernel(me_ref, *refs):
+    ms, first_low, gin, residual, theirs, mine, left, canon = refs[:4], *refs[4:]
+    low, f, z = jnp.bfloat16, me_ref[0], me_ref[1]
+
+    def order():
+        for kf in range(8):
+            left[96 * kf : 96 * kf + 96] = canon[pl.ds(pl.multiple_of((f ^ kf) * 96, 32), 96)]
+
+    def spread(value, entry):
+        value = value.astype(low)
+        for kf in range(8):
+            out = theirs if kf % 2 else mine
+            for zz in range(4):
+                out[kf // 2, zz, entry] = value[96 * kf + 24 * zz : 96 * kf + 24 * zz + 24]
+
+    canon[...] = xpose(first_low[...])
+    order()
+    for c in range(4):
+        spread(dot(left[...], gin[:, 768 * c : 768 * c + 768]), 1 + c)
+    for k in range(4):
+        canon[pl.ds(pl.multiple_of((z ^ k) * 192, 64), 192)] = ms[k][...]
+    order()
+    spread(dot(left[...], residual[...].astype(low)), 0)
+
+
+def feed_grad_call(me, ms, first_low, gin, residual):
+    return pl.pallas_call(
+        feed_grad_kernel,
+        out_shape=[shape(4, 4, 5, 24, 768)] * 2,
+        in_specs=[SM] + [VM] * 7,
+        out_specs=[VM] * 2,
+        scratch_shapes=[pltpu.VMEM((768, 256), jnp.bfloat16)] * 2,
+        cost_estimate=cost(4_000_000_000, 10_000_000),
+        name="feed_grad",
+    )(me, *ms, first_low, gin, residual)
+
+
+def attend_back_kernel(*refs):
+    ds, refs = refs[:4], refs[4:]
+    q_ref, k_ref, v_ref, lse, seg_row, seg_col, all_rows = refs[:7]
+    keys, values, gout, gk, gv = refs[7:]
+    low = jnp.bfloat16
+    for h in range(3):
+        keys[h] = xpose(k_ref[h])
+        values[h] = xpose(v_ref[h])
+        for k in range(4):
+            gout[h, :, 256 * k : 256 * k + 256] = ds[k][64 * h : 64 * h + 64]
+    gk[...] = jnp.zeros_like(gk)
+    gv[...] = jnp.zeros_like(gv)
+
+    def step(i, carry):
+        h, b = lax.shift_right_logical(i, 2), i & 3
+        at = pl.ds(pl.multiple_of(b * 256, 256), 256)
+        query, grad = q_ref[h, :, at], gout[h, :, at]
+        scores = dot(keys[h], query)
+        column = seg_col[...]
+        allowed = jnp.concatenate([column, column], axis=1) == seg_row[:, at]
+        probs = jnp.where(allowed, jnp.exp(jnp.where(allowed, scores, NEGATIVE) - lse[h, :, at]), 0.0)
+        gprobs = dot(values[h], grad)
+        delta = jnp.sum(probs * gprobs, axis=0, keepdims=True)
+        gscores = (probs * (gprobs - delta)).astype(low)
+        all_rows[h, :, at] = (dot(k_ref[h], gscores) * HD**-0.5).astype(low)
+        gk[h] += dot(query, gscores, NT)
+        gv[h] += dot(grad, probs.astype(low), NT)
+        return carry
+
+    lax.fori_loop(0, 12, step, 0)
+    all_rows[3:6] = gk[...].astype(low)
+    all_rows[6:9] = gv[...].astype(low)
+    all_rows[9] = jnp.zeros((64, 1024), low)
+
+
+def attend_back_call(ds, queries, keys, values, lse, seg_row, seg_col):
+    f32 = jnp.float32
+    return pl.pallas_call(
+        attend_back_kernel,
+        out_shape=shape(10, 64, 1024),
+        in_specs=[VM] * 10,
+        out_specs=VM,
+        scratch_shapes=[
+            pltpu.VMEM((3, 1024, 64), jnp.bfloat16),
+            pltpu.VMEM((3, 1024, 64), jnp.bfloat16),
+            pltpu.VMEM((3, 64, 1024), jnp.bfloat16),
+            pltpu.VMEM((3, 64, 1024), f32),
+            pltpu.VMEM((3, 64, 1024), f32),
+        ],
+        cost_estimate=cost(12_000_000_000, 6_000_000, 3_145_728),
+        name="attend_back",
+    )(*ds, queries, keys, values, lse, seg_row, seg_col)
+
+
+def project_back_kernel(me_ref, rows_ref, wt, xt, sums_one, sums_two, isums, *refs):
+    own, b1, b2, b3, theirs, mine = refs[:6]
+    canon, rel, rows, heap = refs[6:]
+    low, f32, f, z = jnp.bfloat16, jnp.float32, me_ref[0], me_ref[1]
+    all_rows = jnp.reshape(rows_ref[...], (640, 1024))
+    for k, out in enumerate((own, b1, b2, b3)):
+        part = xpose(all_rows[:, 256 * k : 256 * k + 256])
+        out[...] = dot(part, wt[...]).astype(out.dtype)
+    qsum = jnp.sum(all_rows[:192].astype(f32), axis=1, keepdims=True)
+    vsum = jnp.sum(all_rows[384:576].astype(f32), axis=1, keepdims=True)
+    rows[...] = jnp.zeros_like(rows)
+    rows[66:69] = sums_one[0:3]
+    rows[69:72] = sums_two[0:3]
+    canon[...] = xpose(rows[...])
+    for g in range(8):
+        heap[g : g + 1] = isums[:, 384 * g : 384 * g + 384]
+    lane = lax.broadcasted_iota(jnp.int32, (96, 128), 1)
+    for c in range(4):
+        part = dot(shares(c), heap[...].astype(low), NT)
+        for g in range(8):
+            canon[96 * g : 96 * g + 96] += jnp.where(lane == 72 + c, part[:, g : g + 1], 0.0)
+    lane = lax.broadcasted_iota(jnp.int32, (192, 128), 1)
+    at = pl.ds(pl.multiple_of(z * 192, 64), 192)
+    canon[at] += jnp.where(lane == 64, qsum, 0.0) + jnp.where(lane == 65, vsum, 0.0)
+    for kf in range(8):
+        rel[96 * kf : 96 * kf + 96] = canon[pl.ds(pl.multiple_of((f ^ kf) * 96, 32), 96)]
+    grads = dot(xt[...], all_rows, NT)
+    heads, tail = grads[:, :512].astype(low), (grads[:, 512:] + rel[...]).astype(low)
+    for kf in range(8):
+        out = theirs if kf % 2 else mine
+        for zz in range(4):
+            rows = slice(96 * kf + 24 * zz, 96 * kf + 24 * zz + 24)
+            out[kf // 2, zz, :, :512] = heads[rows]
+            out[kf // 2, zz, :, 512:] = tail[rows]
+
+
+def project_back_call(me, rows, wt, xt, sums_one, sums_two, isums):
+    f32 = jnp.float32
+    outs = [shape(256, 768, dtype=f32)] + [shape(256, 768)] * 3 + [shape(4, 4, 24, 640)] * 2
+    return pl.pallas_call(
+        project_back_kernel,
+        out_shape=outs,
+        in_specs=[SM] + [VM] * 6,
+        out_specs=[VM] * len(outs),
+        scratch_shapes=[
+            pltpu.VMEM((768, 128), f32),
+            pltpu.VMEM((768, 128), f32),
+            pltpu.VMEM((128, 768), f32),
+            pltpu.VMEM((8, 384), f32),
+        ],
+        cost_estimate=cost(5_000_000_000, 10_000_000),
+        name="project_back",
+    )(me, rows, wt, xt, sums_one, sums_two, isums)
+
+
+def on_block(
+    tokens,
+    segments,
+    cotangent,
+    query_weight,
+    query_bias,
+    key_weight,
+    value_weight,
+    value_bias,
+    mixer_weight,
+    mixer_bias,
+    first_gain,
+    first_shift,
+    inner_weight,
+    inner_bias,
+    outer_weight,
+    outer_bias,
+    second_gain,
+    second_shift,
+):
+    f, z = lax.axis_index("fsdp"), lax.axis_index("seq")
+    me = jnp.stack([f, z]).astype(jnp.int32)
+    low, f32 = jnp.bfloat16, jnp.float32
+    vectors = jnp.stack(
+        [
+            query_bias,
+            value_bias,
+            mixer_bias,
+            first_gain,
+            first_shift,
+            outer_bias,
+            second_gain,
+            second_shift,
+        ]
+        + list(inner_bias.reshape(4, 24))
+    )
+    *messages, both, outers, seg_row, seg_col = pack_call(
+        me, vectors, segments, query_weight, key_weight, value_weight, mixer_weight, inner_weight, outer_weight
+    )
+    got = [messages[0]] + [hop(messages[k], "seq", k, 4) for k in (1, 2, 3)]
+    pieces = spread_plane(jnp.stack(got))
+    outers = spread_seq(outers)
+    both = spread_seq(both)
+    tokens_late, *outers = after((tokens, *outers))
+    xs = spread_seq(tokens_late)
+    both, _ = after((jnp.stack(both), xs[1]))
+    outers = spread_plane(jnp.stack(outers))
+    both = spread_plane(both)
+
+    wt, rows, ibias, bias = prepare_call(me, pieces)
+    queries, keys, values, *ms, lse = attend_call(xs, wt, bias, seg_row, seg_col)
+    *xs_late, ms[0] = after((*xs, ms[0]))
+    xt = turn_call(me, xs_late)
+    ms = [ms[0]] + [hop(ms[k], "seq", k, 4) for k in (1, 2, 3)]
+    *ms, xt = after((*ms, xt))
+    result, slope, first_low, normed, scale, second, gouter, sums_two, theirs, mine = feed_call(
+        me, ms, tokens, cotangent, rows, ibias, both, outers
+    )
+    outer_mine = mine.reshape(4, 4, 96, 768)
+    outer_got = hop(theirs.reshape(4, 4, 96, 768), "fsdp", 1, 8)
+    residual, sums_one, isums, gin, *ds = feed_back_call(
+        me, rows, slope, normed, scale, second, gouter, both, outers
+    )
+    ds = [ds[0]] + [hop(ds[k], "seq", k, 4) for k in (1, 2, 3)]
+    gin, outer_got = after((gin, outer_got))
+    outer_far = sum_far(outer_got, outer_mine)
+    theirs, both_mine = feed_grad_call(me, ms, first_low, gin, residual)
+    both_got = hop(theirs, "fsdp", 1, 8)
+    *ds, far_y, far_x = after((*ds, *outer_far))
+    outer_near = sum_near(outer_got, outer_mine, far_y, far_x)
+    rows_back = attend_back_call(ds, queries, keys, values, lse, seg_row, seg_col)
+    rows_back, both_got, *outer_near = after((rows_back, both_got, *outer_near))
+    outer_total = outer_mine[0] + outer_got[0] + outer_near[0] + outer_near[1]
+    both_far = sum_far(both_got, both_mine)
+    own, one, two, three, theirs, mine = project_back_call(
+        me, rows_back, wt, xt, sums_one, sums_two, isums
+    )
+    outer_sum = sum_place(outer_total, z)
+    both_near = sum_near(both_got, both_mine, *both_far)
+    both_total = both_mine[0] + both_got[0] + both_near[0] + both_near[1]
+    both_sum = sum_place(both_total, z)
+    grad_tokens = residual + sum_seq(two, one, three, own)
+    total = sum_plane(theirs, mine)
+    parts = [pick(total, z)] + [hop(pick(total, z ^ k), "seq", k, 4) for k in (1, 2, 3)]
+    parts = jnp.stack(parts)
+    parts = jnp.stack([pick(parts, j ^ z) for j in range(4)]).astype(f32)
+    weights = [
+        jnp.concatenate([parts[j, :, k * 192 : (k + 1) * 192] for j in range(4)], axis=1)
+        for k in range(3)
+    ]
+    sums = jnp.sum(parts[:, :, 576:588], axis=0).T
     return (
-        pick(blocks, z).astype(jnp.float32)
-        + near.astype(jnp.float32)
-        + last.astype(jnp.float32)
-    )
-
-
-def gather_rows(own, fast, f, z):
-    if not fast:
-        return lax.all_gather(own, ("fsdp", "seq"), axis=0, tiled=True)
-    rows, width = own.shape
-    pieces = jnp.stack(spread_plane(jnp.stack(spread_seq(own))))
-    pieces = in_order(pieces, f)
-    pieces = jnp.stack([pick(pieces.swapaxes(0, 1), j ^ z) for j in range(4)], axis=1)
-    return pieces.reshape(32 * rows, width)
-
-
-def reduce_rows(grad, fast, f, z):
-    if not fast:
-        return lax.psum_scatter(
-            grad.astype(jnp.float32), ("fsdp", "seq"), scatter_dimension=0, tiled=True
-        )
-    rows = grad.shape[0] // 32
-    mine = sum_plane(grad.reshape(8, 4, rows, grad.shape[1]), f)
-    return sum_seq(mine, z)
+        result,
+        grad_tokens.astype(low),
+        weights[0],
+        sums[0],
+        weights[1],
+        weights[2],
+        sums[1],
+        both_sum[0],
+        sums[2],
+        sums[3],
+        sums[4],
+        both_sum[1:].swapaxes(0, 1).reshape(24, 3072),
+        sums[8:].reshape(-1),
+        outer_sum,
+        sums[5],
+        sums[6],
+        sums[7],
+    )
+
+
+def gather_rows(own):
+    return lax.all_gather(own, ("fsdp", "seq"), axis=0, tiled=True)
+
+
+def reduce_all(grad):
+    return lax.psum_scatter(
+        grad.astype(jnp.float32), ("fsdp", "seq"), scatter_dimension=0, tiled=True
+    )
 
 
 def on_device(
@@ -235,8 +877,7 @@
     second_shift,
 ):
     nf, nz = sizes
-    fast = (nf, nz) == (8, 4)
-    f, z = lax.axis_index("fsdp"), lax.axis_index("seq")
+    z = lax.axis_index("seq")
     low = jnp.bfloat16
     share, width = query_weight.shape
     wide = inner_weight.shape[1]
@@ -263,11 +904,7 @@
         piece.astype(low).reshape(share, nz, cut) for piece in (query_weight, key_weight, value_weight)
     ]
 
-    if fast:
-        pieces = jnp.stack(spread_seq(tokens))
-        rows_all = in_order(pieces, z).reshape(-1, width)
-    else:
-        rows_all = lax.all_gather(tokens, "seq", axis=0, tiled=True)
+    rows_all = lax.all_gather(tokens, "seq", axis=0, tiled=True)
 
     def message(target):
         return jnp.concatenate(
@@ -275,25 +912,18 @@
             axis=1,
         )
 
-    if fast:
-        got = [message(z)] + [hop(message(z ^ k), "seq", k, 4) for k in (1, 2, 3)]
-        got = jnp.stack(spread_plane(jnp.stack(got)))
-        got = in_order(got, f)
-        got = jnp.stack([pick(got.swapaxes(0, 1), j ^ z) for j in range(4)], axis=1)
-        heads_full = got.reshape(width, -1)
-    else:
-        packed = jnp.concatenate(
-            [piece.astype(low) for piece in (query_weight, key_weight, value_weight)] + [small], axis=1
-        )
-        packed = lax.all_gather(packed, ("fsdp", "seq"), axis=0, tiled=True)
-        heads_full = jnp.concatenate(
-            [
-                lax.dynamic_slice_in_dim(packed, k * width + z * cut, cut, axis=1)
-                for k in range(3)
-            ]
-            + [packed[:, 3 * width :]],
-            axis=1,
-        )
+    packed = jnp.concatenate(
+        [piece.astype(low) for piece in (query_weight, key_weight, value_weight)] + [small], axis=1
+    )
+    packed = lax.all_gather(packed, ("fsdp", "seq"), axis=0, tiled=True)
+    heads_full = jnp.concatenate(
+        [
+            lax.dynamic_slice_in_dim(packed, k * width + z * cut, cut, axis=1)
+            for k in range(3)
+        ]
+        + [packed[:, 3 * width :]],
+        axis=1,
+    )
     small_full = heads_full[:, 3 * cut :].astype(jnp.float32).T
     (qbias, vbias, mbias, gain_one, shift_one, obias, gain_two, shift_two) = [
         small_full[k] for k in range(8)
@@ -309,12 +939,12 @@
         + [inner_weight[:, k * width : (k + 1) * width].astype(low) for k in range(ratio)],
         axis=0,
     )
-    packed = gather_rows(packed, fast, f, z).reshape(nf * nz, 1 + ratio, share, width)
+    packed = gather_rows(packed).reshape(nf * nz, 1 + ratio, share, width)
     mixer_full = packed[:, 0].reshape(width, width)
     inner_full = jnp.concatenate(
         [packed[:, 1 + k].reshape(width, width) for k in range(ratio)], axis=1
     )
-    outer_full = gather_rows(outer_weight.astype(low), fast, f, z)
+    outer_full = gather_rows(outer_weight.astype(low))
 
     projected = product(rows_all, heads_full[:, : 3 * cut])
     query_heads = (projected[:, :cut] + qbias).astype(low)
@@ -339,7 +969,7 @@
     grad_outer = grad_second.astype(low)
     grad_outer_weight = product_tn(active_low, grad_outer).astype(low)
     grad_outer_bias = column_sum(grad_outer)
-    outer_sum = reduce_rows(grad_outer_weight, fast, f, z)
+    outer_sum = reduce_all(grad_outer_weight)
     grad_inner = gelu_back(product_nt(grad_outer, outer_full))[0].astype(low)
     grad_inner_weight = product_tn(first_low, grad_inner).astype(low)
     grad_inner_bias = column_sum(grad_inner)
@@ -358,7 +988,7 @@
         ],
         axis=1,
     ).reshape(-1, width)
-    packed_sum = reduce_rows(packed, fast, f, z)
+    packed_sum = reduce_all(packed)
     mixer_sum = packed_sum[:share]
     inner_sum = jnp.concatenate(
         [packed_sum[(1 + k) * share : (2 + k) * share] for k in range(ratio)], axis=1
@@ -386,15 +1016,10 @@
         axis=1,
     ).astype(low)
     heads_grad = jnp.concatenate([heads_grad, small_grad], axis=1)
-    if fast:
-        mine = sum_plane(heads_grad.reshape(8, 4, share, -1), f)
-        parts = [pick(mine, z)] + [hop(pick(mine, z ^ k), "seq", k, 4) for k in (1, 2, 3)]
-        parts = in_order(jnp.stack(parts), z)
-    else:
-        mine = lax.psum_scatter(heads_grad, "fsdp", scatter_dimension=0, tiled=True)
-        parts = lax.all_to_all(
-            mine.reshape(nz, share, -1), "seq", split_axis=0, concat_axis=0, tiled=True
-        )
+    mine = lax.psum_scatter(heads_grad, "fsdp", scatter_dimension=0, tiled=True)
+    parts = lax.all_to_all(
+        mine.reshape(nz, share, -1), "seq", split_axis=0, concat_axis=0, tiled=True
+    )
     parts = parts.astype(jnp.float32)
     projections = [
         jnp.concatenate([parts[j, :, k * cut : (k + 1) * cut] for j in range(nz)], axis=1)
@@ -402,10 +1027,7 @@
     ]
     small_sum = jnp.sum(parts[:, :, 3 * cut :], axis=0).T
     back_rows = product_nt(grads, heads_full[:, : 3 * cut]).astype(low).reshape(nz, -1, width)
-    if fast:
-        back = sum_seq(back_rows, z)
-    else:
-        back = lax.psum_scatter(back_rows, "seq", scatter_dimension=0, tiled=True)[0]
+    back = lax.psum_scatter(back_rows, "seq", scatter_dimension=0, tiled=True)[0]
     grad_tokens = grad_residual + back
     return (
         result.astype(low),
@@ -451,7 +1073,7 @@
     )
     sizes = (mesh.shape["fsdp"], mesh.shape["seq"])
     return jax.shard_map(
-        functools.partial(on_device, sizes),
+        on_block if sizes == (8, 4) else functools.partial(on_device, sizes),
         mesh=mesh,
         in_specs=placed,
         out_specs=(

time: 346 us -> 282 us (0.82); the launches traced: 341 us -> 281 us
  Pallas kernels: 0 us -> 81.8 us
  matrix products: 54.5 us -> 0 us
  other arithmetic: 54.5 us -> 19.5 us
  local copies, waits for them, and re-layouts: 50.3 us -> 15.3 us
  starting transfers between devices: 96.4 us -> 82.4 us
    pallas_call x0 -> x9, Pallas kernels: none -> 81.8 us  [the longest x1 16.6 us: feed_call(): pl.pallas_call(feed_kernel, out_shape=outs, in_specs=[SM] + [VM] * 8 + [A...]
    dot_general x26 -> x0, matrix products: 54.5 us -> none  [the longest x4 12.6 us: product(): return jnp.dot(left, right, preferred_element_type=jnp.float32)]
    all_to_all x2 -> x0, starting transfers between devices: 19.8 us -> none  [the longest x1 14.9 us: on_device(): lax.all_to_all(mixed_heads, 'seq', split_axis=0, concat_axis=1, tiled=True)]
    another operation x25 -> x5, other arithmetic: 17.1 us -> 3.38 us  [the longest x1 1.02 us: on_block(): both, _ = after((jnp.stack(both), xs[1]))]
    unnamed x157 -> x87, local copies, waits for them, and re-layouts: 17.4 us -> 4.36 us
    convert_element_type x11 -> x2, other arithmetic: 10.9 us -> 1.92 us  [the longest x1 1.89 us: on_block(): grad_tokens.astype(low)]
    reduce_sum x10 -> x1, other arithmetic: 8.3 us -> 0.08 us  [on_block(): sums = jnp.sum(parts[:, :, 576:588], axis=0).T]
    ppermute x66 -> x72, starting transfers between devices: 76.6 us -> 82.4 us  [hop(): return lax.ppermute(value, axis, [(i, i ^ bit) for i in range(size)])]
  transfers between devices with their start and end apart: 68 -> 72, of which waited for: 27 -> 27; matrix products, arithmetic and copies ran while one was open for 34% -> 8% of each run, Pallas kernels for 0% -> 20%
where the time goes in v2:
time: 282 us; the launch traced here: 281 us
  starting transfers between devices  82.4 us (29%)
  Pallas kernels  81.8 us (29%)
  waiting for transfers between devices  80.8 us (29%)
  other arithmetic  19.5 us (7%)
  local copies, waits for them, and re-layouts  15.3 us (5%)
    ppermute x72, starting transfers between devices, hop(): return lax.ppermute(value, axis, [(i, i ^ bit) for i in range(size)])  82.4 us
    ppermute x72, waiting for transfers between devices, hop(): return lax.ppermute(value, axis, [(i, i ^ bit) for i in range(size)])  80.8 us
    pallas_call x1, Pallas kernels, feed_call(): pl.pallas_call(feed_kernel, out_shape=outs, in_specs=[SM] + [VM] * 8 + [A...  16.6 us
    pallas_call x1, Pallas kernels, attend_back_call(): pl.pallas_call(attend_back_kernel, out_shape=shape(10, 64, 1024), in_spec...  16.2 us
    pallas_call x1, Pallas kernels, attend_call(): pl.pallas_call(attend_kernel, out_shape=outs, in_specs=[VM] * 8, out_spec...  14.4 us
    pallas_call x1, Pallas kernels, feed_back_call(): pl.pallas_call(feed_back_kernel, out_shape=outs, in_specs=[SM] + [VM] * 6...  12.2 us
    pallas_call x1, Pallas kernels, feed_grad_call(): pl.pallas_call(feed_grad_kernel, out_shape=[shape(4, 4, 5, 24, 768)] * 2,...  7.11 us
    pallas_call x1, Pallas kernels, project_back_call(): pl.pallas_call(project_back_kernel, out_shape=outs, in_specs=[SM] + [VM]...  6.21 us
  transfers between devices with their start and end apart: 72, of which 27 were waited for; matrix products, arithmetic and copies ran while one was open for 8% of the time, Pallas kernels for 20%

profile of v2, /device:TPU:0, one launch (start us, length us, event | category | flops | bytes accessed | tf_op | source)
XLA Modules:
  0.0 281.2 jit_solution(323683751066758087)
XLA Ops:
  2.1 2.0 stack.112.vectors
  4.1 2.4 pack.1
  6.5 3.1 %collective-permute-start.6 = (bf16[24,640]{1,0:T(8,128)(2,1)}, bf16[24,640]{1,0:T(8,128)(2,1)S(1)}, u32[]{:S(2)}, u32[]{:S(2)}) collective-permute-start(bf16[24,640]{1,0:T(8,128)(2,1)} %get-tuple-element.94), channel_id=1, source_target_pairs={{0,1},{1,0},{2,3},{3,2},{4,5},{5,4},{6,7},{7,6},{8,9},{9,8},{10,11... | collective-permute-start | bytes 92168 | tf_op jit(solution)/shard_map/ppermute | solution.py:142
  9.6 2.6 collective-permute-start.7
  12.2 3.8 %collective-permute-start.1 = (bf16[96,768]{1,0:T(8,128)(2,1)}, bf16[96,768]{1,0:T(8,128)(2,1)S(1)}, u32[]{:S(2)}, u32[]{:S(2)}) collective-permute-start(bf16[96,768]{1,0:T(8,128)(2,1)} %get-tuple-element.118), channel_id=1, source_target_pairs={{0,3},{1,2},{2,1},{3,0},{4,7},{5,6},{6,5},{7,4},{8,11},{9,10},{10,... | collective-permute-start | bytes 442376 | tf_op jit(solution)/shard_map/ppermute | solution.py:142
  16.0 2.5 collective-permute-done.8
  19.2 1.6 collective-permute-start.10
  23.0 2.2 collective-permute-start.22
  27.8 2.3 collective-permute-done.12.refs_4_
  30.0 3.3 %collective-permute-start.4 = (bf16[256,768]{1,0:T(8,128)(2,1)}, bf16[256,768]{1,0:T(8,128)(2,1)S(1)}, u32[]{:S(2)}, u32[]{:S(2)}) collective-permute-start(bf16[256,768]{1,0:T(8,128)(2,1)} %refs_4_.1), channel_id=1, source_target_pairs={{0,3},{1,2},{2,1},{3,0},{4,7},{5,6},{6,5},{7,4},{8,11},{9,10},{10,... | collective-permute-start | bytes 1179656 | tf_op jit(solution)/shard_map/ppermute | solution.py:142
  33.4 2.5 collective-permute-start.14
  35.8 1.5 collective-permute-start.15
  41.8 1.5 collective-permute-start.34
  43.4 13.2 %collective-permute-done.23 = bf16[5,24,768]{2,1,0:T(8,128)(2,1)S(1)} collective-permute-done((bf16[5,24,768]{2,1,0:T(8,128)(2,1)S(1)}, bf16[5,24,768]{2,1,0:T(8,128)(2,1)S(1)}, u32[]{:S(2)}, u32[]{:S(2)}) %collective-permute-start.23) | collective-permute-done | bytes 184352 | tf_op jit(solution)/shard_map/ppermute | solution.py:142
  58.9 1.6 collective-permute-start.25
  60.4 7.7 %collective-permute-done.5.refs_2_ = bf16[256,768]{1,0:T(8,128)(2,1)S(1)} collective-permute-done((bf16[256,768]{1,0:T(8,128)(2,1)S(1)}, bf16[256,768]{1,0:T(8,128)(2,1)S(1)}, u32[]{:S(2)}, u32[]{:S(2)}) %collective-permute-start.5) | collective-permute-done | bytes 393248 | tf_op jit(solution)/shard_map/ppermute | solution.py:142
  68.9 1.6 collective-permute-start.27
  70.5 3.5 %prepare.1 = (bf16[640,768]{1,0:T(8,128)(2,1)}, f32[16,768]{1,0:T(8,128)}, f32[1,3072]{1,0:T(1,128)}, f32[2,192,128]{2,1,0:T(8,128)}) custom-call(s32[2]{0:T(128)} %pad_add_fusion.me_ref, bf16[4,24,640]{2,1,0:T(8,128)(2,1)} %copy-done.22, bf16[4,24,640]{2,1,0:T(8,128)(2,1)} %copy-done.29, bf16[4,24,640]{2,1,0:T(8,128)(2,1)} %copy-done.27, ...), custom_call_target="tpu_custom_call" | custom-call | flops 1 | bytes 1 | tf_op jit(solution)/shard_map/prepare/pallas_call | solution.py:331
  74.0 14.4 %attend.1 = (bf16[3,64,1024]{2,1,0:T(8,128)(2,1)}, bf16[3,64,1024]{2,1,0:T(8,128)(2,1)}, bf16[3,64,1024]{2,1,0:T(8,128)(2,1)}, bf16[192,256]{1,0:T(8,128)(2,1)},...) custom-call(bf16[256,768]{1,0:T(8,128)(2,1)} %refs_4_.1, ...), custom_call_target="tpu_custom_call" | custom-call | flops 1 | bytes 1 | tf_op jit(solution)/shard_map/attend/pallas_call | solution.py:360
  88.4 1.8 collective-permute-start.18
  90.4 2.9 %collective-permute-done.18.refs_1_ = bf16[192,256]{1,0:T(8,128)(2,1)S(1)} collective-permute-done((bf16[192,256]{1,0:T(8,128)(2,1)}, bf16[192,256]{1,0:T(8,128)(2,1)S(1)}, u32[]{:S(2)}, u32[]{:S(2)}) %collective-permute-start.18) | collective-permute-done | bytes 98336 | tf_op jit(solution)/shard_map/ppermute | solution.py:142
  93.3 2.0 collective-permute-start.19
  96.3 2.7 collective-permute-done.19.refs_2_
  100.6 5.1 %collective-permute-done.39.refs_25_.refs_23_ = bf16[2,96,768]{2,1,0:T(8,128)(2,1)S(1)} collective-permute-done((bf16[2,96,768]{2,1,0:T(8,128)(2,1)S(1)}, bf16[2,96,768]{2,1,0:T(8,128)(2,1)S(1)}, u32[]{:S(2)}, u32[]{:S(2)}) %collective-permute-start.39) | collective-permute-done | bytes 294944 | tf_op jit(solution)/shard_map/ppermute | solution.py:142
  106.3 4.0 %collective-permute-start.20 = (bf16[192,256]{1,0:T(8,128)(2,1)}, bf16[192,256]{1,0:T(8,128)(2,1)S(1)}, u32[]{:S(2)}, u32[]{:S(2)}) collective-permute-start(bf16[192,256]{1,0:T(8,128)(2,1)} %get-tuple-element.105), channel_id=1, source_target_pairs={{0,3},{1,2},{2,1},{3,0},{4,7},{5,6},{6,5},{7,4},{8,11},{9,10},{10,... | collective-permute-start | bytes 294920 | tf_op jit(solution)/shard_map/ppermute | solution.py:142
  110.3 3.3 %collective-permute-done.20.refs_3_ = bf16[192,256]{1,0:T(8,128)(2,1)S(1)} collective-permute-done((bf16[192,256]{1,0:T(8,128)(2,1)}, bf16[192,256]{1,0:T(8,128)(2,1)S(1)}, u32[]{:S(2)}, u32[]{:S(2)}) %collective-permute-start.20) | collective-permute-done | bytes 98336 | tf_op jit(solution)/shard_map/ppermute | solution.py:142
  113.6 1.6 collective-permute-start.29
  118.2 5.5 %collective-permute-done.29.refs_14_.refs_12_ = bf16[2,5,24,768]{3,2,1,0:T(8,128)(2,1)} collective-permute-done((bf16[2,5,24,768]{3,2,1,0:T(8,128)(2,1)S(1)}, bf16[2,5,24,768]{3,2,1,0:T(8,128)(2,1)}, u32[]{:S(2)}, u32[]{:S(2)}) %collective-permute-start.29) | collective-permute-done | bytes 368672 | tf_op jit(solution)/shard_map/ppermute | solution.py:142
  124.8 3.2 %turn.1.xt = bf16[768,1024]{1,0:T(8,128)(2,1)} custom-call(s32[2]{0:T(128)} %pad_add_fusion.me_ref, bf16[256,768]{1,0:T(8,128)(2,1)} %refs_4_.1, bf16[256,768]{1,0:T(8,128)(2,1)} %copy-done.14, bf16[256,768]{1,0:T(8,128)(2,1)} %copy-done.15, bf16[256,768]{1,0:T(8,128)(2,1)} %copy-done.13), custom_call_target="tpu_custom_call" | custom-call | flops 1 | bytes 1 | tf_op jit(solution)/shard_map/turn/pallas_call | solution.py:347
  128.9 16.6 %feed.1 = (bf16[256,768]{1,0:T(8,128)(2,1)}, f32[256,3072]{1,0:T(8,128)}, bf16[256,768]{1,0:T(8,128)(2,1)}, f32[256,768]{1,0:T(8,128)}, f32[256,128]{1,0:T(8,128...) custom-call(s32[2]{0:T(128)} %pad_add_fusion.me_ref, ...), custom_call_target="tpu_custom_call" | custom-call | flops 1 | bytes 1 | tf_op jit(solution)/shard_map/feed/pallas_call | solution.py:513
  146.1 12.2 %feed_back.1 = (f32[256,768]{1,0:T(8,128)}, f32[8,768]{1,0:T(8,128)}, f32[1,3072]{1,0:T(1,128)}, bf16[256,3072]{1,0:T(8,128)(2,1)}, bf16[192,256]{1,0:T(8,128)(2...) custom-call(s32[2]{0:T(128)} %pad_add_fusion.me_ref, ...), custom_call_target="tpu_custom_call" | custom-call | flops 1 | bytes 1 | tf_op jit(solution)/shard_map/feed_back/pallas_call | solution.py:574
  158.3 7.1 %feed_grad.1 = (bf16[4,4,5,24,768]{4,3,2,1,0:T(8,128)(2,1)}, bf16[4,4,5,24,768]{4,3,2,1,0:T(8,128)(2,1)}) custom-call(s32[2]{0:T(128)} %pad_add_fusion.me_ref, bf16[192,256]{1,0:T(8,128)(2,1)} %get-tuple-element.110.refs_0_, bf16[192,256]{1,0:T(8,128)(2,1)} %copy-done.23, bf16[192,256]{1,0:T(8,128)(2,1)} %copy-done.24, bf16[192,256]{1,0:T(8,128)(2,1)} %copy-done.25, ...), custom_call_target="tpu_custom_call" | custom-call | flops 1 | bytes 1 | tf_op jit(solution)/shard_map/feed_grad/pallas_call | solution.py:616
  165.6 1.7 fusion.6
  168.1 1.5 collective-permute-start.47
  170.8 2.5 collective-permute-start.43
  173.3 2.1 collective-permute-done.42.refs_1_
  175.4 3.1 %collective-permute-start.44 = (bf16[192,256]{1,0:T(8,128)(2,1)S(1)}, bf16[192,256]{1,0:T(8,128)(2,1)S(1)}, u32[]{:S(2)}, u32[]{:S(2)}) collective-permute-start(bf16[192,256]{1,0:T(8,128)(2,1)S(1)} %copy-done.40), channel_id=1, source_target_pairs={{0,3},{1,2},{2,1},{3,0},{4,7},{5,6},{6,5},{7,4},{8,11},{9,10},{10,... | collective-permute-start | bytes 294920 | tf_op jit(solution)/shard_map/ppermute | solution.py:142
  179.6 2.3 collective-permute-done.44.refs_3_
  186.3 1.9 slice.288
  188.3 16.2 %attend_back.1.rows_ref = bf16[10,64,1024]{2,1,0:T(8,128)(2,1)} custom-call(bf16[192,256]{1,0:T(8,128)(2,1)} %get-tuple-element.137.refs_0_, bf16[192,256]{1,0:T(8,128)(2,1)} %copy-done.32, bf16[192,256]{1,0:T(8,128)(2,1)} %copy-done.33, bf16[192,256]{1,0:T(8,128)(2,1)} %copy-done.34, bf16[3,64,1024]{2,1,0:T(8,128)(2,1)} %get-tuple-element.141.refs_4_, ...), custom_call_target="tpu_custom_call" | custom-call | flops 1 | bytes 1 | tf_op jit(solution)/shard_map/attend_back/pallas_call | solution.py:664
  204.5 1.6 copy-done.7
  206.1 1.7 fusion.2
  208.6 2.0 collective-permute-start.69
  210.6 6.2 %project_back.1 = (f32[256,768]{1,0:T(8,128)}, bf16[256,768]{1,0:T(8,128)(2,1)}, bf16[256,768]{1,0:T(8,128)(2,1)}, bf16[256,768]{1,0:T(8,128)(2,1)}, bf16[4,4,24...) custom-call(s32[2]{0:T(128)} %pad_add_fusion.me_ref, bf16[10,64,1024]{2,1,0:T(8,128)(2,1)} %attend_back.1.rows_ref, ...), custom_call_target="tpu_custom_call" | custom-call | flops 1 | bytes 1 | tf_op jit(solution)/shard_map/project_back/pallas_call | solution.py:720
  217.8 2.1 collective-permute-start.71
  219.9 1.6 add_bitcast_fusion.3
  221.6 1.6 collective-permute-start.62
  227.2 1.7 fusion.12
  229.0 1.7 collective-permute-start.55
  230.6 2.3 collective-permute-done.62
  234.6 2.5 collective-permute-done.57
  237.2 1.6 collective-permute-start.56
  238.8 1.6 collective-permute-start.58
  240.5 1.7 collective-permute-done.56
  242.2 1.6 collective-permute-done.58
  243.9 2.3 collective-permute-start.60
  246.2 2.1 collective-permute-start.61
  249.1 1.6 collective-permute-start.65
  253.8 9.0 %collective-permute-done.63 = bf16[4,5,24,768]{3,2,1,0:T(8,128)(2,1)S(1)} collective-permute-done((bf16[4,5,24,768]{3,2,1,0:T(8,128)(2,1)S(1)}, bf16[4,5,24,768]{3,2,1,0:T(8,128)(2,1)S(1)}, u32[]{:S(2)}, u32[]{:S(2)}) %collective-permute-start.63) | collective-permute-done | bytes 737312 | tf_op jit(solution)/shard_map/ppermute | solution.py:142
  266.7 1.6 pad_maximum_fusion.10
  268.3 2.0 collective-permute-start.66
  270.3 1.9 collective-permute-done.67
  273.8 1.9 add_convert_fusion
  275.6 4.1 %collective-permute-done.68 = bf16[5,24,768]{2,1,0:T(8,128)(2,1)S(1)} collective-permute-done((bf16[5,24,768]{2,1,0:T(8,128)(2,1)S(1)}, bf16[5,24,768]{2,1,0:T(8,128)(2,1)S(1)}, u32[]{:S(2)}, u32[]{:S(2)}) %collective-permute-start.68) | collective-permute-done | bytes 184352 | tf_op jit(solution)/shard_map/ppermute | solution.py:142
  (226 shorter events, 49.4 us)
Async XLA Ops:
  6.5 9.5 %collective-permute-start.6 = (bf16[24,640]{1,0:T(8,128)(2,1)}, bf16[24,640]{1,0:T(8,128)(2,1)S(1)}, u32[]{:S(2)}, u32[]{:S(2)}) collective-permute-start(bf16[24,640]{1,0:T(8,128)(2,1)} %get-tuple-element.94), channel_id=1, source_target_pairs={{0,1},{1,0},{2,3},{3,2},{4,5},{5,4},{6,7},{7,6},{8,9},{9,8},{10,11... | collective-permute-start | bytes 92168 | tf_op jit(solution)/shard_map/ppermute | solution.py:142
  9.6 6.4 %collective-permute-start.7 = (bf16[24,640]{1,0:T(8,128)(2,1)}, bf16[24,640]{1,0:T(8,128)(2,1)S(1)}, u32[]{:S(2)}, u32[]{:S(2)}) collective-permute-start(bf16[24,640]{1,0:T(8,128)(2,1)} %get-tuple-element.95), channel_id=1, source_target_pairs={{0,2},{1,3},{2,0},{3,1},{4,6},{5,7},{6,4},{7,5},{8,10},{9,11},{10,... | collective-permute-start | bytes 92168 | tf_op jit(solution)/shard_map/ppermute | solution.py:142
  12.1 6.3 %collective-permute-start.8 = (bf16[24,640]{1,0:T(8,128)(2,1)}, bf16[24,640]{1,0:T(8,128)(2,1)S(1)}, u32[]{:S(2)}, u32[]{:S(2)}) collective-permute-start(bf16[24,640]{1,0:T(8,128)(2,1)} %get-tuple-element.96), channel_id=1, source_target_pairs={{0,3},{1,2},{2,1},{3,0},{4,7},{5,6},{6,5},{7,4},{8,11},{9,10},{10,... | collective-permute-start | bytes 92168 | tf_op jit(solution)/shard_map/ppermute | solution.py:142
  12.2 9.3 %collective-permute-start.1 = (bf16[96,768]{1,0:T(8,128)(2,1)}, bf16[96,768]{1,0:T(8,128)(2,1)S(1)}, u32[]{:S(2)}, u32[]{:S(2)}) collective-permute-start(bf16[96,768]{1,0:T(8,128)(2,1)} %get-tuple-element.118), channel_id=1, source_target_pairs={{0,3},{1,2},{2,1},{3,0},{4,7},{5,6},{6,5},{7,4},{8,11},{9,10},{10,... | collective-permute-start | bytes 442376 | tf_op jit(solution)/shard_map/ppermute | solution.py:142
  16.0 10.7 %collective-permute-start = (bf16[96,768]{1,0:T(8,128)(2,1)}, bf16[96,768]{1,0:T(8,128)(2,1)S(1)}, u32[]{:S(2)}, u32[]{:S(2)}) collective-permute-start(bf16[96,768]{1,0:T(8,128)(2,1)} %get-tuple-element.118), channel_id=1, source_target_pairs={{0,1},{1,0},{2,3},{3,2},{4,5},{5,4},{6,7},{7,6},{8,9},{9,8},{10,11... | collective-permute-start | bytes 442376 | tf_op jit(solution)/shard_map/ppermute | solution.py:142
  19.2 7.8 %collective-permute-start.10 = (bf16[4,24,640]{2,1,0:T(8,128)(2,1)S(1)}, bf16[4,24,640]{2,1,0:T(8,128)(2,1)S(1)}, u32[]{:S(2)}, u32[]{:S(2)}) collective-permute-start(bf16[4,24,640]{2,1,0:T(8,128)(2,1)S(1)} %pad_maximum_fusion.6.refs_0_), channel_id=1, source_target_pairs={{0,8},{4,12},{8,0},{12,4},{16,24},{20,28},{24,16},{28,20},{1,9},{5... | collective-permute-start | bytes 368648 | tf_op jit(solution)/shard_map/ppermute | solution.py:142
  21.5 6.3 %collective-permute-start.2 = (bf16[96,768]{1,0:T(8,128)(2,1)S(1)}, bf16[96,768]{1,0:T(8,128)(2,1)S(1)}, u32[]{:S(2)}, u32[]{:S(2)}) collective-permute-start(bf16[96,768]{1,0:T(8,128)(2,1)S(1)} %collective-permute-done.1), channel_id=1, source_target_pairs={{0,1},{1,0},{2,3},{3,2},{4,5},{5,4},{6,7},{7,6},{8,9},{9,8},{10,11... | collective-permute-start | bytes 442376 | tf_op jit(solution)/shard_map/ppermute | solution.py:142
  23.0 12.9 %collective-permute-start.22 = (bf16[5,24,768]{2,1,0:T(8,128)(2,1)}, bf16[5,24,768]{2,1,0:T(8,128)(2,1)S(1)}, u32[]{:S(2)}, u32[]{:S(2)}) collective-permute-start(bf16[5,24,768]{2,1,0:T(8,128)(2,1)} %get-tuple-element.116), channel_id=1, source_target_pairs={{0,3},{1,2},{2,1},{3,0},{4,7},{5,6},{6,5},{7,4},{8,11},{9,10},{10,... | collective-permute-start | bytes 552968 | tf_op jit(solution)/shard_map/ppermute | solution.py:142
  25.2 4.9 %collective-permute-start.12 = (bf16[4,24,640]{2,1,0:T(8,128)(2,1)S(1)}, bf16[4,24,640]{2,1,0:T(8,128)(2,1)S(1)}, u32[]{:S(2)}, u32[]{:S(2)}) collective-permute-start(bf16[4,24,640]{2,1,0:T(8,128)(2,1)S(1)} %pad_maximum_fusion.6.refs_0_), channel_id=1, source_target_pairs={{0,16},{4,20},{8,24},{12,28},{16,0},{20,4},{24,8},{28,12},{1,17},{... | collective-permute-start | bytes 368648 | tf_op jit(solution)/shard_map/ppermute | solution.py:142
  26.7 10.7 %collective-permute-start.21 = (bf16[5,24,768]{2,1,0:T(8,128)(2,1)}, bf16[5,24,768]{2,1,0:T(8,128)(2,1)S(1)}, u32[]{:S(2)}, u32[]{:S(2)}) collective-permute-start(bf16[5,24,768]{2,1,0:T(8,128)(2,1)} %get-tuple-element.116), channel_id=1, source_target_pairs={{0,1},{1,0},{2,3},{3,2},{4,5},{5,4},{6,7},{7,6},{8,9},{9,8},{10,11... | collective-permute-start | bytes 552968 | tf_op jit(solution)/shard_map/ppermute | solution.py:142
  27.0 6.3 %collective-permute-start.9 = (bf16[4,24,640]{2,1,0:T(8,128)(2,1)S(1)}, bf16[4,24,640]{2,1,0:T(8,128)(2,1)S(1)}, u32[]{:S(2)}, u32[]{:S(2)}) collective-permute-start(bf16[4,24,640]{2,1,0:T(8,128)(2,1)S(1)} %pad_maximum_fusion.6.refs_0_), channel_id=1, source_target_pairs={{0,4},{4,0},{8,12},{12,8},{16,20},{20,16},{24,28},{28,24},{1,5},{5... | collective-permute-start | bytes 368648 | tf_op jit(solution)/shard_map/ppermute | solution.py:142
  27.8 12.4 %collective-permute-start.11 = (bf16[4,24,640]{2,1,0:T(8,128)(2,1)S(1)}, bf16[4,24,640]{2,1,0:T(8,128)(2,1)S(1)}, u32[]{:S(2)}, u32[]{:S(2)}) collective-permute-start(bf16[4,24,640]{2,1,0:T(8,128)(2,1)S(1)} %collective-permute-done.10.refs_2_), channel_id=1, source_target_pairs={{0,4},{4,0},{8,12},{12,8},{16,20},{20,16},{24,28},{28,24},{1,5},{5... | collective-permute-start | bytes 368648 | tf_op jit(solution)/shard_map/ppermute | solution.py:142
  30.0 26.6 %collective-permute-start.4 = (bf16[256,768]{1,0:T(8,128)(2,1)}, bf16[256,768]{1,0:T(8,128)(2,1)S(1)}, u32[]{:S(2)}, u32[]{:S(2)}) collective-permute-start(bf16[256,768]{1,0:T(8,128)(2,1)} %refs_4_.1), channel_id=1, source_target_pairs={{0,3},{1,2},{2,1},{3,0},{4,7},{5,6},{6,5},{7,4},{8,11},{9,10},{10,... | collective-permute-start | bytes 1179656 | tf_op jit(solution)/shard_map/ppermute | solution.py:142
  37.4 20.2 %collective-permute-start.3 = (bf16[256,768]{1,0:T(8,128)(2,1)}, bf16[256,768]{1,0:T(8,128)(2,1)S(1)}, u32[]{:S(2)}, u32[]{:S(2)}) collective-permute-start(bf16[256,768]{1,0:T(8,128)(2,1)} %refs_4_.1), channel_id=1, source_target_pairs={{0,1},{1,0},{2,3},{3,2},{4,5},{5,4},{6,7},{7,6},{8,9},{9,8},{10,11... | collective-permute-start | bytes 1179656 | tf_op jit(solution)/shard_map/ppermute | solution.py:142
  38.2 18.4 %collective-permute-start.23 = (bf16[5,24,768]{2,1,0:T(8,128)(2,1)S(1)}, bf16[5,24,768]{2,1,0:T(8,128)(2,1)S(1)}, u32[]{:S(2)}, u32[]{:S(2)}) collective-permute-start(bf16[5,24,768]{2,1,0:T(8,128)(2,1)S(1)} %collective-permute-done.22), channel_id=1, source_target_pairs={{0,1},{1,0},{2,3},{3,2},{4,5},{5,4},{6,7},{7,6},{8,9},{9,8},{10,11... | collective-permute-start | bytes 552968 | tf_op jit(solution)/shard_map/ppermute | solution.py:142
  41.8 46.6 %collective-permute-start.34 = (bf16[4,96,768]{2,1,0:T(8,128)(2,1)S(1)}, bf16[4,96,768]{2,1,0:T(8,128)(2,1)S(1)}, u32[]{:S(2)}, u32[]{:S(2)}) collective-permute-start(bf16[4,96,768]{2,1,0:T(8,128)(2,1)S(1)} %pad_maximum_fusion.3.refs_18_.refs_16_), channel_id=1, source_target_pairs={{0,8},{4,12},{8,0},{12,4},{16,24},{20,28},{24,16},{28,20},{1,9},{5... | collective-permute-start | bytes 1769480 | tf_op jit(solution)/shard_map/ppermute | solution.py:142
  43.4 46.9 %collective-permute-start.36 = (bf16[4,96,768]{2,1,0:T(8,128)(2,1)S(1)}, bf16[4,96,768]{2,1,0:T(8,128)(2,1)}, u32[]{:S(2)}, u32[]{:S(2)}) collective-permute-start(bf16[4,96,768]{2,1,0:T(8,128)(2,1)S(1)} %pad_maximum_fusion.3.refs_18_.refs_16_), channel_id=1, source_target_pairs={{0,16},{4,20},{8,24},{12,28},{16,0},{20,4},{24,8},{28,12},{1,17},{... | collective-permute-start | bytes 1769480 | tf_op jit(solution)/shard_map/ppermute | solution.py:142
  56.6 33.7 %collective-permute-start.33 = (bf16[4,96,768]{2,1,0:T(8,128)(2,1)S(1)}, bf16[4,96,768]{2,1,0:T(8,128)(2,1)}, u32[]{:S(2)}, u32[]{:S(2)}) collective-permute-start(bf16[4,96,768]{2,1,0:T(8,128)(2,1)S(1)} %pad_maximum_fusion.3.refs_18_.refs_16_), channel_id=1, source_target_pairs={{0,4},{4,0},{8,12},{12,8},{16,20},{20,16},{24,28},{28,24},{1,5},{5... | collective-permute-start | bytes 1769480 | tf_op jit(solution)/shard_map/ppermute | solution.py:142
  56.7 11.5 %collective-permute-start.5 = (bf16[256,768]{1,0:T(8,128)(2,1)S(1)}, bf16[256,768]{1,0:T(8,128)(2,1)S(1)}, u32[]{:S(2)}, u32[]{:S(2)}) collective-permute-start(bf16[256,768]{1,0:T(8,128)(2,1)S(1)} %collective-permute-done.4.refs_3_), channel_id=1, source_target_pairs={{0,1},{1,0},{2,3},{3,2},{4,5},{5,4},{6,7},{7,6},{8,9},{9,8},{10,11... | collective-permute-start | bytes 1179656 | tf_op jit(solution)/shard_map/ppermute | solution.py:142
  58.9 46.9 %collective-permute-start.25 = (bf16[4,5,24,768]{3,2,1,0:T(8,128)(2,1)S(1)}, bf16[4,5,24,768]{3,2,1,0:T(8,128)(2,1)S(1)}, u32[]{:S(2)}, u32[]{:S(2)}) collective-permute-start(bf16[4,5,24,768]{3,2,1,0:T(8,128)(2,1)S(1)} %pad_maximum_fusion.refs_8_.refs_6_), channel_id=1, source_target_pairs={{0,8},{4,12},{8,0},{12,4},{16,24},{20,28},{24,16},{28,20},{1,9},{5... | collective-permute-start | bytes 2211848 | tf_op jit(solution)/shard_map/ppermute | solution.py:142
  68.9 37.4 %collective-permute-start.27 = (bf16[4,5,24,768]{3,2,1,0:T(8,128)(2,1)S(1)}, bf16[4,5,24,768]{3,2,1,0:T(8,128)(2,1)S(1)}, u32[]{:S(2)}, u32[]{:S(2)}) collective-permute-start(bf16[4,5,24,768]{3,2,1,0:T(8,128)(2,1)S(1)} %pad_maximum_fusion.refs_8_.refs_6_), channel_id=1, source_target_pairs={{0,16},{4,20},{8,24},{12,28},{16,0},{20,4},{24,8},{28,12},{1,17},{... | collective-permute-start | bytes 2211848 | tf_op jit(solution)/shard_map/ppermute | solution.py:142
  88.4 4.9 %collective-permute-start.18 = (bf16[192,256]{1,0:T(8,128)(2,1)}, bf16[192,256]{1,0:T(8,128)(2,1)S(1)}, u32[]{:S(2)}, u32[]{:S(2)}) collective-permute-start(bf16[192,256]{1,0:T(8,128)(2,1)} %get-tuple-element.103), channel_id=1, source_target_pairs={{0,1},{1,0},{2,3},{3,2},{4,5},{5,4},{6,7},{7,6},{8,9},{9,8},{10,11... | collective-permute-start | bytes 294920 | tf_op jit(solution)/shard_map/ppermute | solution.py:142
  90.2 10.3 %collective-permute-start.38 = (bf16[2,96,768]{2,1,0:T(8,128)(2,1)S(1)}, bf16[2,96,768]{2,1,0:T(8,128)(2,1)S(1)}, u32[]{:S(2)}, u32[]{:S(2)}) collective-permute-start(bf16[2,96,768]{2,1,0:T(8,128)(2,1)S(1)} %slice.297), channel_id=1, source_target_pairs={{0,16},{4,20},{8,24},{12,28},{16,0},{20,4},{24,8},{28,12},{1,17},{... | collective-permute-start | bytes 884744 | tf_op jit(solution)/shard_map/ppermute | solution.py:142
  90.3 24.9 %collective-permute-start.24 = (bf16[4,5,24,768]{3,2,1,0:T(8,128)(2,1)S(1)}, bf16[4,5,24,768]{3,2,1,0:T(8,128)(2,1)S(1)}, u32[]{:S(2)}, u32[]{:S(2)}) collective-permute-start(bf16[4,5,24,768]{3,2,1,0:T(8,128)(2,1)S(1)} %pad_maximum_fusion.refs_8_.refs_6_), channel_id=1, source_target_pairs={{0,4},{4,0},{8,12},{12,8},{16,20},{20,16},{24,28},{28,24},{1,5},{5... | collective-permute-start | bytes 2211848 | tf_op jit(solution)/shard_map/ppermute | solution.py:142
  93.3 5.7 %collective-permute-start.19 = (bf16[192,256]{1,0:T(8,128)(2,1)}, bf16[192,256]{1,0:T(8,128)(2,1)S(1)}, u32[]{:S(2)}, u32[]{:S(2)}) collective-permute-start(bf16[192,256]{1,0:T(8,128)(2,1)} %get-tuple-element.104), channel_id=1, source_target_pairs={{0,2},{1,3},{2,0},{3,1},{4,6},{5,7},{6,4},{7,5},{8,10},{9,11},{10,... | collective-permute-start | bytes 294920 | tf_op jit(solution)/shard_map/ppermute | solution.py:142
  99.1 6.7 %collective-permute-start.39 = (bf16[2,96,768]{2,1,0:T(8,128)(2,1)S(1)}, bf16[2,96,768]{2,1,0:T(8,128)(2,1)S(1)}, u32[]{:S(2)}, u32[]{:S(2)}) collective-permute-start(bf16[2,96,768]{2,1,0:T(8,128)(2,1)S(1)} %slice.298), channel_id=1, source_target_pairs={{0,8},{4,12},{8,0},{12,4},{16,24},{20,28},{24,16},{28,20},{1,9},{5... | collective-permute-start | bytes 884744 | tf_op jit(solution)/shard_map/ppermute | solution.py:142
  100.6 16.7 %collective-permute-start.35 = (bf16[4,96,768]{2,1,0:T(8,128)(2,1)S(1)}, bf16[4,96,768]{2,1,0:T(8,128)(2,1)S(1)}, u32[]{:S(2)}, u32[]{:S(2)}) collective-permute-start(bf16[4,96,768]{2,1,0:T(8,128)(2,1)S(1)} %collective-permute-done.34.refs_20_.refs_18_), channel_id=1, source_target_pairs={{0,4},{4,0},{8,12},{12,8},{16,20},{20,16},{24,28},{28,24},{1,5},{5... | collective-permute-start | bytes 1769480 | tf_op jit(solution)/shard_map/ppermute | solution.py:142
  105.8 10.9 %collective-permute-start.40 = (bf16[2,96,768]{2,1,0:T(8,128)(2,1)S(1)}, bf16[2,96,768]{2,1,0:T(8,128)(2,1)S(1)}, u32[]{:S(2)}, u32[]{:S(2)}) collective-permute-start(bf16[2,96,768]{2,1,0:T(8,128)(2,1)S(1)} %collective-permute-done.38.refs_24_.refs_22_), channel_id=1, source_target_pairs={{0,4},{4,0},{8,12},{12,8},{16,20},{20,16},{24,28},{28,24},{1,5},{5... | collective-permute-start | bytes 884744 | tf_op jit(solution)/shard_map/ppermute | solution.py:142
  105.8 10.9 %collective-permute-start.41 = (bf16[2,96,768]{2,1,0:T(8,128)(2,1)S(1)}, bf16[2,96,768]{2,1,0:T(8,128)(2,1)S(1)}, u32[]{:S(2)}, u32[]{:S(2)}) collective-permute-start(bf16[2,96,768]{2,1,0:T(8,128)(2,1)S(1)} %collective-permute-done.39.refs_25_.refs_23_), channel_id=1, source_target_pairs={{0,4},{4,0},{8,12},{12,8},{16,20},{20,16},{24,28},{28,24},{1,5},{5... | collective-permute-start | bytes 884744 | tf_op jit(solution)/shard_map/ppermute | solution.py:142
  106.3 7.3 %collective-permute-start.20 = (bf16[192,256]{1,0:T(8,128)(2,1)}, bf16[192,256]{1,0:T(8,128)(2,1)S(1)}, u32[]{:S(2)}, u32[]{:S(2)}) collective-permute-start(bf16[192,256]{1,0:T(8,128)(2,1)} %get-tuple-element.105), channel_id=1, source_target_pairs={{0,3},{1,2},{2,1},{3,0},{4,7},{5,6},{6,5},{7,4},{8,11},{9,10},{10,... | collective-permute-start | bytes 294920 | tf_op jit(solution)/shard_map/ppermute | solution.py:142
  113.6 10.1 %collective-permute-start.29 = (bf16[2,5,24,768]{3,2,1,0:T(8,128)(2,1)S(1)}, bf16[2,5,24,768]{3,2,1,0:T(8,128)(2,1)}, u32[]{:S(2)}, u32[]{:S(2)}) collective-permute-start(bf16[2,5,24,768]{3,2,1,0:T(8,128)(2,1)S(1)} %slice.295), channel_id=1, source_target_pairs={{0,16},{4,20},{8,24},{12,28},{16,0},{20,4},{24,8},{28,12},{1,17},{... | collective-permute-start | bytes 1105928 | tf_op jit(solution)/shard_map/ppermute | solution.py:142
  115.2 9.5 %collective-permute-start.30 = (bf16[2,5,24,768]{3,2,1,0:T(8,128)(2,1)S(1)}, bf16[2,5,24,768]{3,2,1,0:T(8,128)(2,1)}, u32[]{:S(2)}, u32[]{:S(2)}) collective-permute-start(bf16[2,5,24,768]{3,2,1,0:T(8,128)(2,1)S(1)} %slice.296), channel_id=1, source_target_pairs={{0,8},{4,12},{8,0},{12,4},{16,24},{20,28},{24,16},{28,20},{1,9},{5... | collective-permute-start | bytes 1105928 | tf_op jit(solution)/shard_map/ppermute | solution.py:142
  116.7 11.3 %collective-permute-start.26 = (bf16[4,5,24,768]{3,2,1,0:T(8,128)(2,1)S(1)}, bf16[4,5,24,768]{3,2,1,0:T(8,128)(2,1)S(1)}, u32[]{:S(2)}, u32[]{:S(2)}) collective-permute-start(bf16[4,5,24,768]{3,2,1,0:T(8,128)(2,1)S(1)} %collective-permute-done.25.refs_10_.refs_8_), channel_id=1, source_target_pairs={{0,4},{4,0},{8,12},{12,8},{16,20},{20,16},{24,28},{28,24},{1,5},{5... | collective-permute-start | bytes 2211848 | tf_op jit(solution)/shard_map/ppermute | solution.py:142
  116.7 11.3 %collective-permute-start.28 = (bf16[4,5,24,768]{3,2,1,0:T(8,128)(2,1)S(1)}, bf16[4,5,24,768]{3,2,1,0:T(8,128)(2,1)}, u32[]{:S(2)}, u32[]{:S(2)}) collective-permute-start(bf16[4,5,24,768]{3,2,1,0:T(8,128)(2,1)S(1)} %collective-permute-done.27.refs_12_.refs_10_), channel_id=1, source_target_pairs={{0,4},{4,0},{8,12},{12,8},{16,20},{20,16},{24,28},{28,24},{1,5},{5... | collective-permute-start | bytes 2211848 | tf_op jit(solution)/shard_map/ppermute | solution.py:142
  118.1 9.9 %collective-permute-start.37 = (bf16[4,96,768]{2,1,0:T(8,128)(2,1)}, bf16[4,96,768]{2,1,0:T(8,128)(2,1)}, u32[]{:S(2)}, u32[]{:S(2)}) collective-permute-start(bf16[4,96,768]{2,1,0:T(8,128)(2,1)} %collective-permute-done.36.refs_22_.refs_20_), channel_id=1, source_target_pairs={{0,4},{4,0},{8,12},{12,8},{16,20},{20,16},{24,28},{28,24},{1,5},{5... | collective-permute-start | bytes 1769480 | tf_op jit(solution)/shard_map/ppermute | solution.py:142
  145.5 12.8 %collective-permute-start.45 = (bf16[4,4,96,768]{3,2,1,0:T(8,128)(2,1)}, bf16[4,4,96,768]{3,2,1,0:T(8,128)(2,1)S(1)}, u32[]{:S(2)}, u32[]{:S(2)}) collective-permute-start(bf16[4,4,96,768]{3,2,1,0:T(8,128)(2,1)} %bitcast.180), channel_id=1, source_target_pairs={{0,4},{4,0},{8,12},{12,8},{16,20},{20,16},{24,28},{28,24},{1,5},{5... | collective-permute-start | bytes 7077896 | tf_op jit(solution)/shard_map/ppermute | solution.py:142
  165.5 39.0 %collective-permute-start.48 = (bf16[4,4,5,24,768]{4,3,2,1,0:T(8,128)(2,1)}, bf16[4,4,5,24,768]{4,3,2,1,0:T(8,128)(2,1)S(1)}, u32[]{:S(2)}, u32[]{:S(2)}) collective-permute-start(bf16[4,4,5,24,768]{4,3,2,1,0:T(8,128)(2,1)} %get-tuple-element.147), channel_id=1, source_target_pairs={{0,4},{4,0},{8,12},{12,8},{16,20},{20,16},{24,28},{28,24},{1,5},{5... | collective-permute-start | bytes 8847368 | tf_op jit(solution)/shard_map/ppermute | solution.py:142
  167.3 14.6 %collective-permute-start.46 = (bf16[2,96,768]{2,1,0:T(8,128)(2,1)S(1)}, bf16[2,96,768]{2,1,0:T(8,128)(2,1)S(1)}, u32[]{:S(2)}, u32[]{:S(2)}) collective-permute-start(bf16[2,96,768]{2,1,0:T(8,128)(2,1)S(1)} %get-tuple-element.182), channel_id=1, source_target_pairs={{0,16},{4,20},{8,24},{12,28},{16,0},{20,4},{24,8},{28,12},{1,17},{... | collective-permute-start | bytes 884744 | tf_op jit(solution)/shard_map/ppermute | solution.py:142
  168.1 13.8 %collective-permute-start.47 = (bf16[2,96,768]{2,1,0:T(8,128)(2,1)S(1)}, bf16[2,96,768]{2,1,0:T(8,128)(2,1)S(1)}, u32[]{:S(2)}, u32[]{:S(2)}) collective-permute-start(bf16[2,96,768]{2,1,0:T(8,128)(2,1)S(1)} %get-tuple-element.181), channel_id=1, source_target_pairs={{0,8},{4,12},{8,0},{12,4},{16,24},{20,28},{24,16},{28,20},{1,9},{5... | collective-permute-start | bytes 884744 | tf_op jit(solution)/shard_map/ppermute | solution.py:142
  169.7 5.7 %collective-permute-start.42 = (bf16[192,256]{1,0:T(8,128)(2,1)S(1)}, bf16[192,256]{1,0:T(8,128)(2,1)S(1)}, u32[]{:S(2)}, u32[]{:S(2)}) collective-permute-start(bf16[192,256]{1,0:T(8,128)(2,1)S(1)} %copy-done.42), channel_id=1, source_target_pairs={{0,1},{1,0},{2,3},{3,2},{4,5},{5,4},{6,7},{7,6},{8,9},{9,8},{10,11... | collective-permute-start | bytes 294920 | tf_op jit(solution)/shard_map/ppermute | solution.py:142
  170.8 8.8 %collective-permute-start.43 = (bf16[192,256]{1,0:T(8,128)(2,1)S(1)}, bf16[192,256]{1,0:T(8,128)(2,1)S(1)}, u32[]{:S(2)}, u32[]{:S(2)}) collective-permute-start(bf16[192,256]{1,0:T(8,128)(2,1)S(1)} %copy-done.41), channel_id=1, source_target_pairs={{0,2},{1,3},{2,0},{3,1},{4,6},{5,7},{6,4},{7,5},{8,10},{9,11},{10,... | collective-permute-start | bytes 294920 | tf_op jit(solution)/shard_map/ppermute | solution.py:142
  175.4 6.5 %collective-permute-start.44 = (bf16[192,256]{1,0:T(8,128)(2,1)S(1)}, bf16[192,256]{1,0:T(8,128)(2,1)S(1)}, u32[]{:S(2)}, u32[]{:S(2)}) collective-permute-start(bf16[192,256]{1,0:T(8,128)(2,1)S(1)} %copy-done.40), channel_id=1, source_target_pairs={{0,3},{1,2},{2,1},{3,0},{4,7},{5,6},{6,5},{7,4},{8,11},{9,10},{10,... | collective-permute-start | bytes 294920 | tf_op jit(solution)/shard_map/ppermute | solution.py:142
  183.3 21.1 %collective-permute-start.50 = (bf16[4,96,768]{2,1,0:T(8,128)(2,1)S(1)}, bf16[4,96,768]{2,1,0:T(8,128)(2,1)}, u32[]{:S(2)}, u32[]{:S(2)}) collective-permute-start(bf16[4,96,768]{2,1,0:T(8,128)(2,1)S(1)} %pad_maximum_fusion.5), channel_id=1, source_target_pairs={{0,16},{4,20},{8,24},{12,28},{16,0},{20,4},{24,8},{28,12},{1,17},{... | collective-permute-start | bytes 1769480 | tf_op jit(solution)/shard_map/ppermute | solution.py:142
  185.7 18.7 %collective-permute-start.49 = (bf16[4,96,768]{2,1,0:T(8,128)(2,1)}, bf16[4,96,768]{2,1,0:T(8,128)(2,1)}, u32[]{:S(2)}, u32[]{:S(2)}) collective-permute-start(bf16[4,96,768]{2,1,0:T(8,128)(2,1)} %pad_maximum_fusion.4), channel_id=1, source_target_pairs={{0,8},{4,12},{8,0},{12,4},{16,24},{20,28},{24,16},{28,20},{1,9},{5... | collective-permute-start | bytes 1769480 | tf_op jit(solution)/shard_map/ppermute | solution.py:142
  208.6 8.3 %collective-permute-start.70 = (bf16[96,768]{1,0:T(8,128)(2,1)}, bf16[96,768]{1,0:T(8,128)(2,1)}, u32[]{:S(2)}, u32[]{:S(2)}) collective-permute-start(bf16[96,768]{1,0:T(8,128)(2,1)} %get-tuple-element.194), channel_id=1, source_target_pairs={{0,1},{1,0},{2,3},{3,2},{4,5},{5,4},{6,7},{7,6},{8,9},{9,8},{10,11... | collective-permute-start | bytes 442376 | tf_op jit(solution)/shard_map/ppermute | solution.py:142
  208.6 16.1 %collective-permute-start.69 = (bf16[96,768]{1,0:T(8,128)(2,1)}, bf16[96,768]{1,0:T(8,128)(2,1)}, u32[]{:S(2)}, u32[]{:S(2)}) collective-permute-start(bf16[96,768]{1,0:T(8,128)(2,1)} %get-tuple-element.193), channel_id=1, source_target_pairs={{0,1},{1,0},{2,3},{3,2},{4,5},{5,4},{6,7},{7,6},{8,9},{9,8},{10,11... | collective-permute-start | bytes 442376 | tf_op jit(solution)/shard_map/ppermute | solution.py:142
  216.8 12.1 %collective-permute-start.54 = (bf16[4,4,24,640]{3,2,1,0:T(8,128)(2,1)}, bf16[4,4,24,640]{3,2,1,0:T(8,128)(2,1)S(1)}, u32[]{:S(2)}, u32[]{:S(2)}) collective-permute-start(bf16[4,4,24,640]{3,2,1,0:T(8,128)(2,1)} %get-tuple-element.160), channel_id=1, source_target_pairs={{0,4},{4,0},{8,12},{12,8},{16,20},{20,16},{24,28},{28,24},{1,5},{5... | collective-permute-start | bytes 1474568 | tf_op jit(solution)/shard_map/ppermute | solution.py:142
  217.8 8.2 %collective-permute-start.71 = (bf16[96,768]{1,0:T(8,128)(2,1)S(1)}, bf16[96,768]{1,0:T(8,128)(2,1)S(1)}, u32[]{:S(2)}, u32[]{:S(2)}) collective-permute-start(bf16[96,768]{1,0:T(8,128)(2,1)S(1)} %bitcast_add_fusion.5), channel_id=1, source_target_pairs={{0,3},{1,2},{2,1},{3,0},{4,7},{5,6},{6,5},{7,4},{8,11},{9,10},{10,... | collective-permute-start | bytes 442376 | tf_op jit(solution)/shard_map/ppermute | solution.py:142
  221.6 11.4 %collective-permute-start.62 = (bf16[2,5,24,768]{3,2,1,0:T(8,128)(2,1)S(1)}, bf16[2,5,24,768]{3,2,1,0:T(8,128)(2,1)S(1)}, u32[]{:S(2)}, u32[]{:S(2)}) collective-permute-start(bf16[2,5,24,768]{3,2,1,0:T(8,128)(2,1)S(1)} %get-tuple-element.175), channel_id=1, source_target_pairs={{0,16},{4,20},{8,24},{12,28},{16,0},{20,4},{24,8},{28,12},{1,17},{... | collective-permute-start | bytes 1105928 | tf_op jit(solution)/shard_map/ppermute | solution.py:142
  223.2 11.3 %collective-permute-start.64 = (bf16[2,5,24,768]{3,2,1,0:T(8,128)(2,1)S(1)}, bf16[2,5,24,768]{3,2,1,0:T(8,128)(2,1)S(1)}, u32[]{:S(2)}, u32[]{:S(2)}) collective-permute-start(bf16[2,5,24,768]{3,2,1,0:T(8,128)(2,1)S(1)} %get-tuple-element.176), channel_id=1, source_target_pairs={{0,8},{4,12},{8,0},{12,4},{16,24},{20,28},{24,16},{28,20},{1,9},{5... | collective-permute-start | bytes 1105928 | tf_op jit(solution)/shard_map/ppermute | solution.py:142
  224.7 23.7 %collective-permute-start.52 = (bf16[256,768]{1,0:T(8,128)(2,1)S(1)}, bf16[256,768]{1,0:T(8,128)(2,1)S(1)}, u32[]{:S(2)}, u32[]{:S(2)}) collective-permute-start(bf16[256,768]{1,0:T(8,128)(2,1)S(1)} %copy-done.39), channel_id=1, source_target_pairs={{0,1},{1,0},{2,3},{3,2},{4,5},{5,4},{6,7},{7,6},{8,9},{9,8},{10,11... | collective-permute-start | bytes 1179656 | tf_op jit(solution)/shard_map/ppermute | solution.py:142
  226.0 47.8 %collective-permute-start.51 = (bf16[256,768]{1,0:T(8,128)(2,1)}, bf16[256,768]{1,0:T(8,128)(2,1)}, u32[]{:S(2)}, u32[]{:S(2)}) collective-permute-start(bf16[256,768]{1,0:T(8,128)(2,1)} %get-tuple-element.156), channel_id=1, source_target_pairs={{0,1},{1,0},{2,3},{3,2},{4,5},{5,4},{6,7},{7,6},{8,9},{9,8},{10,11... | collective-permute-start | bytes 1179656 | tf_op jit(solution)/shard_map/ppermute | solution.py:142
  229.0 5.6 %collective-permute-start.55 = (bf16[2,24,640]{2,1,0:T(8,128)(2,1)S(1)}, bf16[2,24,640]{2,1,0:T(8,128)(2,1)S(1)}, u32[]{:S(2)}, u32[]{:S(2)}) collective-permute-start(bf16[2,24,640]{2,1,0:T(8,128)(2,1)S(1)} %get-tuple-element.187), channel_id=1, source_target_pairs={{0,16},{4,20},{8,24},{12,28},{16,0},{20,4},{24,8},{28,12},{1,17},{... | collective-permute-start | bytes 184328 | tf_op jit(solution)/shard_map/ppermute | solution.py:142
  237.2 4.9 %collective-permute-start.56 = (bf16[4,24,640]{2,1,0:T(8,128)(2,1)S(1)}, bf16[4,24,640]{2,1,0:T(8,128)(2,1)S(1)}, u32[]{:S(2)}, u32[]{:S(2)}) collective-permute-start(bf16[4,24,640]{2,1,0:T(8,128)(2,1)S(1)} %pad_maximum_fusion.7), channel_id=1, source_target_pairs={{0,8},{4,12},{8,0},{12,4},{16,24},{20,28},{24,16},{28,20},{1,9},{5... | collective-permute-start | bytes 368648 | tf_op jit(solution)/shard_map/ppermute | solution.py:142
  238.8 4.9 %collective-permute-start.58 = (bf16[4,24,640]{2,1,0:T(8,128)(2,1)S(1)}, bf16[4,24,640]{2,1,0:T(8,128)(2,1)S(1)}, u32[]{:S(2)}, u32[]{:S(2)}) collective-permute-start(bf16[4,24,640]{2,1,0:T(8,128)(2,1)S(1)} %pad_maximum_fusion.8), channel_id=1, source_target_pairs={{0,16},{4,20},{8,24},{12,28},{16,0},{20,4},{24,8},{28,12},{1,17},{... | collective-permute-start | bytes 368648 | tf_op jit(solution)/shard_map/ppermute | solution.py:142
  243.8 5.2 %collective-permute-start.59 = (bf16[24,640]{1,0:T(8,128)(2,1)S(1)}, bf16[24,640]{1,0:T(8,128)(2,1)S(1)}, u32[]{:S(2)}, u32[]{:S(2)}) collective-permute-start(bf16[24,640]{1,0:T(8,128)(2,1)S(1)} %get-tuple-element.214), channel_id=1, source_target_pairs={{0,1},{1,0},{2,3},{3,2},{4,5},{5,4},{6,7},{7,6},{8,9},{9,8},{10,11... | collective-permute-start | bytes 92168 | tf_op jit(solution)/shard_map/ppermute | solution.py:142
  243.9 6.8 %collective-permute-start.60 = (bf16[24,640]{1,0:T(8,128)(2,1)S(1)}, bf16[24,640]{1,0:T(8,128)(2,1)S(1)}, u32[]{:S(2)}, u32[]{:S(2)}) collective-permute-start(bf16[24,640]{1,0:T(8,128)(2,1)S(1)} %get-tuple-element.213), channel_id=1, source_target_pairs={{0,2},{1,3},{2,0},{3,1},{4,6},{5,7},{6,4},{7,5},{8,10},{9,11},{10,... | collective-permute-start | bytes 92168 | tf_op jit(solution)/shard_map/ppermute | solution.py:142
  246.2 6.0 %collective-permute-start.61 = (bf16[24,640]{1,0:T(8,128)(2,1)S(1)}, bf16[24,640]{1,0:T(8,128)(2,1)S(1)}, u32[]{:S(2)}, u32[]{:S(2)}) collective-permute-start(bf16[24,640]{1,0:T(8,128)(2,1)S(1)} %get-tuple-element.212), channel_id=1, source_target_pairs={{0,3},{1,2},{2,1},{3,0},{4,7},{5,6},{6,5},{7,4},{8,11},{9,10},{10,... | collective-permute-start | bytes 92168 | tf_op jit(solution)/shard_map/ppermute | solution.py:142
  248.4 14.4 %collective-permute-start.63 = (bf16[4,5,24,768]{3,2,1,0:T(8,128)(2,1)S(1)}, bf16[4,5,24,768]{3,2,1,0:T(8,128)(2,1)S(1)}, u32[]{:S(2)}, u32[]{:S(2)}) collective-permute-start(bf16[4,5,24,768]{3,2,1,0:T(8,128)(2,1)S(1)} %pad_maximum_fusion.1), channel_id=1, source_target_pairs={{0,8},{4,12},{8,0},{12,4},{16,24},{20,28},{24,16},{28,20},{1,9},{5... | collective-permute-start | bytes 2211848 | tf_op jit(solution)/shard_map/ppermute | solution.py:142
  249.1 14.1 %collective-permute-start.65 = (bf16[4,5,24,768]{3,2,1,0:T(8,128)(2,1)S(1)}, bf16[4,5,24,768]{3,2,1,0:T(8,128)(2,1)S(1)}, u32[]{:S(2)}, u32[]{:S(2)}) collective-permute-start(bf16[4,5,24,768]{3,2,1,0:T(8,128)(2,1)S(1)} %pad_maximum_fusion.2), channel_id=1, source_target_pairs={{0,16},{4,20},{8,24},{12,28},{16,0},{20,4},{24,8},{28,12},{1,17},{... | collective-permute-start | bytes 2211848 | tf_op jit(solution)/shard_map/ppermute | solution.py:142
  250.7 23.0 %collective-permute-start.53 = (bf16[256,768]{1,0:T(8,128)(2,1)S(1)}, bf16[256,768]{1,0:T(8,128)(2,1)S(1)}, u32[]{:S(2)}, u32[]{:S(2)}) collective-permute-start(bf16[256,768]{1,0:T(8,128)(2,1)S(1)} %add.231), channel_id=1, source_target_pairs={{0,3},{1,2},{2,1},{3,0},{4,7},{5,6},{6,5},{7,4},{8,11},{9,10},{10,... | collective-permute-start | bytes 1179656 | tf_op jit(solution)/shard_map/ppermute | solution.py:142
  265.2 7.1 %collective-permute-start.67 = (bf16[5,24,768]{2,1,0:T(8,128)(2,1)}, bf16[5,24,768]{2,1,0:T(8,128)(2,1)S(1)}, u32[]{:S(2)}, u32[]{:S(2)}) collective-permute-start(bf16[5,24,768]{2,1,0:T(8,128)(2,1)} %get-tuple-element.192), channel_id=1, source_target_pairs={{0,1},{1,0},{2,3},{3,2},{4,5},{5,4},{6,7},{7,6},{8,9},{9,8},{10,11... | collective-permute-start | bytes 552968 | tf_op jit(solution)/shard_map/ppermute | solution.py:142
  268.3 7.3 %collective-permute-start.66 = (bf16[5,24,768]{2,1,0:T(8,128)(2,1)S(1)}, bf16[5,24,768]{2,1,0:T(8,128)(2,1)S(1)}, u32[]{:S(2)}, u32[]{:S(2)}) collective-permute-start(bf16[5,24,768]{2,1,0:T(8,128)(2,1)S(1)} %get-tuple-element.191), channel_id=1, source_target_pairs={{0,1},{1,0},{2,3},{3,2},{4,5},{5,4},{6,7},{7,6},{8,9},{9,8},{10,11... | collective-permute-start | bytes 552968 | tf_op jit(solution)/shard_map/ppermute | solution.py:142
  272.2 7.5 %collective-permute-start.68 = (bf16[5,24,768]{2,1,0:T(8,128)(2,1)S(1)}, bf16[5,24,768]{2,1,0:T(8,128)(2,1)S(1)}, u32[]{:S(2)}, u32[]{:S(2)}) collective-permute-start(bf16[5,24,768]{2,1,0:T(8,128)(2,1)S(1)} %bitcast_add_fusion.4), channel_id=1, source_target_pairs={{0,3},{1,2},{2,1},{3,0},{4,7},{5,6},{6,5},{7,4},{8,11},{9,10},{10,... | collective-permute-start | bytes 552968 | tf_op jit(solution)/shard_map/ppermute | solution.py:142
  (51 other events, 635.3 us)
